TPU v7x, 768 devices: a whole 4x8x12 slice. The times are simulated.
768 devices in a mesh: section: 12 (over x, z_hi), dp: 64 (over y, z_lo, core).
Axes of the slice: x: 4, y: 8, z: 12 (z_hi: 3, z_lo: 4; z = z_hi * 4 + z_lo), core: 2. Of those that a mesh axis runs over, the one named last changes fastest.
Arguments:
- buffer: bfloat16 [12, 512, 2048], P('section', 'dp'), may hold values from -6 to 6
- gate_weight: bfloat16 [12, 2, 2048, 8192], P('section', None, None, 'dp'), may hold values from -0.125 to 0.125
- up_weight: bfloat16 [12, 2, 2048, 8192], P('section', None, None, 'dp'), may hold values from -0.125 to 0.125
- down_weight: bfloat16 [12, 2, 8192, 2048], P('section', None, 'dp'), may hold values from -0.09375 to 0.09375
- norm_gain: float32 [12, 2, 2048], P('section'), may hold values from 0.1 to 1.9
- repeat_index: int32 [2, 12], P(None, 'section'), may hold values from 0 to 1
Outputs:
- final_buffer: bfloat16 [12, 512, 2048], P('section', 'dp')
Inputs may be any that keep to these rules, and one draw needn't show every extreme that they name: `repeat_index`: the layer each section applies, one of its 2.
All inputs are finite; a program needn't handle non-finite values.
Results may differ from a plain program's by a relative error of at most 0.01.
Values may be sent and summed in bfloat16 or wider, within the bound.
No kernel may reach another device: no remote copies, remote signals or barrier semaphores. Data moves between devices by JAX's collectives and lax.ppermute only.
A program may use at most 32 MiB of HBM per device.

v0:
```python
import jax
import jax.numpy as jnp
from jax import lax
from jax.sharding import PartitionSpec as P

TICKS = 2


epsilon = 0.5


def from_partner(value, axis, bit):
    mask = 2**bit
    pairs = [(source, source ^ mask) for source in range(lax.axis_size(axis))]
    return lax.ppermute(value, axis, pairs)


def passed_along(block, axis, distance):
    devices = range(lax.axis_size(axis))
    route = [((i - distance) % len(devices), i) for i in devices]
    return lax.ppermute(block, axis, route)


def feed_forward(block_rows, gate_slab, up_slab, down_slab):
    gate_value = jnp.dot(block_rows, gate_slab, preferred_element_type=jnp.float32)
    up_value = jnp.dot(block_rows, up_slab, preferred_element_type=jnp.float32)
    hidden = (jax.nn.silu(gate_value) * up_value).astype(jnp.bfloat16)
    return jnp.dot(hidden, down_slab, preferred_element_type=jnp.float32)


def on_device(buffer, gate_weight, up_weight, down_weight, norm_gain, repeat_index):
    current = buffer[0]
    levels = lax.axis_size("dp").bit_length() - 1
    position = lax.axis_index("dp")
    for tick_index in range(TICKS):
        chosen = repeat_index[tick_index, 0]
        gate_slab = lax.dynamic_index_in_dim(gate_weight[0], chosen, 0, keepdims=False)
        up_slab = lax.dynamic_index_in_dim(up_weight[0], chosen, 0, keepdims=False)
        down_slab = lax.dynamic_index_in_dim(down_weight[0], chosen, 0, keepdims=False)
        gain_row = lax.dynamic_index_in_dim(norm_gain[0], chosen, 0, keepdims=False)
        widened = current.astype(jnp.float32)
        squares = jnp.mean(widened * widened, axis=-1, keepdims=True)
        normed = (widened * lax.rsqrt(squares + epsilon) * gain_row[None, :]).astype(jnp.bfloat16)
        paired = from_partner((gate_slab, up_slab, down_slab), "dp", 0)
        gate_both = jnp.concatenate([gate_slab, paired[0]], axis=1)
        up_both = jnp.concatenate([up_slab, paired[1]], axis=1)
        down_both = jnp.concatenate([down_slab, paired[2]], axis=0)
        group_block = normed
        for bit_number in range(1, levels):
            partner = from_partner(group_block, "dp", bit_number)
            upper_half = position >> bit_number & 1 == 1
            group_block = jnp.where(
                upper_half,
                jnp.concatenate([partner, group_block], axis=0),
                jnp.concatenate([group_block, partner], axis=0),
            )
        partial_value = feed_forward(group_block, gate_both, up_both, down_both)
        for bit_number in reversed(range(1, levels)):
            half_rows = partial_value.shape[0] // 2
            lower_part = partial_value[:half_rows]
            higher_part = partial_value[half_rows:]
            upper_half = position >> bit_number & 1 == 1
            kept_half = jnp.where(upper_half, higher_part, lower_part)
            sent_half = jnp.where(upper_half, lower_part, higher_part)
            partial_value = kept_half + from_partner(
                sent_half.astype(jnp.bfloat16), "dp", bit_number
            ).astype(sent_half.dtype)
        advanced = (widened + partial_value).astype(jnp.bfloat16)
        current = passed_along(advanced, "section", 1)
    return current[None]


def solution(mesh):
    placed = (
        P("section", "dp", None),
        P("section", None, None, "dp"),
        P("section", None, None, "dp"),
        P("section", None, "dp", None),
        P("section", None, None),
        P(None, "section"),
    )
    return jax.shard_map(
        on_device, mesh=mesh, in_specs=placed, out_specs=P("section", "dp", None), check_vma=False
    )
```

profile of v0, /device:TPU:56, one launch (start us, length us, event | category | flops | bytes accessed | tf_op | source)
XLA Modules:
  0.0 297.2 jit_solution(17691757048121864814)
XLA Ops:
  7.9 4.3 %collective-permute-start = (bf16[8,2048]{1,0:T(8,128)(2,1)S(1)}, bf16[8,2048]{1,0:T(8,128)(2,1)S(1)}, u32[]{:S(2)}, u32[]{:S(2)}) collective-permute-start(bf16[8,2048]{1,0:T(8,128)(2,1)S(1)} %fusion.40), channel_id=1, source_target_pairs={{0,2},{1,3},{2,0},{3,1},{4,6},{5,7},{6,4},{7,5},{8,10},{9,11},{10,... | collective-permute-start | bytes 98312 | tf_op jit(solution)/shard_map/ppermute | solution.py:15
  14.1 6.1 %collective-permute-start.1 = (bf16[16,2048]{1,0:T(8,128)(2,1)S(1)}, bf16[16,2048]{1,0:T(8,128)(2,1)S(1)}, u32[]{:S(2)}, u32[]{:S(2)}) collective-permute-start(bf16[16,2048]{1,0:T(8,128)(2,1)S(1)} %maximum_select_fusion.20), channel_id=1, source_target_pairs={{0,4},{1,5},{2,6},{3,7},{4,0},{5,1},{6,2},{7,3},{8,12},{9,13},{10,... | collective-permute-start | bytes 196616 | tf_op jit(solution)/shard_map/ppermute | solution.py:15
  20.2 2.4 collective-permute-done.1
  22.6 3.3 %collective-permute-start.2 = (bf16[32,2048]{1,0:T(8,128)(2,1)S(1)}, bf16[32,2048]{1,0:T(8,128)(2,1)S(1)}, u32[]{:S(2)}, u32[]{:S(2)}) collective-permute-start(bf16[32,2048]{1,0:T(8,128)(2,1)S(1)} %maximum_select_fusion.18), channel_id=1, source_target_pairs={{0,8},{1,9},{2,10},{3,11},{4,12},{5,13},{6,14},{7,15},{8,0},{9,1},... | collective-permute-start | bytes 393224 | tf_op jit(solution)/shard_map/ppermute | solution.py:15
  25.8 3.6 %collective-permute-done.2 = bf16[32,2048]{1,0:T(8,128)(2,1)S(1)} collective-permute-done((bf16[32,2048]{1,0:T(8,128)(2,1)S(1)}, bf16[32,2048]{1,0:T(8,128)(2,1)S(1)}, u32[]{:S(2)}, u32[]{:S(2)}) %collective-permute-start.2) | collective-permute-done | bytes 131104 | tf_op jit(solution)/shard_map/ppermute | solution.py:15
  29.5 4.0 %collective-permute-start.3 = (bf16[64,2048]{1,0:T(8,128)(2,1)S(1)}, bf16[64,2048]{1,0:T(8,128)(2,1)}, u32[]{:S(2)}, u32[]{:S(2)}) collective-permute-start(bf16[64,2048]{1,0:T(8,128)(2,1)S(1)} %maximum_select_fusion.4), channel_id=1, source_target_pairs={{0,16},{1,17},{2,18},{3,19},{4,20},{5,21},{6,22},{7,23},{8,24},{9,... | collective-permute-start | bytes 786440 | tf_op jit(solution)/shard_map/ppermute | solution.py:15
  33.5 2.2 dynamic-slice_bitcast_fusion.2
  35.7 2.0 collective-permute-start.5
  37.9 2.4 collective-permute-start.6
  40.3 2.7 collective-permute-done.3
  44.2 7.8 %collective-permute-start.4 = (bf16[128,2048]{1,0:T(8,128)(2,1)S(1)}, bf16[128,2048]{1,0:T(8,128)(2,1)}, u32[]{:S(2)}, u32[]{:S(2)}) collective-permute-start(bf16[128,2048]{1,0:T(8,128)(2,1)S(1)} %maximum_select_fusion.2), channel_id=1, source_target_pairs={{0,32},{1,33},{2,34},{3,35},{4,36},{5,37},{6,38},{7,39},{8,40},{9,... | collective-permute-start | bytes 1572872 | tf_op jit(solution)/shard_map/ppermute | solution.py:15
  54.8 19.4 %collective-permute-done.4 = bf16[128,2048]{1,0:T(8,128)(2,1)} collective-permute-done((bf16[128,2048]{1,0:T(8,128)(2,1)S(1)}, bf16[128,2048]{1,0:T(8,128)(2,1)}, u32[]{:S(2)}, u32[]{:S(2)}) %collective-permute-start.4) | collective-permute-done | bytes 524320 | tf_op jit(solution)/shard_map/ppermute | solution.py:15
  74.2 2.0 fusion
  76.3 3.1 %fusion.8 = f32[256,2048]{1,0:T(8,128)S(1)} fusion(bf16[128,2048]{1,0:T(8,128)(2,1)} %collective-permute-done.7, bf16[128,2048]{1,0:T(8,128)(2,1)} %copy-done.5, f32[256,256]{1,0:T(8,128)S(1)} %fusion, bf16[2048,128]{1,0:T(8,128)(2,1)} %collective-permute-done.6, bf16[2048,128]{1,0:T(8,128)(2,1)} %copy-done.4, ...), kind=kOutput, calls=%fused_computation.9 | convolution fusion | flops 546177024 | bytes 5505025 | tf_op jit(solution)/shard_map/dot_general | solution.py:28
  79.5 6.1 %collective-permute-start.8 = (bf16[128,2048]{1,0:T(8,128)(2,1)S(1)}, bf16[128,2048]{1,0:T(8,128)(2,1)S(1)}, u32[]{:S(2)}, u32[]{:S(2)}) collective-permute-start(bf16[128,2048]{1,0:T(8,128)(2,1)S(1)} %select_convert_fusion.1), channel_id=1, source_target_pairs={{0,32},{1,33},{2,34},{3,35},{4,36},{5,37},{6,38},{7,39},{8,40},{9,... | collective-permute-start | bytes 1572872 | tf_op jit(solution)/shard_map/ppermute | solution.py:15
  85.7 16.7 %collective-permute-done.8 = bf16[128,2048]{1,0:T(8,128)(2,1)S(1)} collective-permute-done((bf16[128,2048]{1,0:T(8,128)(2,1)S(1)}, bf16[128,2048]{1,0:T(8,128)(2,1)S(1)}, u32[]{:S(2)}, u32[]{:S(2)}) %collective-permute-start.8) | collective-permute-done | bytes 524320 | tf_op jit(solution)/shard_map/ppermute | solution.py:15
  102.6 7.0 %collective-permute-start.9 = (bf16[64,2048]{1,0:T(8,128)(2,1)S(1)}, bf16[64,2048]{1,0:T(8,128)(2,1)S(1)}, u32[]{:S(2)}, u32[]{:S(2)}) collective-permute-start(bf16[64,2048]{1,0:T(8,128)(2,1)S(1)} %select_convert_fusion.3), channel_id=1, source_target_pairs={{0,16},{1,17},{2,18},{3,19},{4,20},{5,21},{6,22},{7,23},{8,24},{9,... | collective-permute-start | bytes 786440 | tf_op jit(solution)/shard_map/ppermute | solution.py:15
  109.7 10.0 %collective-permute-done.9 = bf16[64,2048]{1,0:T(8,128)(2,1)S(1)} collective-permute-done((bf16[64,2048]{1,0:T(8,128)(2,1)S(1)}, bf16[64,2048]{1,0:T(8,128)(2,1)S(1)}, u32[]{:S(2)}, u32[]{:S(2)}) %collective-permute-start.9) | collective-permute-done | bytes 262176 | tf_op jit(solution)/shard_map/ppermute | solution.py:15
  119.8 2.7 collective-permute-start.10
  122.5 4.3 %collective-permute-done.10 = bf16[32,2048]{1,0:T(8,128)(2,1)S(1)} collective-permute-done((bf16[32,2048]{1,0:T(8,128)(2,1)S(1)}, bf16[32,2048]{1,0:T(8,128)(2,1)S(1)}, u32[]{:S(2)}, u32[]{:S(2)}) %collective-permute-start.10) | collective-permute-done | bytes 131104 | tf_op jit(solution)/shard_map/ppermute | solution.py:15
  126.8 2.4 collective-permute-start.11
  129.3 5.3 %collective-permute-done.11 = bf16[16,2048]{1,0:T(8,128)(2,1)S(1)} collective-permute-done((bf16[16,2048]{1,0:T(8,128)(2,1)S(1)}, bf16[16,2048]{1,0:T(8,128)(2,1)S(1)}, u32[]{:S(2)}, u32[]{:S(2)}) %collective-permute-start.11) | collective-permute-done | bytes 65568 | tf_op jit(solution)/shard_map/ppermute | solution.py:15
  134.6 4.2 %collective-permute-start.12 = (bf16[8,2048]{1,0:T(8,128)(2,1)S(1)}, bf16[8,2048]{1,0:T(8,128)(2,1)S(1)}, u32[]{:S(2)}, u32[]{:S(2)}) collective-permute-start(bf16[8,2048]{1,0:T(8,128)(2,1)S(1)} %select_convert_fusion.9), channel_id=1, source_target_pairs={{0,2},{1,3},{2,0},{3,1},{4,6},{5,7},{6,4},{7,5},{8,10},{9,11},{10,... | collective-permute-start | bytes 98312 | tf_op jit(solution)/shard_map/ppermute | solution.py:15
  140.7 4.1 %collective-permute-start.13 = (bf16[8,2048]{1,0:T(8,128)(2,1)S(1)}, bf16[8,2048]{1,0:T(8,128)(2,1)S(1)}, u32[]{:S(2)}, u32[]{:S(2)}) collective-permute-start(bf16[8,2048]{1,0:T(8,128)(2,1)S(1)} %fusion.41), channel_id=1, source_target_pairs={{704,0},{0,64},{64,128},{128,192},{192,256},{256,320},{320,384},{3... | collective-permute-start | bytes 98312 | tf_op jit(solution)/shard_map/ppermute | solution.py:21
  144.9 7.8 %collective-permute-done.13 = bf16[8,2048]{1,0:T(8,128)(2,1)S(1)} collective-permute-done((bf16[8,2048]{1,0:T(8,128)(2,1)S(1)}, bf16[8,2048]{1,0:T(8,128)(2,1)S(1)}, u32[]{:S(2)}, u32[]{:S(2)}) %collective-permute-start.13) | collective-permute-done | bytes 32800 | tf_op jit(solution)/shard_map/ppermute | solution.py:21
  152.9 3.9 %collective-permute-start.14 = (bf16[8,2048]{1,0:T(8,128)(2,1)S(1)}, bf16[8,2048]{1,0:T(8,128)(2,1)S(1)}, u32[]{:S(2)}, u32[]{:S(2)}) collective-permute-start(bf16[8,2048]{1,0:T(8,128)(2,1)S(1)} %fusion.36), channel_id=1, source_target_pairs={{0,2},{1,3},{2,0},{3,1},{4,6},{5,7},{6,4},{7,5},{8,10},{9,11},{10,... | collective-permute-start | bytes 98312 | tf_op jit(solution)/shard_map/ppermute | solution.py:15
  156.7 1.9 collective-permute-done.14
  158.7 3.5 %collective-permute-start.15 = (bf16[16,2048]{1,0:T(8,128)(2,1)S(1)}, bf16[16,2048]{1,0:T(8,128)(2,1)S(1)}, u32[]{:S(2)}, u32[]{:S(2)}) collective-permute-start(bf16[16,2048]{1,0:T(8,128)(2,1)S(1)} %maximum_select_fusion.21), channel_id=1, source_target_pairs={{0,4},{1,5},{2,6},{3,7},{4,0},{5,1},{6,2},{7,3},{8,12},{9,13},{10,... | collective-permute-start | bytes 196616 | tf_op jit(solution)/shard_map/ppermute | solution.py:15
  162.2 3.6 %collective-permute-done.15 = bf16[16,2048]{1,0:T(8,128)(2,1)S(1)} collective-permute-done((bf16[16,2048]{1,0:T(8,128)(2,1)S(1)}, bf16[16,2048]{1,0:T(8,128)(2,1)S(1)}, u32[]{:S(2)}, u32[]{:S(2)}) %collective-permute-start.15) | collective-permute-done | bytes 65568 | tf_op jit(solution)/shard_map/ppermute | solution.py:15
  165.8 2.7 collective-permute-start.16
  168.5 5.3 %collective-permute-done.16 = bf16[32,2048]{1,0:T(8,128)(2,1)S(1)} collective-permute-done((bf16[32,2048]{1,0:T(8,128)(2,1)S(1)}, bf16[32,2048]{1,0:T(8,128)(2,1)S(1)}, u32[]{:S(2)}, u32[]{:S(2)}) %collective-permute-start.16) | collective-permute-done | bytes 131104 | tf_op jit(solution)/shard_map/ppermute | solution.py:15
  173.9 4.7 %collective-permute-start.17 = (bf16[64,2048]{1,0:T(8,128)(2,1)S(1)}, bf16[64,2048]{1,0:T(8,128)(2,1)S(1)}, u32[]{:S(2)}, u32[]{:S(2)}) collective-permute-start(bf16[64,2048]{1,0:T(8,128)(2,1)S(1)} %maximum_select_fusion.5), channel_id=1, source_target_pairs={{0,16},{1,17},{2,18},{3,19},{4,20},{5,21},{6,22},{7,23},{8,24},{9,... | collective-permute-start | bytes 786440 | tf_op jit(solution)/shard_map/ppermute | solution.py:15
  180.5 5.2 %collective-permute-done.17 = bf16[64,2048]{1,0:T(8,128)(2,1)S(1)} collective-permute-done((bf16[64,2048]{1,0:T(8,128)(2,1)S(1)}, bf16[64,2048]{1,0:T(8,128)(2,1)S(1)}, u32[]{:S(2)}, u32[]{:S(2)}) %collective-permute-start.17) | collective-permute-done | bytes 262176 | tf_op jit(solution)/shard_map/ppermute | solution.py:15
  185.9 13.8 %collective-permute-start.18 = (bf16[128,2048]{1,0:T(8,128)(2,1)S(1)}, bf16[128,2048]{1,0:T(8,128)(2,1)S(1)}, u32[]{:S(2)}, u32[]{:S(2)}) collective-permute-start(bf16[128,2048]{1,0:T(8,128)(2,1)S(1)} %maximum_select_fusion.3), channel_id=1, source_target_pairs={{0,32},{1,33},{2,34},{3,35},{4,36},{5,37},{6,38},{7,39},{8,40},{9,... | collective-permute-start | bytes 1572872 | tf_op jit(solution)/shard_map/ppermute | solution.py:15
  199.6 1.9 collective-permute-start.20
  201.6 2.4 collective-permute-start.21
  204.0 10.4 %collective-permute-done.18 = bf16[128,2048]{1,0:T(8,128)(2,1)S(1)} collective-permute-done((bf16[128,2048]{1,0:T(8,128)(2,1)S(1)}, bf16[128,2048]{1,0:T(8,128)(2,1)S(1)}, u32[]{:S(2)}, u32[]{:S(2)}) %collective-permute-start.18) | collective-permute-done | bytes 524320 | tf_op jit(solution)/shard_map/ppermute | solution.py:15
  216.0 3.0 %fusion.20 = f32[256,2048]{1,0:T(8,128)S(1)} fusion(bf16[128,2048]{1,0:T(8,128)(2,1)} %collective-permute-done.21, bf16[128,2048]{1,0:T(8,128)(2,1)} %get-tuple-element.9, f32[256,256]{1,0:T(8,128)S(1)} %fusion.12, bf16[2048,128]{1,0:T(8,128)(2,1)} %copy-done.8, bf16[2048,128]{1,0:T(8,128)(2,1)S(1)} %get-tuple-element.5, ...), kind=kOutput, calls=%fused_computation.22 | convolution fusion | flops 546177024 | bytes 5505025 | tf_op jit(solution)/shard_map/dot_general | solution.py:28
  219.1 5.3 %collective-permute-start.22 = (bf16[128,2048]{1,0:T(8,128)(2,1)S(1)}, bf16[128,2048]{1,0:T(8,128)(2,1)S(1)}, u32[]{:S(2)}, u32[]{:S(2)}) collective-permute-start(bf16[128,2048]{1,0:T(8,128)(2,1)S(1)} %select_convert_fusion), channel_id=1, source_target_pairs={{0,32},{1,33},{2,34},{3,35},{4,36},{5,37},{6,38},{7,39},{8,40},{9,... | collective-permute-start | bytes 1572872 | tf_op jit(solution)/shard_map/ppermute | solution.py:15
  224.4 16.7 %collective-permute-done.22 = bf16[128,2048]{1,0:T(8,128)(2,1)S(1)} collective-permute-done((bf16[128,2048]{1,0:T(8,128)(2,1)S(1)}, bf16[128,2048]{1,0:T(8,128)(2,1)S(1)}, u32[]{:S(2)}, u32[]{:S(2)}) %collective-permute-start.22) | collective-permute-done | bytes 524320 | tf_op jit(solution)/shard_map/ppermute | solution.py:15
  243.2 8.9 %collective-permute-done.23 = bf16[64,2048]{1,0:T(8,128)(2,1)S(1)} collective-permute-done((bf16[64,2048]{1,0:T(8,128)(2,1)S(1)}, bf16[64,2048]{1,0:T(8,128)(2,1)S(1)}, u32[]{:S(2)}, u32[]{:S(2)}) %collective-permute-start.23) | collective-permute-done | bytes 262176 | tf_op jit(solution)/shard_map/ppermute | solution.py:15
  252.3 4.5 %collective-permute-start.24 = (bf16[32,2048]{1,0:T(8,128)(2,1)S(1)}, bf16[32,2048]{1,0:T(8,128)(2,1)S(1)}, u32[]{:S(2)}, u32[]{:S(2)}) collective-permute-start(bf16[32,2048]{1,0:T(8,128)(2,1)S(1)} %select_convert_fusion.4), channel_id=1, source_target_pairs={{0,8},{1,9},{2,10},{3,11},{4,12},{5,13},{6,14},{7,15},{8,0},{9,1},... | collective-permute-start | bytes 393224 | tf_op jit(solution)/shard_map/ppermute | solution.py:15
  256.8 2.9 collective-permute-done.24
  259.8 16.8 %collective-permute-start.25 = (bf16[16,2048]{1,0:T(8,128)(2,1)S(1)}, bf16[16,2048]{1,0:T(8,128)(2,1)S(1)}, u32[]{:S(2)}, u32[]{:S(2)}) collective-permute-start(bf16[16,2048]{1,0:T(8,128)(2,1)S(1)} %select_convert_fusion.6), channel_id=1, source_target_pairs={{0,4},{1,5},{2,6},{3,7},{4,0},{5,1},{6,2},{7,3},{8,12},{9,13},{10,... | collective-permute-start | bytes 196616 | tf_op jit(solution)/shard_map/ppermute | solution.py:15
  276.6 2.2 collective-permute-done.25
  280.8 3.9 %collective-permute-done.26 = bf16[8,2048]{1,0:T(8,128)(2,1)S(1)} collective-permute-done((bf16[8,2048]{1,0:T(8,128)(2,1)S(1)}, bf16[8,2048]{1,0:T(8,128)(2,1)S(1)}, u32[]{:S(2)}, u32[]{:S(2)}) %collective-permute-start.26) | collective-permute-done | bytes 32800 | tf_op jit(solution)/shard_map/ppermute | solution.py:15
  284.7 2.7 collective-permute-start.27
  287.4 9.2 %collective-permute-done.27 = bf16[8,2048]{1,0:T(8,128)(2,1)S(1)} collective-permute-done((bf16[8,2048]{1,0:T(8,128)(2,1)S(1)}, bf16[8,2048]{1,0:T(8,128)(2,1)S(1)}, u32[]{:S(2)}, u32[]{:S(2)}) %collective-permute-start.27) | collective-permute-done | bytes 32800 | tf_op jit(solution)/shard_map/ppermute | solution.py:21
  (70 shorter events, 21.3 us)
Async XLA Ops:
  0.0 37.8 %copy-start = (bf16[1,2,2048,128]{3,2,1,0:T(8,128)(2,1)S(1)}, bf16[1,2,2048,128]{3,2,1,0:T(8,128)(2,1)}, u32[]{:S(2)}) copy-start(bf16[1,2,2048,128]{3,2,1,0:T(8,128)(2,1)} %param.8) | copy-start | bytes 3145732
  7.9 6.2 %collective-permute-start = (bf16[8,2048]{1,0:T(8,128)(2,1)S(1)}, bf16[8,2048]{1,0:T(8,128)(2,1)S(1)}, u32[]{:S(2)}, u32[]{:S(2)}) collective-permute-start(bf16[8,2048]{1,0:T(8,128)(2,1)S(1)} %fusion.40), channel_id=1, source_target_pairs={{0,2},{1,3},{2,0},{3,1},{4,6},{5,7},{6,4},{7,5},{8,10},{9,11},{10,... | collective-permute-start | bytes 98312 | tf_op jit(solution)/shard_map/ppermute | solution.py:15
  14.1 8.5 %collective-permute-start.1 = (bf16[16,2048]{1,0:T(8,128)(2,1)S(1)}, bf16[16,2048]{1,0:T(8,128)(2,1)S(1)}, u32[]{:S(2)}, u32[]{:S(2)}) collective-permute-start(bf16[16,2048]{1,0:T(8,128)(2,1)S(1)} %maximum_select_fusion.20), channel_id=1, source_target_pairs={{0,4},{1,5},{2,6},{3,7},{4,0},{5,1},{6,2},{7,3},{8,12},{9,13},{10,... | collective-permute-start | bytes 196616 | tf_op jit(solution)/shard_map/ppermute | solution.py:15
  22.6 6.9 %collective-permute-start.2 = (bf16[32,2048]{1,0:T(8,128)(2,1)S(1)}, bf16[32,2048]{1,0:T(8,128)(2,1)S(1)}, u32[]{:S(2)}, u32[]{:S(2)}) collective-permute-start(bf16[32,2048]{1,0:T(8,128)(2,1)S(1)} %maximum_select_fusion.18), channel_id=1, source_target_pairs={{0,8},{1,9},{2,10},{3,11},{4,12},{5,13},{6,14},{7,15},{8,0},{9,1},... | collective-permute-start | bytes 393224 | tf_op jit(solution)/shard_map/ppermute | solution.py:15
  29.5 13.5 %collective-permute-start.3 = (bf16[64,2048]{1,0:T(8,128)(2,1)S(1)}, bf16[64,2048]{1,0:T(8,128)(2,1)}, u32[]{:S(2)}, u32[]{:S(2)}) collective-permute-start(bf16[64,2048]{1,0:T(8,128)(2,1)S(1)} %maximum_select_fusion.4), channel_id=1, source_target_pairs={{0,16},{1,17},{2,18},{3,19},{4,20},{5,21},{6,22},{7,23},{8,24},{9,... | collective-permute-start | bytes 786440 | tf_op jit(solution)/shard_map/ppermute | solution.py:15
  35.7 16.2 %copy-start.1 = (bf16[1,2,128,2048]{3,2,1,0:T(8,128)(2,1)S(1)}, bf16[1,2,128,2048]{3,2,1,0:T(8,128)(2,1)}, u32[]{:S(2)}) copy-start(bf16[1,2,128,2048]{3,2,1,0:T(8,128)(2,1)} %param.9) | copy-start | bytes 3145732
  35.7 19.1 %collective-permute-start.5 = (bf16[2048,128]{1,0:T(8,128)(2,1)}, bf16[2048,128]{1,0:T(8,128)(2,1)}, u32[]{:S(2)}, u32[]{:S(2)}) collective-permute-start(bf16[2048,128]{1,0:T(8,128)(2,1)} %get-tuple-element.8), channel_id=1, source_target_pairs={{0,1},{1,0},{2,3},{3,2},{4,5},{5,4},{6,7},{7,6},{8,9},{9,8},{10,11... | collective-permute-start | bytes 1572872 | tf_op jit(solution)/shard_map/ppermute | solution.py:15
  37.9 38.4 %copy-start.4 = (bf16[2048,128]{1,0:T(8,128)(2,1)}, bf16[2048,128]{1,0:T(8,128)(2,1)S(1)}, u32[]{:S(2)}) copy-start(bf16[2048,128]{1,0:T(8,128)(2,1)S(1)} %get-tuple-element.6) | copy-start | bytes 1572868
  37.9 38.4 %collective-permute-start.6 = (bf16[2048,128]{1,0:T(8,128)(2,1)S(1)}, bf16[2048,128]{1,0:T(8,128)(2,1)}, u32[]{:S(2)}, u32[]{:S(2)}) collective-permute-start(bf16[2048,128]{1,0:T(8,128)(2,1)S(1)} %get-tuple-element.6), channel_id=1, source_target_pairs={{0,1},{1,0},{2,3},{3,2},{4,5},{5,4},{6,7},{7,6},{8,9},{9,8},{10,11... | collective-permute-start | bytes 1572872 | tf_op jit(solution)/shard_map/ppermute | solution.py:15
  44.2 30.1 %collective-permute-start.4 = (bf16[128,2048]{1,0:T(8,128)(2,1)S(1)}, bf16[128,2048]{1,0:T(8,128)(2,1)}, u32[]{:S(2)}, u32[]{:S(2)}) collective-permute-start(bf16[128,2048]{1,0:T(8,128)(2,1)S(1)} %maximum_select_fusion.2), channel_id=1, source_target_pairs={{0,32},{1,33},{2,34},{3,35},{4,36},{5,37},{6,38},{7,39},{8,40},{9,... | collective-permute-start | bytes 1572872 | tf_op jit(solution)/shard_map/ppermute | solution.py:15
  52.9 23.4 %copy-start.5 = (bf16[128,2048]{1,0:T(8,128)(2,1)}, bf16[128,2048]{1,0:T(8,128)(2,1)S(1)}, u32[]{:S(2)}) copy-start(bf16[128,2048]{1,0:T(8,128)(2,1)S(1)} %get-tuple-element.10) | copy-start | bytes 1572868
  52.9 23.4 %collective-permute-start.7 = (bf16[128,2048]{1,0:T(8,128)(2,1)S(1)}, bf16[128,2048]{1,0:T(8,128)(2,1)}, u32[]{:S(2)}, u32[]{:S(2)}) collective-permute-start(bf16[128,2048]{1,0:T(8,128)(2,1)S(1)} %get-tuple-element.10), channel_id=1, source_target_pairs={{0,1},{1,0},{2,3},{3,2},{4,5},{5,4},{6,7},{7,6},{8,9},{9,8},{10,11... | collective-permute-start | bytes 1572872 | tf_op jit(solution)/shard_map/ppermute | solution.py:15
  79.5 22.9 %collective-permute-start.8 = (bf16[128,2048]{1,0:T(8,128)(2,1)S(1)}, bf16[128,2048]{1,0:T(8,128)(2,1)S(1)}, u32[]{:S(2)}, u32[]{:S(2)}) collective-permute-start(bf16[128,2048]{1,0:T(8,128)(2,1)S(1)} %select_convert_fusion.1), channel_id=1, source_target_pairs={{0,32},{1,33},{2,34},{3,35},{4,36},{5,37},{6,38},{7,39},{8,40},{9,... | collective-permute-start | bytes 1572872 | tf_op jit(solution)/shard_map/ppermute | solution.py:15
  102.6 38.1 %copy-start.6 = (bf16[1,8,2048]{2,1,0:T(8,128)(2,1)S(1)}, bf16[1,8,2048]{2,1,0:T(8,128)(2,1)}, u32[]{:S(2)}) copy-start(bf16[1,8,2048]{2,1,0:T(8,128)(2,1)} %param.6) | copy-start | bytes 98308
  102.6 17.0 %collective-permute-start.9 = (bf16[64,2048]{1,0:T(8,128)(2,1)S(1)}, bf16[64,2048]{1,0:T(8,128)(2,1)S(1)}, u32[]{:S(2)}, u32[]{:S(2)}) collective-permute-start(bf16[64,2048]{1,0:T(8,128)(2,1)S(1)} %select_convert_fusion.3), channel_id=1, source_target_pairs={{0,16},{1,17},{2,18},{3,19},{4,20},{5,21},{6,22},{7,23},{8,24},{9,... | collective-permute-start | bytes 786440 | tf_op jit(solution)/shard_map/ppermute | solution.py:15
  119.7 58.9 %copy-start.2 = (bf16[2048,128]{1,0:T(8,128)(2,1)S(1)}, bf16[2048,128]{1,0:T(8,128)(2,1)}, u32[]{:S(2)}) copy-start(bf16[2048,128]{1,0:T(8,128)(2,1)} %get-tuple-element.7) | copy-start | bytes 1572868
  119.7 81.9 %copy-start.3 = (bf16[128,2048]{1,0:T(8,128)(2,1)S(1)}, bf16[128,2048]{1,0:T(8,128)(2,1)}, u32[]{:S(2)}) copy-start(bf16[128,2048]{1,0:T(8,128)(2,1)} %get-tuple-element.9) | copy-start | bytes 1572868
  119.8 7.0 %collective-permute-start.10 = (bf16[32,2048]{1,0:T(8,128)(2,1)S(1)}, bf16[32,2048]{1,0:T(8,128)(2,1)S(1)}, u32[]{:S(2)}, u32[]{:S(2)}) collective-permute-start(bf16[32,2048]{1,0:T(8,128)(2,1)S(1)} %select_convert_fusion.5), channel_id=1, source_target_pairs={{0,8},{1,9},{2,10},{3,11},{4,12},{5,13},{6,14},{7,15},{8,0},{9,1},... | collective-permute-start | bytes 393224 | tf_op jit(solution)/shard_map/ppermute | solution.py:15
  126.8 7.8 %collective-permute-start.11 = (bf16[16,2048]{1,0:T(8,128)(2,1)S(1)}, bf16[16,2048]{1,0:T(8,128)(2,1)S(1)}, u32[]{:S(2)}, u32[]{:S(2)}) collective-permute-start(bf16[16,2048]{1,0:T(8,128)(2,1)S(1)} %select_convert_fusion.7), channel_id=1, source_target_pairs={{0,4},{1,5},{2,6},{3,7},{4,0},{5,1},{6,2},{7,3},{8,12},{9,13},{10,... | collective-permute-start | bytes 196616 | tf_op jit(solution)/shard_map/ppermute | solution.py:15
  134.6 6.1 %collective-permute-start.12 = (bf16[8,2048]{1,0:T(8,128)(2,1)S(1)}, bf16[8,2048]{1,0:T(8,128)(2,1)S(1)}, u32[]{:S(2)}, u32[]{:S(2)}) collective-permute-start(bf16[8,2048]{1,0:T(8,128)(2,1)S(1)} %select_convert_fusion.9), channel_id=1, source_target_pairs={{0,2},{1,3},{2,0},{3,1},{4,6},{5,7},{6,4},{7,5},{8,10},{9,11},{10,... | collective-permute-start | bytes 98312 | tf_op jit(solution)/shard_map/ppermute | solution.py:15
  140.7 11.9 %collective-permute-start.13 = (bf16[8,2048]{1,0:T(8,128)(2,1)S(1)}, bf16[8,2048]{1,0:T(8,128)(2,1)S(1)}, u32[]{:S(2)}, u32[]{:S(2)}) collective-permute-start(bf16[8,2048]{1,0:T(8,128)(2,1)S(1)} %fusion.41), channel_id=1, source_target_pairs={{704,0},{0,64},{64,128},{128,192},{192,256},{256,320},{320,384},{3... | collective-permute-start | bytes 98312 | tf_op jit(solution)/shard_map/ppermute | solution.py:21
  152.9 5.8 %collective-permute-start.14 = (bf16[8,2048]{1,0:T(8,128)(2,1)S(1)}, bf16[8,2048]{1,0:T(8,128)(2,1)S(1)}, u32[]{:S(2)}, u32[]{:S(2)}) collective-permute-start(bf16[8,2048]{1,0:T(8,128)(2,1)S(1)} %fusion.36), channel_id=1, source_target_pairs={{0,2},{1,3},{2,0},{3,1},{4,6},{5,7},{6,4},{7,5},{8,10},{9,11},{10,... | collective-permute-start | bytes 98312 | tf_op jit(solution)/shard_map/ppermute | solution.py:15
  158.7 7.1 %collective-permute-start.15 = (bf16[16,2048]{1,0:T(8,128)(2,1)S(1)}, bf16[16,2048]{1,0:T(8,128)(2,1)S(1)}, u32[]{:S(2)}, u32[]{:S(2)}) collective-permute-start(bf16[16,2048]{1,0:T(8,128)(2,1)S(1)} %maximum_select_fusion.21), channel_id=1, source_target_pairs={{0,4},{1,5},{2,6},{3,7},{4,0},{5,1},{6,2},{7,3},{8,12},{9,13},{10,... | collective-permute-start | bytes 196616 | tf_op jit(solution)/shard_map/ppermute | solution.py:15
  165.8 8.0 %collective-permute-start.16 = (bf16[32,2048]{1,0:T(8,128)(2,1)S(1)}, bf16[32,2048]{1,0:T(8,128)(2,1)S(1)}, u32[]{:S(2)}, u32[]{:S(2)}) collective-permute-start(bf16[32,2048]{1,0:T(8,128)(2,1)S(1)} %maximum_select_fusion.19), channel_id=1, source_target_pairs={{0,8},{1,9},{2,10},{3,11},{4,12},{5,13},{6,14},{7,15},{8,0},{9,1},... | collective-permute-start | bytes 393224 | tf_op jit(solution)/shard_map/ppermute | solution.py:15
  173.9 11.9 %collective-permute-start.17 = (bf16[64,2048]{1,0:T(8,128)(2,1)S(1)}, bf16[64,2048]{1,0:T(8,128)(2,1)S(1)}, u32[]{:S(2)}, u32[]{:S(2)}) collective-permute-start(bf16[64,2048]{1,0:T(8,128)(2,1)S(1)} %maximum_select_fusion.5), channel_id=1, source_target_pairs={{0,16},{1,17},{2,18},{3,19},{4,20},{5,21},{6,22},{7,23},{8,24},{9,... | collective-permute-start | bytes 786440 | tf_op jit(solution)/shard_map/ppermute | solution.py:15
  178.6 25.4 %collective-permute-start.19 = (bf16[2048,128]{1,0:T(8,128)(2,1)S(1)}, bf16[2048,128]{1,0:T(8,128)(2,1)S(1)}, u32[]{:S(2)}, u32[]{:S(2)}) collective-permute-start(bf16[2048,128]{1,0:T(8,128)(2,1)S(1)} %copy-done.2), channel_id=1, source_target_pairs={{0,1},{1,0},{2,3},{3,2},{4,5},{5,4},{6,7},{7,6},{8,9},{9,8},{10,11... | collective-permute-start | bytes 1572872 | tf_op jit(solution)/shard_map/ppermute | solution.py:15
  185.9 28.5 %collective-permute-start.18 = (bf16[128,2048]{1,0:T(8,128)(2,1)S(1)}, bf16[128,2048]{1,0:T(8,128)(2,1)S(1)}, u32[]{:S(2)}, u32[]{:S(2)}) collective-permute-start(bf16[128,2048]{1,0:T(8,128)(2,1)S(1)} %maximum_select_fusion.3), channel_id=1, source_target_pairs={{0,32},{1,33},{2,34},{3,35},{4,36},{5,37},{6,38},{7,39},{8,40},{9,... | collective-permute-start | bytes 1572872 | tf_op jit(solution)/shard_map/ppermute | solution.py:15
  199.6 15.6 %collective-permute-start.20 = (bf16[2048,128]{1,0:T(8,128)(2,1)S(1)}, bf16[2048,128]{1,0:T(8,128)(2,1)S(1)}, u32[]{:S(2)}, u32[]{:S(2)}) collective-permute-start(bf16[2048,128]{1,0:T(8,128)(2,1)S(1)} %get-tuple-element.5), channel_id=1, source_target_pairs={{0,1},{1,0},{2,3},{3,2},{4,5},{5,4},{6,7},{7,6},{8,9},{9,8},{10,11... | collective-permute-start | bytes 1572872 | tf_op jit(solution)/shard_map/ppermute | solution.py:15
  201.6 14.4 %collective-permute-start.21 = (bf16[128,2048]{1,0:T(8,128)(2,1)S(1)}, bf16[128,2048]{1,0:T(8,128)(2,1)}, u32[]{:S(2)}, u32[]{:S(2)}) collective-permute-start(bf16[128,2048]{1,0:T(8,128)(2,1)S(1)} %copy-done.3), channel_id=1, source_target_pairs={{0,1},{1,0},{2,3},{3,2},{4,5},{5,4},{6,7},{7,6},{8,9},{9,8},{10,11... | collective-permute-start | bytes 1572872 | tf_op jit(solution)/shard_map/ppermute | solution.py:15
  214.4 0.8 copy-start.7
  215.2 0.8 copy-start.8
  219.1 22.0 %collective-permute-start.22 = (bf16[128,2048]{1,0:T(8,128)(2,1)S(1)}, bf16[128,2048]{1,0:T(8,128)(2,1)S(1)}, u32[]{:S(2)}, u32[]{:S(2)}) collective-permute-start(bf16[128,2048]{1,0:T(8,128)(2,1)S(1)} %select_convert_fusion), channel_id=1, source_target_pairs={{0,32},{1,33},{2,34},{3,35},{4,36},{5,37},{6,38},{7,39},{8,40},{9,... | collective-permute-start | bytes 1572872 | tf_op jit(solution)/shard_map/ppermute | solution.py:15
  241.3 10.8 %collective-permute-start.23 = (bf16[64,2048]{1,0:T(8,128)(2,1)S(1)}, bf16[64,2048]{1,0:T(8,128)(2,1)S(1)}, u32[]{:S(2)}, u32[]{:S(2)}) collective-permute-start(bf16[64,2048]{1,0:T(8,128)(2,1)S(1)} %select_convert_fusion.2), channel_id=1, source_target_pairs={{0,16},{1,17},{2,18},{3,19},{4,20},{5,21},{6,22},{7,23},{8,24},{9,... | collective-permute-start | bytes 786440 | tf_op jit(solution)/shard_map/ppermute | solution.py:15
  252.3 7.5 %collective-permute-start.24 = (bf16[32,2048]{1,0:T(8,128)(2,1)S(1)}, bf16[32,2048]{1,0:T(8,128)(2,1)S(1)}, u32[]{:S(2)}, u32[]{:S(2)}) collective-permute-start(bf16[32,2048]{1,0:T(8,128)(2,1)S(1)} %select_convert_fusion.4), channel_id=1, source_target_pairs={{0,8},{1,9},{2,10},{3,11},{4,12},{5,13},{6,14},{7,15},{8,0},{9,1},... | collective-permute-start | bytes 393224 | tf_op jit(solution)/shard_map/ppermute | solution.py:15
  259.8 19.1 %collective-permute-start.25 = (bf16[16,2048]{1,0:T(8,128)(2,1)S(1)}, bf16[16,2048]{1,0:T(8,128)(2,1)S(1)}, u32[]{:S(2)}, u32[]{:S(2)}) collective-permute-start(bf16[16,2048]{1,0:T(8,128)(2,1)S(1)} %select_convert_fusion.6), channel_id=1, source_target_pairs={{0,4},{1,5},{2,6},{3,7},{4,0},{5,1},{6,2},{7,3},{8,12},{9,13},{10,... | collective-permute-start | bytes 196616 | tf_op jit(solution)/shard_map/ppermute | solution.py:15
  278.9 5.8 %collective-permute-start.26 = (bf16[8,2048]{1,0:T(8,128)(2,1)S(1)}, bf16[8,2048]{1,0:T(8,128)(2,1)S(1)}, u32[]{:S(2)}, u32[]{:S(2)}) collective-permute-start(bf16[8,2048]{1,0:T(8,128)(2,1)S(1)} %select_convert_fusion.8), channel_id=1, source_target_pairs={{0,2},{1,3},{2,0},{3,1},{4,6},{5,7},{6,4},{7,5},{8,10},{9,11},{10,... | collective-permute-start | bytes 98312 | tf_op jit(solution)/shard_map/ppermute | solution.py:15
  284.7 11.8 %collective-permute-start.27 = (bf16[8,2048]{1,0:T(8,128)(2,1)S(1)}, bf16[8,2048]{1,0:T(8,128)(2,1)S(1)}, u32[]{:S(2)}, u32[]{:S(2)}) collective-permute-start(bf16[8,2048]{1,0:T(8,128)(2,1)S(1)} %fusion.37), channel_id=1, source_target_pairs={{704,0},{0,64},{64,128},{128,192},{192,256},{256,320},{320,384},{3... | collective-permute-start | bytes 98312 | tf_op jit(solution)/shard_map/ppermute | solution.py:21
where the time goes:
time: 299 us; the launch traced here: 297 us
  waiting for transfers between devices  146 us (49%)
  starting transfers between devices  126 us (42%)
  matrix products  8.67 us (3%)
  local copies, waits for them, and re-layouts  7.06 us (2%)
  between operations  4.54 us (2%)
  other arithmetic  4.48 us (1%)
    ppermute x26, waiting for transfers between devices, from_partner(): return lax.ppermute(value, axis, pairs)  129 us
    ppermute x26, starting transfers between devices, from_partner(): return lax.ppermute(value, axis, pairs)  120 us
    ppermute x2, waiting for transfers between devices, passed_along(): return lax.ppermute(block, axis, route)  17 us
    ppermute x2, starting transfers between devices, passed_along(): return lax.ppermute(block, axis, route)  6.76 us
    dot_general x2, matrix products, feed_forward(): return jnp.dot(hidden, down_slab, preferred_element_type=jnp.float32)  6.12 us
  transfers between devices with their start and end apart: 28, of which 22 were waited for; matrix products, arithmetic and copies ran while one was open for 2% of the time, Pallas kernels for 0%

commit v1 on v0

v1 whole, which is shorter than its diff:
```python
import jax
import jax.numpy as jnp
from jax import lax
from jax.sharding import PartitionSpec as P

TICKS = 2


epsilon = 0.5


def from_partner(value, axis, bit):
    mask = 2**bit
    pairs = [(source, source ^ mask) for source in range(lax.axis_size(axis))]
    return lax.ppermute(value, axis, pairs)


def passed_along(block, axis, distance):
    devices = range(lax.axis_size(axis))
    route = [((i - distance) % len(devices), i) for i in devices]
    return lax.ppermute(block, axis, route)


def same_core(axis):
    size = lax.axis_size(axis)
    return [[device for device in range(size) if device & 1 == core] for core in range(2)]


def exchange(blocks, axis, groups):
    return lax.all_to_all(blocks, axis, 0, 0, tiled=True, axis_index_groups=groups)


def feed_forward(block_rows, gate_slab, up_slab, down_slab):
    gate_value = jnp.dot(block_rows, gate_slab, preferred_element_type=jnp.float32)
    up_value = jnp.dot(block_rows, up_slab, preferred_element_type=jnp.float32)
    hidden = (jax.nn.silu(gate_value) * up_value).astype(jnp.bfloat16)
    return jnp.dot(hidden, down_slab, preferred_element_type=jnp.float32)


def on_device(buffer, gate_weight, up_weight, down_weight, norm_gain, repeat_index):
    current = buffer[0]
    groups = same_core("dp")
    members = len(groups[0])
    mine = (gate_weight[0], up_weight[0], down_weight[0])
    theirs = from_partner(mine, "dp", 0)
    for tick_index in range(TICKS):
        chosen = repeat_index[tick_index, 0]

        def pick(stack):
            return lax.dynamic_index_in_dim(stack, chosen, 0, keepdims=False)

        gain_row = pick(norm_gain[0])
        gate_both = jnp.concatenate([pick(mine[0]), pick(theirs[0])], axis=1)
        up_both = jnp.concatenate([pick(mine[1]), pick(theirs[1])], axis=1)
        down_both = jnp.concatenate([pick(mine[2]), pick(theirs[2])], axis=0)
        widened = current.astype(jnp.float32)
        squares = jnp.mean(widened * widened, axis=-1, keepdims=True)
        normed = (widened * lax.rsqrt(squares + epsilon) * gain_row[None, :]).astype(jnp.bfloat16)
        rows = normed.shape[0]
        copies = jnp.broadcast_to(normed[None], (members, *normed.shape)).reshape(members * rows, -1)
        group_block = exchange(copies, "dp", groups)
        partial_value = feed_forward(group_block, gate_both, up_both, down_both)
        parts = exchange(partial_value.astype(jnp.bfloat16), "dp", groups)
        output = jnp.sum(parts.reshape(members, rows, -1).astype(jnp.float32), axis=0)
        advanced = (widened + output).astype(jnp.bfloat16)
        current = passed_along(advanced, "section", 1)
    return current[None]


def solution(mesh):
    placed = (
        P("section", "dp", None),
        P("section", None, None, "dp"),
        P("section", None, None, "dp"),
        P("section", None, "dp", None),
        P("section", None, None),
        P(None, "section"),
    )
    return jax.shard_map(
        on_device, mesh=mesh, in_specs=placed, out_specs=P("section", "dp", None), check_vma=False
    )
```

time: 299 us -> 188 us (0.63)
  waiting for transfers between devices: 146 us -> 22.6 us
  blocking collectives: 0 us -> 99.1 us
  starting transfers between devices: 126 us -> 38 us
  local copies, waits for them, and re-layouts: 7.06 us -> 11.9 us
    ppermute x26 -> x3, waiting for transfers between devices: 129 us -> 0.01 us  [from_partner(): return lax.ppermute(value, axis, pairs)]
    ppermute x26 -> x3, starting transfers between devices: 120 us -> 6.25 us  [from_partner(): return lax.ppermute(value, axis, pairs)]
    all_to_all x0 -> x3, blocking collectives: none -> 99.1 us  [exchange(): lax.all_to_all(blocks, axis, 0, 0, tiled=True, axis_index_groups=groups)]
    all_to_all x0 -> x1, waiting for transfers between devices: none -> 13.6 us  [exchange(): lax.all_to_all(blocks, axis, 0, 0, tiled=True, axis_index_groups=groups)]
    all_to_all x0 -> x1, starting transfers between devices: none -> 12.7 us  [exchange(): lax.all_to_all(blocks, axis, 0, 0, tiled=True, axis_index_groups=groups)]
    ppermute x2, starting transfers between devices: 6.76 us -> 19.1 us  [passed_along(): return lax.ppermute(block, axis, route)]
    ppermute x2, waiting for transfers between devices: 17 us -> 9.05 us  [passed_along(): return lax.ppermute(block, axis, route)]
  transfers between devices with their start and end apart: 28 -> 6, of which waited for: 22 -> 3; matrix products, arithmetic and copies ran while one was open for 2% -> 3% of each run, Pallas kernels for 0% -> 0%
where the time goes in v1:
time: 188 us; the launch traced here: 184 us
  blocking collectives  99.1 us (53%)
  starting transfers between devices  38 us (20%)
  waiting for transfers between devices  22.6 us (12%)
  local copies, waits for them, and re-layouts  11.9 us (6%)
  matrix products  5.99 us (3%)
  between operations  4.01 us (2%)
  other arithmetic  2.27 us (1%)
    all_to_all x3, blocking collectives, exchange(): lax.all_to_all(blocks, axis, 0, 0, tiled=True, axis_index_groups=groups)  99.1 us
    ppermute x2, starting transfers between devices, passed_along(): return lax.ppermute(block, axis, route)  19.1 us
    all_to_all x1, waiting for transfers between devices, exchange(): lax.all_to_all(blocks, axis, 0, 0, tiled=True, axis_index_groups=groups)  13.6 us
    all_to_all x1, starting transfers between devices, exchange(): lax.all_to_all(blocks, axis, 0, 0, tiled=True, axis_index_groups=groups)  12.7 us
    ppermute x2, waiting for transfers between devices, passed_along(): return lax.ppermute(block, axis, route)  9.05 us
    ppermute x3, starting transfers between devices, from_partner(): return lax.ppermute(value, axis, pairs)  6.25 us
    squeeze x6, local copies, waits for them, and re-layouts, pick(): return lax.dynamic_index_in_dim(stack, chosen, 0, keepdims=False)  5.35 us
    dot_general x2, matrix products, feed_forward(): return jnp.dot(hidden, down_slab, preferred_element_type=jnp.float32)  5.12 us
  transfers between devices with their start and end apart: 6, of which 3 were waited for; matrix products, arithmetic and copies ran while one was open for 3% of the time, Pallas kernels for 0%

profile of v1, /device:TPU:56, one launch (start us, length us, event | category | flops | bytes accessed | tf_op | source)
XLA Modules:
  0.0 183.8 jit_solution(15569328129163744706)
XLA Ops:
  0.0 1.3 fusion.67
  3.9 0.9 fusion.50
  6.1 0.8 constant_dynamic-slice_fusion
  6.9 0.8 fusion.58
  7.8 1.1 broadcast_in_dim.9
  8.8 0.0 copy-start
  8.8 0.0 copy-start.1
  8.8 12.7 %all-to-all-start = ((bf16[32,8,2048]{2,1,0:T(8,128)(2,1)}), bf16[32,8,2048]{2,1,0:T(8,128)(2,1)S(1)}, u32[]{:S(2)}, u32[]{:S(2)}) async-start(bf16[32,8,2048]{2,1,0:T(8,128)(2,1)} %broadcast_in_dim.9), calls=%async_computation | async-start | bytes 2097152 | tf_op jit(solution)/shard_map/all_to_all | solution.py:30
  21.5 0.0 copy-done
  21.5 1.9 %collective-permute-start.2 = (bf16[2,128,2048]{2,1,0:T(8,128)(2,1)S(1)}, bf16[2,128,2048]{2,1,0:T(8,128)(2,1)S(1)}, u32[]{:S(2)}, u32[]{:S(2)}) collective-permute-start(bf16[2,128,2048]{2,1,0:T(8,128)(2,1)S(1)} %bitcast.62), channel_id=1, source_target_pairs={{0,1},{1,0},{2,3},{3,2},{4,5},{5,4},{6,7},{7,6},{8,9},{9,8},{10,11... | collective-permute-start | bytes 3145736 | tf_op jit(solution)/shard_map/ppermute | solution.py:15
  23.5 0.0 copy-done.1
  23.5 2.4 %collective-permute-start.1 = (bf16[2,2048,128]{2,1,0:T(8,128)(2,1)S(1)}, bf16[2,2048,128]{2,1,0:T(8,128)(2,1)S(1)}, u32[]{:S(2)}, u32[]{:S(2)}) collective-permute-start(bf16[2,2048,128]{2,1,0:T(8,128)(2,1)S(1)} %bitcast.63), channel_id=1, source_target_pairs={{0,1},{1,0},{2,3},{3,2},{4,5},{5,4},{6,7},{7,6},{8,9},{9,8},{10,11... | collective-permute-start | bytes 3145736 | tf_op jit(solution)/shard_map/ppermute | solution.py:15
  25.9 1.9 %collective-permute-start = (bf16[2,2048,128]{2,1,0:T(8,128)(2,1)}, bf16[2,2048,128]{2,1,0:T(8,128)(2,1)S(1)}, u32[]{:S(2)}, u32[]{:S(2)}) collective-permute-start(bf16[2,2048,128]{2,1,0:T(8,128)(2,1)} %bitcast.64), channel_id=1, source_target_pairs={{0,1},{1,0},{2,3},{3,2},{4,5},{5,4},{6,7},{7,6},{8,9},{9,8},{10,11... | collective-permute-start | bytes 3145736 | tf_op jit(solution)/shard_map/ppermute | solution.py:15
  27.8 1.1 dynamic-slice_bitcast_fusion.7
  28.9 1.0 dynamic-slice_bitcast_fusion.9
  29.9 0.6 copy-done.2
  30.5 1.0 dynamic-slice_bitcast_fusion.5
  31.5 0.0 collective-permute-done.2
  31.5 1.0 dynamic-slice_bitcast_fusion.6
  32.6 0.0 collective-permute-done.1
  32.6 1.1 dynamic-slice_bitcast_fusion.8
  33.7 0.0 collective-permute-done
  33.7 0.1 dynamic-slice_bitcast_fusion.4
  33.7 13.6 %all-to-all-done = bf16[32,8,2048]{2,1,0:T(8,128)(2,1)S(1)} async-done(((bf16[32,8,2048]{2,1,0:T(8,128)(2,1)}), bf16[32,8,2048]{2,1,0:T(8,128)(2,1)S(1)}, u32[]{:S(2)}, u32[]{:S(2)}) %all-to-all-start) | async-done | bytes 1048608 | tf_op jit(solution)/shard_map/all_to_all | solution.py:30
  47.3 0.0 copy-done.7
  47.3 0.4 fusion.4
  47.8 0.6 copy-done.6
  48.4 2.6 %fusion = bf16[32,8,2048]{2,1,0:T(8,128)(2,1)S(1)} fusion(bf16[128,2048]{1,0:T(8,128)(2,1)} %get-tuple-element.15, bf16[128,2048]{1,0:T(8,128)(2,1)S(1)} %copy-done.6, bf16[2048,128]{1,0:T(8,128)(2,1)} %get-tuple-element.11, bf16[2048,128]{1,0:T(8,128)(2,1)} %get-tuple-element.9, bf16[32,8,2048]{2,1,0:T(8,128)(2,1)S(1)} %all-to-all-done, ...), kind=kOutput, calls=%fused_computation.2 | convolution fusion | flops 541982720 | bytes 4456448 | tf_op jit(solution)/shard_map/dot_general | solution.py:37
  51.0 33.2 %all_to_all.36 = bf16[32,8,2048]{2,1,0:T(8,128)(2,1)S(1)} all-to-all(bf16[32,8,2048]{2,1,0:T(8,128)(2,1)S(1)} %fusion), channel_id=1, replica_groups={{0,2,4,6,8,10,12,14,16,18,20,22,24,26,28,30,32,34,36,38,40,42,44,46,48,..., dimensions={0} | all-to-all | bytes 2097152 | tf_op jit(solution)/shard_map/all_to_all | solution.py:30
  84.2 0.2 convert_reduce_fusion.1
  84.4 0.6 copy-done.8
  85.0 12.3 %collective-permute-start.3 = (bf16[8,2048]{1,0:T(8,128)(2,1)S(1)}, bf16[8,2048]{1,0:T(8,128)(2,1)S(1)}, u32[]{:S(2)}, u32[]{:S(2)}) collective-permute-start(bf16[8,2048]{1,0:T(8,128)(2,1)S(1)} %fusion.51), channel_id=1, source_target_pairs={{704,0},{0,64},{64,128},{128,192},{192,256},{256,320},{320,384},{3... | collective-permute-start | bytes 98312 | tf_op jit(solution)/shard_map/ppermute | solution.py:21
  97.3 3.7 %collective-permute-done.3 = bf16[8,2048]{1,0:T(8,128)(2,1)S(1)} collective-permute-done((bf16[8,2048]{1,0:T(8,128)(2,1)S(1)}, bf16[8,2048]{1,0:T(8,128)(2,1)S(1)}, u32[]{:S(2)}, u32[]{:S(2)}) %collective-permute-start.3) | collective-permute-done | bytes 32800 | tf_op jit(solution)/shard_map/ppermute | solution.py:21
  101.0 0.1 fusion.54
  101.1 0.1 fusion.56
  101.2 0.1 broadcast_in_dim.10
  101.3 0.0 copy-start.5
  101.3 33.6 %all_to_all.37 = bf16[32,8,2048]{2,1,0:T(8,128)(2,1)S(1)} all-to-all(bf16[32,8,2048]{2,1,0:T(8,128)(2,1)S(1)} %broadcast_in_dim.10), channel_id=1, replica_groups={{0,2,4,6,8,10,12,14,16,18,20,22,24,26,28,30,32,34,36,38,40,42,44,46,48,..., dimensions={0} | all-to-all | bytes 2097152 | tf_op jit(solution)/shard_map/all_to_all | solution.py:30
  134.9 0.0 copy-done.5
  134.9 0.4 fusion.14
  135.4 0.6 copy-done.3
  136.0 0.2 copy-done.4
  136.1 2.5 %fusion.1 = bf16[32,8,2048]{2,1,0:T(8,128)(2,1)S(1)} fusion(bf16[128,2048]{1,0:T(8,128)(2,1)} %get-tuple-element.16, bf16[128,2048]{1,0:T(8,128)(2,1)S(1)} %copy-done.3, bf16[2048,128]{1,0:T(8,128)(2,1)} %get-tuple-element.12, bf16[2048,128]{1,0:T(8,128)(2,1)S(1)} %copy-done.4, bf16[32,8,2048]{2,1,0:T(8,128)(2,1)S(1)} %all_to_all.37, f32[256,256]{1,0:T(8,128)S(1)} %fusion.14), kind=kOutput, calls=%fused_computation.3 | convolution fusion | flops 541982720 | bytes 4456448 | tf_op jit(solution)/shard_map/dot_general | solution.py:37
  138.6 32.3 %all_to_all.38 = bf16[32,8,2048]{2,1,0:T(8,128)(2,1)S(1)} all-to-all(bf16[32,8,2048]{2,1,0:T(8,128)(2,1)S(1)} %fusion.1), channel_id=1, replica_groups={{0,2,4,6,8,10,12,14,16,18,20,22,24,26,28,30,32,34,36,38,40,42,44,46,48,..., dimensions={0} | all-to-all | bytes 2097152 | tf_op jit(solution)/shard_map/all_to_all | solution.py:30
  170.9 0.2 convert_reduce_fusion
  171.1 6.8 %collective-permute-start.4 = (bf16[8,2048]{1,0:T(8,128)(2,1)S(1)}, bf16[8,2048]{1,0:T(8,128)(2,1)S(1)}, u32[]{:S(2)}, u32[]{:S(2)}) collective-permute-start(bf16[8,2048]{1,0:T(8,128)(2,1)S(1)} %fusion.57), channel_id=1, source_target_pairs={{704,0},{0,64},{64,128},{128,192},{192,256},{256,320},{320,384},{3... | collective-permute-start | bytes 98312 | tf_op jit(solution)/shard_map/ppermute | solution.py:21
  177.9 5.4 %collective-permute-done.4 = bf16[8,2048]{1,0:T(8,128)(2,1)S(1)} collective-permute-done((bf16[8,2048]{1,0:T(8,128)(2,1)S(1)}, bf16[8,2048]{1,0:T(8,128)(2,1)S(1)}, u32[]{:S(2)}, u32[]{:S(2)}) %collective-permute-start.4) | collective-permute-done | bytes 32800 | tf_op jit(solution)/shard_map/ppermute | solution.py:21
  183.2 0.6 copy.8
  (10 shorter events, 0.0 us)
Async XLA Ops:
  8.8 12.7 %copy-start = (bf16[1,2,128,2048]{3,2,1,0:T(8,128)(2,1)S(1)}, bf16[1,2,128,2048]{3,2,1,0:T(8,128)(2,1)}, u32[]{:S(2)}) copy-start(bf16[1,2,128,2048]{3,2,1,0:T(8,128)(2,1)} %param.9) | copy-start | bytes 3145732
  8.8 14.6 %copy-start.1 = (bf16[1,2,2048,128]{3,2,1,0:T(8,128)(2,1)S(1)}, bf16[1,2,2048,128]{3,2,1,0:T(8,128)(2,1)}, u32[]{:S(2)}) copy-start(bf16[1,2,2048,128]{3,2,1,0:T(8,128)(2,1)} %param.8) | copy-start | bytes 3145732
  8.8 38.5 %all-to-all-start = ((bf16[32,8,2048]{2,1,0:T(8,128)(2,1)}), bf16[32,8,2048]{2,1,0:T(8,128)(2,1)S(1)}, u32[]{:S(2)}, u32[]{:S(2)}) async-start(bf16[32,8,2048]{2,1,0:T(8,128)(2,1)} %broadcast_in_dim.9), calls=%async_computation | async-start | bytes 2097152 | tf_op jit(solution)/shard_map/all_to_all | solution.py:30
  21.5 10.0 %collective-permute-start.2 = (bf16[2,128,2048]{2,1,0:T(8,128)(2,1)S(1)}, bf16[2,128,2048]{2,1,0:T(8,128)(2,1)S(1)}, u32[]{:S(2)}, u32[]{:S(2)}) collective-permute-start(bf16[2,128,2048]{2,1,0:T(8,128)(2,1)S(1)} %bitcast.62), channel_id=1, source_target_pairs={{0,1},{1,0},{2,3},{3,2},{4,5},{5,4},{6,7},{7,6},{8,9},{9,8},{10,11... | collective-permute-start | bytes 3145736 | tf_op jit(solution)/shard_map/ppermute | solution.py:15
  23.5 9.1 %collective-permute-start.1 = (bf16[2,2048,128]{2,1,0:T(8,128)(2,1)S(1)}, bf16[2,2048,128]{2,1,0:T(8,128)(2,1)S(1)}, u32[]{:S(2)}, u32[]{:S(2)}) collective-permute-start(bf16[2,2048,128]{2,1,0:T(8,128)(2,1)S(1)} %bitcast.63), channel_id=1, source_target_pairs={{0,1},{1,0},{2,3},{3,2},{4,5},{5,4},{6,7},{7,6},{8,9},{9,8},{10,11... | collective-permute-start | bytes 3145736 | tf_op jit(solution)/shard_map/ppermute | solution.py:15
  25.9 7.8 %collective-permute-start = (bf16[2,2048,128]{2,1,0:T(8,128)(2,1)}, bf16[2,2048,128]{2,1,0:T(8,128)(2,1)S(1)}, u32[]{:S(2)}, u32[]{:S(2)}) collective-permute-start(bf16[2,2048,128]{2,1,0:T(8,128)(2,1)} %bitcast.64), channel_id=1, source_target_pairs={{0,1},{1,0},{2,3},{3,2},{4,5},{5,4},{6,7},{7,6},{8,9},{9,8},{10,11... | collective-permute-start | bytes 3145736 | tf_op jit(solution)/shard_map/ppermute | solution.py:15
  28.9 1.6 copy-start.2
  33.7 13.7 %copy-start.7 = (bf16[2048,128]{1,0:T(8,128)(2,1)S(1)}, bf16[2048,128]{1,0:T(8,128)(2,1)}, u32[]{:S(2)}) copy-start(bf16[2048,128]{1,0:T(8,128)(2,1)} %get-tuple-element.6) | copy-start | bytes 1572868
  47.3 1.0 copy-start.6
  84.2 0.8 copy-start.8
  85.0 16.0 %collective-permute-start.3 = (bf16[8,2048]{1,0:T(8,128)(2,1)S(1)}, bf16[8,2048]{1,0:T(8,128)(2,1)S(1)}, u32[]{:S(2)}, u32[]{:S(2)}) collective-permute-start(bf16[8,2048]{1,0:T(8,128)(2,1)S(1)} %fusion.51), channel_id=1, source_target_pairs={{704,0},{0,64},{64,128},{128,192},{192,256},{256,320},{320,384},{3... | collective-permute-start | bytes 98312 | tf_op jit(solution)/shard_map/ppermute | solution.py:21
  101.3 33.6 %copy-start.5 = (bf16[2048,128]{1,0:T(8,128)(2,1)S(1)}, bf16[2048,128]{1,0:T(8,128)(2,1)}, u32[]{:S(2)}) copy-start(bf16[2048,128]{1,0:T(8,128)(2,1)} %get-tuple-element.5) | copy-start | bytes 1572868
  134.9 1.0 copy-start.3
  134.9 1.2 copy-start.4
  171.1 12.2 %collective-permute-start.4 = (bf16[8,2048]{1,0:T(8,128)(2,1)S(1)}, bf16[8,2048]{1,0:T(8,128)(2,1)S(1)}, u32[]{:S(2)}, u32[]{:S(2)}) collective-permute-start(bf16[8,2048]{1,0:T(8,128)(2,1)S(1)} %fusion.57), channel_id=1, source_target_pairs={{704,0},{0,64},{64,128},{128,192},{192,256},{256,320},{320,384},{3... | collective-permute-start | bytes 98312 | tf_op jit(solution)/shard_map/ppermute | solution.py:21

commit v2 on v1

v2 whole, which is shorter than its diff:
```python
import jax
import jax.numpy as jnp
from jax import lax
from jax.experimental import pallas as pl
from jax.experimental.pallas import tpu as pltpu
from jax.sharding import PartitionSpec as P


TICKS = 2
INTERPRET = False


epsilon = 0.5


def passed_along(block, axis, distance):
    devices = range(lax.axis_size(axis))
    route = [((i - distance) % len(devices), i) for i in devices]
    return lax.ppermute(block, axis, route)


def colour(place):
    return (place >> 1 ^ place >> 3) & 1


def same_kind(axis):
    size = lax.axis_size(axis)
    return [
        [place for place in range(size) if place & 1 == core and colour(place) == shade]
        for core in range(2)
        for shade in range(2)
    ]


def to_other_core(value, axis):
    return lax.ppermute(value, axis, [(place, place ^ 1) for place in range(lax.axis_size(axis))])


def to_other_colour(value, axis):
    size = lax.axis_size(axis)
    route = [(place, place ^ 2 if place & 1 else (place + 8) % size) for place in range(size)]
    return lax.ppermute(value, axis, route)


def exchange(blocks, axis, groups):
    return lax.all_to_all(blocks, axis, 0, 0, tiled=True, axis_index_groups=groups)


def room(mebibytes):
    return pltpu.CompilerParams(vmem_limit_bytes=mebibytes << 20)


def spread_kernel(tick, chosen_ref, rows_ref, gain_ref, copies_ref):
    widened = rows_ref[...].astype(jnp.float32)
    squares = jnp.mean(widened * widened, axis=-1, keepdims=True)
    gain_row = gain_ref[pl.ds(chosen_ref[tick], 1), :]
    normed = (widened * lax.rsqrt(squares + epsilon) * gain_row).astype(copies_ref.dtype)
    for member in range(copies_ref.shape[0]):
        copies_ref[member] = normed


def spread(tick, repeat_index, rows, gains, members):
    count, width = rows.shape
    return pl.pallas_call(
        lambda *refs: spread_kernel(tick, *refs),
        out_shape=jax.ShapeDtypeStruct((members, count, width), rows.dtype),
        in_specs=[
            pl.BlockSpec(memory_space=pltpu.SMEM),
            pl.BlockSpec(memory_space=pltpu.VMEM),
            pl.BlockSpec(memory_space=pltpu.VMEM),
        ],
        out_specs=pl.BlockSpec(memory_space=pltpu.VMEM),
        cost_estimate=pl.CostEstimate(flops=8 * count * width, bytes_accessed=2 * members * count * width, transcendentals=8),
        compiler_params=room(4),
        name="spread",
        interpret=INTERPRET,
    )(repeat_index, rows, gains)


def pack_kernel(chosen_ref, gate_ref, up_ref, down_ref, packed_ref):
    width, lanes = gate_ref.shape[1:]
    packed_ref[0:width] = gate_ref[0]
    packed_ref[width : 2 * width] = up_ref[0]
    for column in range(width // lanes):
        start = 2 * width + column * lanes
        packed_ref[start : start + lanes] = down_ref[0, :, column * lanes : (column + 1) * lanes]


def pack(tick, repeat_index, gate_weight, up_weight, down_weight):
    _, width, lanes = gate_weight.shape
    return pl.pallas_call(
        pack_kernel,
        out_shape=jax.ShapeDtypeStruct((3 * width, lanes), gate_weight.dtype),
        grid_spec=pltpu.PrefetchScalarGridSpec(
            num_scalar_prefetch=1,
            grid=(1,),
            in_specs=[
                pl.BlockSpec((1, width, lanes), lambda _, chosen: (chosen[tick], 0, 0)),
                pl.BlockSpec((1, width, lanes), lambda _, chosen: (chosen[tick], 0, 0)),
                pl.BlockSpec((1, lanes, width), lambda _, chosen: (chosen[tick], 0, 0)),
            ],
            out_specs=pl.BlockSpec((3 * width, lanes), lambda _, chosen: (0, 0)),
        ),
        cost_estimate=pl.CostEstimate(flops=3 * width * lanes, bytes_accessed=12 * width * lanes, transcendentals=0),
        compiler_params=room(8),
        name="pack",
        interpret=INTERPRET,
    )(repeat_index, gate_weight, up_weight, down_weight)


def feed_forward_kernel(tokens_ref, *refs):
    packs, out_ref = refs[:-1], refs[-1]
    members, count, width = tokens_ref.shape
    tokens = tokens_ref[...].reshape(members * count, width)
    lanes = packs[0].shape[1]
    hidden = []
    for packed in packs:
        both = jnp.concatenate([packed[0:width], packed[width : 2 * width]], axis=1)
        value = jnp.dot(tokens, both, preferred_element_type=jnp.float32)
        gate_value, up_value = value[:, :lanes], value[:, lanes:]
        hidden.append((gate_value / (1.0 + jnp.exp(-gate_value)) * up_value).astype(tokens.dtype))
    hidden = jnp.concatenate(hidden, axis=1)
    for column in range(0, width // lanes, 2):
        slabs = []
        for step in range(2):
            start = 2 * width + (column + step) * lanes
            slabs.append(jnp.concatenate([packed[start : start + lanes] for packed in packs], axis=0))
        value = jnp.dot(hidden, jnp.concatenate(slabs, axis=1), preferred_element_type=jnp.float32)
        out_ref[:, :, column * lanes : (column + 2) * lanes] = value.astype(out_ref.dtype).reshape(
            members, count, 2 * lanes
        )


def feed_forward(tokens, packs):
    members, count, width = tokens.shape
    lanes = packs[0].shape[1]
    flops = 6 * members * count * width * lanes * len(packs)
    return pl.pallas_call(
        feed_forward_kernel,
        out_shape=jax.ShapeDtypeStruct(tokens.shape, tokens.dtype),
        in_specs=[pl.BlockSpec(memory_space=pltpu.VMEM)] * (1 + len(packs)),
        out_specs=pl.BlockSpec(memory_space=pltpu.VMEM),
        cost_estimate=pl.CostEstimate(flops=flops, bytes_accessed=6 * width * lanes * len(packs), transcendentals=0),
        compiler_params=room(12),
        name="ffn",
        interpret=INTERPRET,
    )(tokens, *packs)


def advance_kernel(parts_ref, rows_ref, out_ref):
    total = rows_ref[...].astype(jnp.float32)
    output = parts_ref[0].astype(jnp.float32)
    for member in range(1, parts_ref.shape[0]):
        output = output + parts_ref[member].astype(jnp.float32)
    out_ref[...] = (total + output).astype(out_ref.dtype)


def advance(parts, rows):
    return pl.pallas_call(
        advance_kernel,
        out_shape=jax.ShapeDtypeStruct(rows.shape, rows.dtype),
        in_specs=[pl.BlockSpec(memory_space=pltpu.VMEM)] * 2,
        out_specs=pl.BlockSpec(memory_space=pltpu.VMEM),
        cost_estimate=pl.CostEstimate(flops=parts.size, bytes_accessed=2 * parts.size, transcendentals=0),
        compiler_params=room(4),
        name="advance",
        interpret=INTERPRET,
    )(parts, rows)


def on_device(buffer, gate_weight, up_weight, down_weight, norm_gain, repeat_index):
    current = buffer[0]
    chosen = repeat_index.reshape(TICKS)
    groups = same_kind("dp")
    members = len(groups[0])
    for tick in range(TICKS):
        own = pack(tick, chosen, gate_weight[0], up_weight[0], down_weight[0])
        near = to_other_colour(own, "dp")
        own_pair = to_other_core(own, "dp")
        near_pair = to_other_core(near, "dp")
        copies = spread(tick, chosen, current, norm_gain[0], members)
        tokens = exchange(copies, "dp", groups)
        partial_value = feed_forward(tokens, (own, own_pair, near, near_pair))
        parts = exchange(partial_value, "dp", groups)
        advanced = advance(parts, current)
        current = passed_along(advanced, "section", 1)
    return current[None]


def solution(mesh):
    placed = (
        P("section", "dp", None),
        P("section", None, None, "dp"),
        P("section", None, None, "dp"),
        P("section", None, "dp", None),
        P("section", None, None),
        P(None, "section"),
    )
    return jax.shard_map(
        on_device, mesh=mesh, in_specs=placed, out_specs=P("section", "dp", None), check_vma=False
    )
```

time: 188 us -> 169 us (0.90)
  the two profiles are of different devices: /device:TPU:56 before, /device:TPU:16 now
where the time goes in v2:
time: 169 us
  waiting for transfers between devices  69.6 us (41%)
  starting transfers between devices  56.9 us (34%)
  blocking collectives  20.8 us (12%)
  Pallas kernels  11.6 us (7%)
  local copies, waits for them, and re-layouts  9.43 us (6%)
    all_to_all x3, starting transfers between devices, exchange(): lax.all_to_all(blocks, axis, 0, 0, tiled=True, axis_index_groups=groups)  29.3 us
    all_to_all x3, waiting for transfers between devices, exchange(): lax.all_to_all(blocks, axis, 0, 0, tiled=True, axis_index_groups=groups)  27.8 us
    ppermute x2, waiting for transfers between devices, to_other_colour(): return lax.ppermute(value, axis, route)  27.8 us
    all_to_all x1, blocking collectives, exchange(): lax.all_to_all(blocks, axis, 0, 0, tiled=True, axis_index_groups=groups)  20.8 us
    ppermute x2, waiting for transfers between devices, passed_along(): return lax.ppermute(block, axis, route)  14 us
    ppermute x2, starting transfers between devices, passed_along(): return lax.ppermute(block, axis, route)  13.2 us
    unnamed x23, local copies, waits for them, and re-layouts  9.43 us
    ppermute x4, starting transfers between devices, to_other_core(): lax.ppermute(value, axis, [(place, place ^ 1) for place in range(lax.axis...  7.99 us
  transfers between devices with their start and end apart: 11, of which 7 were waited for; matrix products, arithmetic and copies ran while one was open for 0% of the time, Pallas kernels for 4%

profile of v2, /device:TPU:16, one launch (start us, length us, event | category | flops | bytes accessed | tf_op | source)
XLA Modules:
  0.0 168.6 jit_solution(11636750862252285691)
XLA Ops:
  0.0 0.0 copy-start
  0.0 1.2 copy-done
  1.2 0.0 copy-start.2
  1.2 1.2 copy-done.2
  2.5 1.2 copy-done.4
  3.7 0.7 copy-done.9
  4.3 0.7 pack.2.refs_0_
  5.0 0.0 copy-start.10
  5.1 3.5 %collective-permute-start.1 = (bf16[6144,128]{1,0:T(8,128)(2,1)S(1)}, bf16[6144,128]{1,0:T(8,128)(2,1)}, u32[]{:S(2)}, u32[]{:S(2)}) collective-permute-start(bf16[6144,128]{1,0:T(8,128)(2,1)S(1)} %pack.2.refs_0_), channel_id=1, source_target_pairs={{0,8},{1,3},{2,10},{3,1},{4,12},{5,7},{6,14},{7,5},{8,16},{9,11},{... | collective-permute-start | bytes 4718600 | tf_op jit(solution)/shard_map/ppermute | solution.py:42
  8.6 2.3 %collective-permute-start = (bf16[6144,128]{1,0:T(8,128)(2,1)S(1)}, bf16[6144,128]{1,0:T(8,128)(2,1)}, u32[]{:S(2)}, u32[]{:S(2)}) collective-permute-start(bf16[6144,128]{1,0:T(8,128)(2,1)S(1)} %pack.2.refs_0_), channel_id=1, source_target_pairs={{0,1},{1,0},{2,3},{3,2},{4,5},{5,4},{6,7},{7,6},{8,9},{9,8},{10,11... | collective-permute-start | bytes 4718600 | tf_op jit(solution)/shard_map/ppermute | solution.py:36
  10.8 16.7 %collective-permute-done.1.refs_2_ = bf16[6144,128]{1,0:T(8,128)(2,1)} collective-permute-done((bf16[6144,128]{1,0:T(8,128)(2,1)S(1)}, bf16[6144,128]{1,0:T(8,128)(2,1)}, u32[]{:S(2)}, u32[]{:S(2)}) %collective-permute-start.1) | collective-permute-done | bytes 1572896 | tf_op jit(solution)/shard_map/ppermute | solution.py:42
  27.5 1.9 %collective-permute-start.2 = (bf16[6144,128]{1,0:T(8,128)(2,1)}, bf16[6144,128]{1,0:T(8,128)(2,1)}, u32[]{:S(2)}, u32[]{:S(2)}) collective-permute-start(bf16[6144,128]{1,0:T(8,128)(2,1)} %collective-permute-done.1.refs_2_), channel_id=1, source_target_pairs={{0,1},{1,0},{2,3},{3,2},{4,5},{5,4},{6,7},{7,6},{8,9},{9,8},{10,11... | collective-permute-start | bytes 4718600 | tf_op jit(solution)/shard_map/ppermute | solution.py:36
  29.4 0.0 copy-done.7
  29.4 0.0 copy-done.8
  29.4 1.5 spread.2
  30.9 14.5 %all-to-all-start = ((bf16[16,8,2048]{2,1,0:T(8,128)(2,1)}), bf16[16,8,2048]{2,1,0:T(8,128)(2,1)}, u32[]{:S(2)}, u32[]{:S(2)}) async-start(bf16[16,8,2048]{2,1,0:T(8,128)(2,1)} %spread.2), calls=%async_computation | async-start | bytes 1048576 | tf_op jit(solution)/shard_map/all_to_all | solution.py:46
  45.4 0.0 copy-done.10
  45.4 0.0 copy-start.1
  45.4 1.2 copy-done.1
  46.6 1.2 copy-done.3
  47.9 1.2 copy-done.5
  49.1 0.7 pack.3.refs_0_
  49.8 2.9 %collective-permute-start.5 = (bf16[6144,128]{1,0:T(8,128)(2,1)S(1)}, bf16[6144,128]{1,0:T(8,128)(2,1)}, u32[]{:S(2)}, u32[]{:S(2)}) collective-permute-start(bf16[6144,128]{1,0:T(8,128)(2,1)S(1)} %pack.3.refs_0_), channel_id=1, source_target_pairs={{0,8},{1,3},{2,10},{3,1},{4,12},{5,7},{6,14},{7,5},{8,16},{9,11},{... | collective-permute-start | bytes 4718600 | tf_op jit(solution)/shard_map/ppermute | solution.py:42
  52.7 10.0 %all-to-all-done.tokens_ref = bf16[16,8,2048]{2,1,0:T(8,128)(2,1)} async-done(((bf16[16,8,2048]{2,1,0:T(8,128)(2,1)}), bf16[16,8,2048]{2,1,0:T(8,128)(2,1)}, u32[]{:S(2)}, u32[]{:S(2)}) %all-to-all-start) | async-done | bytes 524320 | tf_op jit(solution)/shard_map/all_to_all | solution.py:46
  62.7 0.0 collective-permute-done.refs_1_
  62.7 0.0 collective-permute-done.2.refs_3_
  62.7 3.6 %ffn.2 = bf16[16,8,2048]{2,1,0:T(8,128)(2,1)S(1)} custom-call(bf16[16,8,2048]{2,1,0:T(8,128)(2,1)} %all-to-all-done.tokens_ref, bf16[6144,128]{1,0:T(8,128)(2,1)S(1)} %pack.2.refs_0_, bf16[6144,128]{1,0:T(8,128)(2,1)} %collective-permute-done.refs_1_, bf16[6144,128]{1,0:T(8,128)(2,1)} %collective-permute-done.1.refs_2_, ...), custom_call_target="tpu_custom_call" | custom-call | flops 805306368 | bytes 6291456 | tf_op jit(solution)/shard_map/ffn/pallas_call | solution.py:138
  66.3 0.0 copy-start.6
  66.3 0.8 copy-done.6
  67.1 5.5 %all-to-all-start.1 = ((bf16[16,8,2048]{2,1,0:T(8,128)(2,1)}), bf16[16,8,2048]{2,1,0:T(8,128)(2,1)S(1)}, u32[]{:S(2)}, u32[]{:S(2)}) async-start(bf16[16,8,2048]{2,1,0:T(8,128)(2,1)} %copy-done.6), calls=%async_computation.1 | async-start | bytes 1048576 | tf_op jit(solution)/shard_map/all_to_all | solution.py:46
  72.6 1.9 %collective-permute-start.4 = (bf16[6144,128]{1,0:T(8,128)(2,1)S(1)}, bf16[6144,128]{1,0:T(8,128)(2,1)}, u32[]{:S(2)}, u32[]{:S(2)}) collective-permute-start(bf16[6144,128]{1,0:T(8,128)(2,1)S(1)} %pack.3.refs_0_), channel_id=1, source_target_pairs={{0,1},{1,0},{2,3},{3,2},{4,5},{5,4},{6,7},{7,6},{8,9},{9,8},{10,11... | collective-permute-start | bytes 4718600 | tf_op jit(solution)/shard_map/ppermute | solution.py:36
  74.5 11.1 %collective-permute-done.5.refs_2_ = bf16[6144,128]{1,0:T(8,128)(2,1)} collective-permute-done((bf16[6144,128]{1,0:T(8,128)(2,1)S(1)}, bf16[6144,128]{1,0:T(8,128)(2,1)}, u32[]{:S(2)}, u32[]{:S(2)}) %collective-permute-start.5) | collective-permute-done | bytes 1572896 | tf_op jit(solution)/shard_map/ppermute | solution.py:42
  85.7 1.9 %collective-permute-start.6 = (bf16[6144,128]{1,0:T(8,128)(2,1)}, bf16[6144,128]{1,0:T(8,128)(2,1)}, u32[]{:S(2)}, u32[]{:S(2)}) collective-permute-start(bf16[6144,128]{1,0:T(8,128)(2,1)} %collective-permute-done.5.refs_2_), channel_id=1, source_target_pairs={{0,1},{1,0},{2,3},{3,2},{4,5},{5,4},{6,7},{7,6},{8,9},{9,8},{10,11... | collective-permute-start | bytes 4718600 | tf_op jit(solution)/shard_map/ppermute | solution.py:36
  87.6 1.4 all-to-all-done.1.parts_ref
  89.0 0.1 advance.2
  89.0 10.1 %collective-permute-start.3 = (bf16[8,2048]{1,0:T(8,128)(2,1)S(1)}, bf16[8,2048]{1,0:T(8,128)(2,1)S(1)}, u32[]{:S(2)}, u32[]{:S(2)}) collective-permute-start(bf16[8,2048]{1,0:T(8,128)(2,1)S(1)} %advance.2), channel_id=1, source_target_pairs={{704,0},{0,64},{64,128},{128,192},{192,256},{256,320},{320,384},{3... | collective-permute-start | bytes 98312 | tf_op jit(solution)/shard_map/ppermute | solution.py:19
  99.2 5.3 %collective-permute-done.3.refs_1_.rows_ref = bf16[8,2048]{1,0:T(8,128)(2,1)S(1)} collective-permute-done((bf16[8,2048]{1,0:T(8,128)(2,1)S(1)}, bf16[8,2048]{1,0:T(8,128)(2,1)S(1)}, u32[]{:S(2)}, u32[]{:S(2)}) %collective-permute-start.3) | collective-permute-done | bytes 32800 | tf_op jit(solution)/shard_map/ppermute | solution.py:19
  104.4 1.5 spread.3
  105.9 9.3 %all-to-all-start.2 = ((bf16[16,8,2048]{2,1,0:T(8,128)(2,1)}), bf16[16,8,2048]{2,1,0:T(8,128)(2,1)S(1)}, u32[]{:S(2)}, u32[]{:S(2)}) async-start(bf16[16,8,2048]{2,1,0:T(8,128)(2,1)} %spread.3), calls=%async_computation.2 | async-start | bytes 1048576 | tf_op jit(solution)/shard_map/all_to_all | solution.py:46
  115.3 0.0 collective-permute-done.4.refs_1_
  115.3 0.0 collective-permute-done.6.refs_3_
  115.3 16.5 %all-to-all-done.2.tokens_ref = bf16[16,8,2048]{2,1,0:T(8,128)(2,1)S(1)} async-done(((bf16[16,8,2048]{2,1,0:T(8,128)(2,1)}), bf16[16,8,2048]{2,1,0:T(8,128)(2,1)S(1)}, u32[]{:S(2)}, u32[]{:S(2)}) %all-to-all-start.2) | async-done | bytes 524320 | tf_op jit(solution)/shard_map/all_to_all | solution.py:46
  131.8 3.4 %ffn.3 = bf16[16,8,2048]{2,1,0:T(8,128)(2,1)S(1)} custom-call(bf16[16,8,2048]{2,1,0:T(8,128)(2,1)S(1)} %all-to-all-done.2.tokens_ref, bf16[6144,128]{1,0:T(8,128)(2,1)S(1)} %pack.3.refs_0_, bf16[6144,128]{1,0:T(8,128)(2,1)} %collective-permute-done.4.refs_1_, bf16[6144,128]{1,0:T(8,128)(2,1)} %collective-permute-done.5.refs_2_, ...), custom_call_target="tpu_custom_call" | custom-call | flops 805306368 | bytes 6291456 | tf_op jit(solution)/shard_map/ffn/pallas_call | solution.py:138
  135.2 20.8 %all_to_all.20.parts_ref = bf16[16,8,2048]{2,1,0:T(8,128)(2,1)S(1)} all-to-all(bf16[16,8,2048]{2,1,0:T(8,128)(2,1)S(1)} %ffn.3), channel_id=1, replica_groups={{0,4,10,14,16,20,26,30,32,36,42,46,48,52,58,62},{2,6,8,12,18,22,24,28,3..., dimensions={0} | all-to-all | bytes 1048576 | tf_op jit(solution)/shard_map/all_to_all | solution.py:46
  156.1 0.1 advance.3
  156.1 3.1 %collective-permute-start.7 = (bf16[8,2048]{1,0:T(8,128)(2,1)S(1)}, bf16[8,2048]{1,0:T(8,128)(2,1)S(1)}, u32[]{:S(2)}, u32[]{:S(2)}) collective-permute-start(bf16[8,2048]{1,0:T(8,128)(2,1)S(1)} %advance.3), channel_id=1, source_target_pairs={{704,0},{0,64},{64,128},{128,192},{192,256},{256,320},{320,384},{3... | collective-permute-start | bytes 98312 | tf_op jit(solution)/shard_map/ppermute | solution.py:19
  159.2 8.7 %collective-permute-done.7 = bf16[8,2048]{1,0:T(8,128)(2,1)S(1)} collective-permute-done((bf16[8,2048]{1,0:T(8,128)(2,1)S(1)}, bf16[8,2048]{1,0:T(8,128)(2,1)S(1)}, u32[]{:S(2)}, u32[]{:S(2)}) %collective-permute-start.7) | collective-permute-done | bytes 32800 | tf_op jit(solution)/shard_map/ppermute | solution.py:19
  168.0 0.6 copy.8
  (6 shorter events, 0.0 us)
Async XLA Ops:
  0.0 1.2 copy-start
  1.2 1.2 copy-start.2
  2.5 1.2 copy-start.4
  3.7 0.7 copy-start.9
  4.3 25.1 %copy-start.7 = (bf16[1,8,2048]{2,1,0:T(8,128)(2,1)S(1)}, bf16[1,8,2048]{2,1,0:T(8,128)(2,1)}, u32[]{:S(2)}) copy-start(bf16[1,8,2048]{2,1,0:T(8,128)(2,1)} %param.6) | copy-start | bytes 98308
  4.3 25.1 %copy-start.8 = (f32[1,2,2048]{2,1,0:T(2,128)S(1)}, f32[1,2,2048]{2,1,0:T(2,128)}, u32[]{:S(2)}) copy-start(f32[1,2,2048]{2,1,0:T(2,128)} %param.10) | copy-start | bytes 49156
  5.0 40.4 %copy-start.10 = (s32[2,1]{0,1:T(1,128)S(1)}, s32[2,1]{0,1:T(1,128)}, u32[]{:S(2)}) copy-start(s32[2,1]{0,1:T(1,128)} %param.11) | copy-start | bytes 28
  5.1 22.4 %collective-permute-start.1 = (bf16[6144,128]{1,0:T(8,128)(2,1)S(1)}, bf16[6144,128]{1,0:T(8,128)(2,1)}, u32[]{:S(2)}, u32[]{:S(2)}) collective-permute-start(bf16[6144,128]{1,0:T(8,128)(2,1)S(1)} %pack.2.refs_0_), channel_id=1, source_target_pairs={{0,8},{1,3},{2,10},{3,1},{4,12},{5,7},{6,14},{7,5},{8,16},{9,11},{... | collective-permute-start | bytes 4718600 | tf_op jit(solution)/shard_map/ppermute | solution.py:42
  8.6 54.2 %collective-permute-start = (bf16[6144,128]{1,0:T(8,128)(2,1)S(1)}, bf16[6144,128]{1,0:T(8,128)(2,1)}, u32[]{:S(2)}, u32[]{:S(2)}) collective-permute-start(bf16[6144,128]{1,0:T(8,128)(2,1)S(1)} %pack.2.refs_0_), channel_id=1, source_target_pairs={{0,1},{1,0},{2,3},{3,2},{4,5},{5,4},{6,7},{7,6},{8,9},{9,8},{10,11... | collective-permute-start | bytes 4718600 | tf_op jit(solution)/shard_map/ppermute | solution.py:36
  27.5 35.2 %collective-permute-start.2 = (bf16[6144,128]{1,0:T(8,128)(2,1)}, bf16[6144,128]{1,0:T(8,128)(2,1)}, u32[]{:S(2)}, u32[]{:S(2)}) collective-permute-start(bf16[6144,128]{1,0:T(8,128)(2,1)} %collective-permute-done.1.refs_2_), channel_id=1, source_target_pairs={{0,1},{1,0},{2,3},{3,2},{4,5},{5,4},{6,7},{7,6},{8,9},{9,8},{10,11... | collective-permute-start | bytes 4718600 | tf_op jit(solution)/shard_map/ppermute | solution.py:36
  30.9 31.8 %all-to-all-start = ((bf16[16,8,2048]{2,1,0:T(8,128)(2,1)}), bf16[16,8,2048]{2,1,0:T(8,128)(2,1)}, u32[]{:S(2)}, u32[]{:S(2)}) async-start(bf16[16,8,2048]{2,1,0:T(8,128)(2,1)} %spread.2), calls=%async_computation | async-start | bytes 1048576 | tf_op jit(solution)/shard_map/all_to_all | solution.py:46
  45.4 1.2 copy-start.1
  46.6 1.2 copy-start.3
  47.9 1.2 copy-start.5
  49.8 35.9 %collective-permute-start.5 = (bf16[6144,128]{1,0:T(8,128)(2,1)S(1)}, bf16[6144,128]{1,0:T(8,128)(2,1)}, u32[]{:S(2)}, u32[]{:S(2)}) collective-permute-start(bf16[6144,128]{1,0:T(8,128)(2,1)S(1)} %pack.3.refs_0_), channel_id=1, source_target_pairs={{0,8},{1,3},{2,10},{3,1},{4,12},{5,7},{6,14},{7,5},{8,16},{9,11},{... | collective-permute-start | bytes 4718600 | tf_op jit(solution)/shard_map/ppermute | solution.py:42
  66.3 0.8 copy-start.6
  67.1 21.8 %all-to-all-start.1 = ((bf16[16,8,2048]{2,1,0:T(8,128)(2,1)}), bf16[16,8,2048]{2,1,0:T(8,128)(2,1)S(1)}, u32[]{:S(2)}, u32[]{:S(2)}) async-start(bf16[16,8,2048]{2,1,0:T(8,128)(2,1)} %copy-done.6), calls=%async_computation.1 | async-start | bytes 1048576 | tf_op jit(solution)/shard_map/all_to_all | solution.py:46
  72.6 42.6 %collective-permute-start.4 = (bf16[6144,128]{1,0:T(8,128)(2,1)S(1)}, bf16[6144,128]{1,0:T(8,128)(2,1)}, u32[]{:S(2)}, u32[]{:S(2)}) collective-permute-start(bf16[6144,128]{1,0:T(8,128)(2,1)S(1)} %pack.3.refs_0_), channel_id=1, source_target_pairs={{0,1},{1,0},{2,3},{3,2},{4,5},{5,4},{6,7},{7,6},{8,9},{9,8},{10,11... | collective-permute-start | bytes 4718600 | tf_op jit(solution)/shard_map/ppermute | solution.py:36
  85.7 29.6 %collective-permute-start.6 = (bf16[6144,128]{1,0:T(8,128)(2,1)}, bf16[6144,128]{1,0:T(8,128)(2,1)}, u32[]{:S(2)}, u32[]{:S(2)}) collective-permute-start(bf16[6144,128]{1,0:T(8,128)(2,1)} %collective-permute-done.5.refs_2_), channel_id=1, source_target_pairs={{0,1},{1,0},{2,3},{3,2},{4,5},{5,4},{6,7},{7,6},{8,9},{9,8},{10,11... | collective-permute-start | bytes 4718600 | tf_op jit(solution)/shard_map/ppermute | solution.py:36
  89.0 15.4 %collective-permute-start.3 = (bf16[8,2048]{1,0:T(8,128)(2,1)S(1)}, bf16[8,2048]{1,0:T(8,128)(2,1)S(1)}, u32[]{:S(2)}, u32[]{:S(2)}) collective-permute-start(bf16[8,2048]{1,0:T(8,128)(2,1)S(1)} %advance.2), channel_id=1, source_target_pairs={{704,0},{0,64},{64,128},{128,192},{192,256},{256,320},{320,384},{3... | collective-permute-start | bytes 98312 | tf_op jit(solution)/shard_map/ppermute | solution.py:19
  105.9 25.8 %all-to-all-start.2 = ((bf16[16,8,2048]{2,1,0:T(8,128)(2,1)}), bf16[16,8,2048]{2,1,0:T(8,128)(2,1)S(1)}, u32[]{:S(2)}, u32[]{:S(2)}) async-start(bf16[16,8,2048]{2,1,0:T(8,128)(2,1)} %spread.3), calls=%async_computation.2 | async-start | bytes 1048576 | tf_op jit(solution)/shard_map/all_to_all | solution.py:46
  156.1 11.8 %collective-permute-start.7 = (bf16[8,2048]{1,0:T(8,128)(2,1)S(1)}, bf16[8,2048]{1,0:T(8,128)(2,1)S(1)}, u32[]{:S(2)}, u32[]{:S(2)}) collective-permute-start(bf16[8,2048]{1,0:T(8,128)(2,1)S(1)} %advance.3), channel_id=1, source_target_pairs={{704,0},{0,64},{64,128},{128,192},{192,256},{256,320},{320,384},{3... | collective-permute-start | bytes 98312 | tf_op jit(solution)/shard_map/ppermute | solution.py:19

commit v3 on v2

--- a/solution.py
+++ b/solution.py
@@ -77,44 +77,109 @@
     )(repeat_index, rows, gains)
 
 
-def pack_kernel(chosen_ref, gate_ref, up_ref, down_ref, packed_ref):
+def slab_copies(chosen, gate_ref, up_ref, down_ref, packed_ref, arrived):
     width, lanes = gate_ref.shape[1:]
-    packed_ref[0:width] = gate_ref[0]
-    packed_ref[width : 2 * width] = up_ref[0]
+    moves = [
+        (gate_ref.at[chosen], packed_ref.at[0:width]),
+        (up_ref.at[chosen], packed_ref.at[width : 2 * width]),
+    ]
     for column in range(width // lanes):
         start = 2 * width + column * lanes
-        packed_ref[start : start + lanes] = down_ref[0, :, column * lanes : (column + 1) * lanes]
-
-
-def pack(tick, repeat_index, gate_weight, up_weight, down_weight):
+        moves.append(
+            (
+                down_ref.at[chosen, :, column * lanes : (column + 1) * lanes],
+                packed_ref.at[start : start + lanes],
+            )
+        )
+    return [pltpu.make_async_copy(*move, arrived.at[index]) for index, move in enumerate(moves)]
+
+
+def pack_kernel(tick, chosen_ref, gate_ref, up_ref, down_ref, packed_ref, arrived):
+    copies = slab_copies(chosen_ref[tick], gate_ref, up_ref, down_ref, packed_ref, arrived)
+    for copy in copies:
+        copy.start()
+    for copy in copies:
+        copy.wait()
+
+
+IN_HBM = pl.BlockSpec(memory_space=pltpu.HBM)
+IN_VMEM = pl.BlockSpec(memory_space=pltpu.VMEM)
+IN_SMEM = pl.BlockSpec(memory_space=pltpu.SMEM)
+
+
+def pack(tick, chosen, gate_weight, up_weight, down_weight):
     _, width, lanes = gate_weight.shape
     return pl.pallas_call(
-        pack_kernel,
+        lambda *refs: pack_kernel(tick, *refs),
         out_shape=jax.ShapeDtypeStruct((3 * width, lanes), gate_weight.dtype),
-        grid_spec=pltpu.PrefetchScalarGridSpec(
-            num_scalar_prefetch=1,
-            grid=(1,),
-            in_specs=[
-                pl.BlockSpec((1, width, lanes), lambda _, chosen: (chosen[tick], 0, 0)),
-                pl.BlockSpec((1, width, lanes), lambda _, chosen: (chosen[tick], 0, 0)),
-                pl.BlockSpec((1, lanes, width), lambda _, chosen: (chosen[tick], 0, 0)),
-            ],
-            out_specs=pl.BlockSpec((3 * width, lanes), lambda _, chosen: (0, 0)),
+        in_specs=[IN_SMEM, IN_HBM, IN_HBM, IN_HBM],
+        out_specs=IN_VMEM,
+        scratch_shapes=[pltpu.SemaphoreType.DMA((2 + width // lanes,))],
+        cost_estimate=pl.CostEstimate(flops=3 * width * lanes, bytes_accessed=12 * width * lanes, transcendentals=0),
+        compiler_params=room(60),
+        name="pack",
+        interpret=INTERPRET,
+    )(chosen, gate_weight, up_weight, down_weight)
+
+
+def begin_kernel(
+    chosen_ref, rows_hbm, gain_hbm, gate_ref, up_ref, down_ref, packed_ref, copies_ref, rows_ref, gain_ref, arrived, loaded
+):
+    loads = [
+        pltpu.make_async_copy(rows_hbm, rows_ref, loaded.at[0]),
+        pltpu.make_async_copy(gain_hbm, gain_ref, loaded.at[1]),
+    ]
+    for load in loads:
+        load.start()
+    copies = slab_copies(chosen_ref[0], gate_ref, up_ref, down_ref, packed_ref, arrived)
+    for copy in copies:
+        copy.start()
+    for load in loads:
+        load.wait()
+    spread_kernel(0, chosen_ref, rows_ref, gain_ref, copies_ref)
+    for copy in copies:
+        copy.wait()
+
+
+def begin(chosen, rows, gains, gate_weight, up_weight, down_weight, members):
+    _, width, lanes = gate_weight.shape
+    count = rows.shape[0]
+    return pl.pallas_call(
+        begin_kernel,
+        out_shape=(
+            jax.ShapeDtypeStruct((3 * width, lanes), gate_weight.dtype),
+            jax.ShapeDtypeStruct((members, count, width), rows.dtype),
         ),
-        cost_estimate=pl.CostEstimate(flops=3 * width * lanes, bytes_accessed=12 * width * lanes, transcendentals=0),
-        compiler_params=room(8),
-        name="pack",
-        interpret=INTERPRET,
-    )(repeat_index, gate_weight, up_weight, down_weight)
+        in_specs=[IN_SMEM] + [IN_HBM] * 5,
+        out_specs=(IN_VMEM, IN_VMEM),
+        scratch_shapes=[
+            pltpu.VMEM(rows.shape, rows.dtype),
+            pltpu.VMEM(gains.shape, gains.dtype),
+            pltpu.SemaphoreType.DMA((2 + width // lanes,)),
+            pltpu.SemaphoreType.DMA((2,)),
+        ],
+        cost_estimate=pl.CostEstimate(flops=3 * width * lanes, bytes_accessed=12 * width * lanes, transcendentals=8),
+        compiler_params=room(60),
+        name="begin",
+        interpret=INTERPRET,
+    )(chosen, rows, gains, gate_weight, up_weight, down_weight)
 
 
 def feed_forward_kernel(tokens_ref, *refs):
-    packs, out_ref = refs[:-1], refs[-1]
-    members, count, width = tokens_ref.shape
-    tokens = tokens_ref[...].reshape(members * count, width)
+    count = (len(refs) - 2) // 2
+    sources, out_ref, packs, arrived = refs[:count], refs[count], refs[count + 1 : -1], refs[-1]
+    copies = [
+        pltpu.make_async_copy(source, slot, arrived.at[index])
+        for index, (source, slot) in enumerate(zip(sources, packs))
+    ]
+    for copy in copies:
+        copy.start()
+    members, rows, width = tokens_ref.shape
+    tokens = tokens_ref[...].reshape(members * rows, width)
     lanes = packs[0].shape[1]
     hidden = []
-    for packed in packs:
+    for copy, packed in zip(copies, packs):
+        copy.wait()
         both = jnp.concatenate([packed[0:width], packed[width : 2 * width]], axis=1)
         value = jnp.dot(tokens, both, preferred_element_type=jnp.float32)
         gate_value, up_value = value[:, :lanes], value[:, lanes:]
@@ -127,21 +192,27 @@
             slabs.append(jnp.concatenate([packed[start : start + lanes] for packed in packs], axis=0))
         value = jnp.dot(hidden, jnp.concatenate(slabs, axis=1), preferred_element_type=jnp.float32)
         out_ref[:, :, column * lanes : (column + 2) * lanes] = value.astype(out_ref.dtype).reshape(
-            members, count, 2 * lanes
+            members, rows, 2 * lanes
         )
 
 
 def feed_forward(tokens, packs):
-    members, count, width = tokens.shape
+    members, rows, width = tokens.shape
     lanes = packs[0].shape[1]
-    flops = 6 * members * count * width * lanes * len(packs)
+    shards = len(packs)
     return pl.pallas_call(
         feed_forward_kernel,
         out_shape=jax.ShapeDtypeStruct(tokens.shape, tokens.dtype),
-        in_specs=[pl.BlockSpec(memory_space=pltpu.VMEM)] * (1 + len(packs)),
-        out_specs=pl.BlockSpec(memory_space=pltpu.VMEM),
-        cost_estimate=pl.CostEstimate(flops=flops, bytes_accessed=6 * width * lanes * len(packs), transcendentals=0),
-        compiler_params=room(12),
+        in_specs=[IN_VMEM] + [IN_HBM] * shards,
+        out_specs=IN_VMEM,
+        scratch_shapes=[pltpu.VMEM(pack.shape, pack.dtype) for pack in packs]
+        + [pltpu.SemaphoreType.DMA((shards,))],
+        cost_estimate=pl.CostEstimate(
+            flops=6 * members * rows * width * lanes * shards,
+            bytes_accessed=6 * width * lanes * shards,
+            transcendentals=members * rows * lanes * shards,
+        ),
+        compiler_params=room(62),
         name="ffn",
         interpret=INTERPRET,
     )(tokens, *packs)
@@ -171,15 +242,19 @@
 def on_device(buffer, gate_weight, up_weight, down_weight, norm_gain, repeat_index):
     current = buffer[0]
     chosen = repeat_index.reshape(TICKS)
+    weights = (gate_weight[0], up_weight[0], down_weight[0])
     groups = same_kind("dp")
     members = len(groups[0])
     for tick in range(TICKS):
-        own = pack(tick, chosen, gate_weight[0], up_weight[0], down_weight[0])
+        if tick == 0:
+            own, copies = begin(chosen, current, norm_gain[0], *weights, members)
+        else:
+            own = pack(tick, chosen, *weights)
+            copies = spread(tick, chosen, current, norm_gain[0], members)
         near = to_other_colour(own, "dp")
+        tokens = exchange(copies, "dp", groups)
         own_pair = to_other_core(own, "dp")
         near_pair = to_other_core(near, "dp")
-        copies = spread(tick, chosen, current, norm_gain[0], members)
-        tokens = exchange(copies, "dp", groups)
         partial_value = feed_forward(tokens, (own, own_pair, near, near_pair))
         parts = exchange(partial_value, "dp", groups)
         advanced = advance(parts, current)

time: 169 us -> 169 us (level)
  local copies, waits for them, and re-layouts: 9.43 us -> 0.64 us
  Pallas kernels: 11.6 us -> 19.5 us
    unnamed x23 -> x9, local copies, waits for them, and re-layouts: 9.43 us -> 0.64 us
    pallas_call x2, Pallas kernels: 1.41 us -> 6.85 us  [the longest x1 3.59 us: begin(): pl.pallas_call(begin_kernel, out_shape=(jax.ShapeDtypeStruct((3 * width,...]
    pallas_call x2, Pallas kernels: 7.05 us -> 11 us  [feed_forward(): pl.pallas_call(feed_forward_kernel, out_shape=jax.ShapeDtypeStruct(tokens...]
    all_to_all x3, waiting for transfers between devices: 27.8 us -> 30.3 us  [exchange(): lax.all_to_all(blocks, axis, 0, 0, tiled=True, axis_index_groups=groups)]
  transfers between devices with their start and end apart: 11 -> 11, of which waited for: 7 -> 7; matrix products, arithmetic and copies ran while one was open for 0% -> 0% of each run, Pallas kernels for 4% -> 6%
where the time goes in v3:
time: 169 us; the launch traced here: 168 us
  waiting for transfers between devices  69.8 us (41%)
  starting transfers between devices  56.6 us (33%)
  blocking collectives  21.1 us (12%)
  Pallas kernels  19.5 us (12%)
    all_to_all x3, waiting for transfers between devices, exchange(): lax.all_to_all(blocks, axis, 0, 0, tiled=True, axis_index_groups=groups)  30.3 us
    all_to_all x3, starting transfers between devices, exchange(): lax.all_to_all(blocks, axis, 0, 0, tiled=True, axis_index_groups=groups)  28.9 us
    ppermute x2, waiting for transfers between devices, to_other_colour(): return lax.ppermute(value, axis, route)  26.2 us
    all_to_all x1, blocking collectives, exchange(): lax.all_to_all(blocks, axis, 0, 0, tiled=True, axis_index_groups=groups)  21.1 us
    ppermute x2, waiting for transfers between devices, passed_along(): return lax.ppermute(block, axis, route)  13.3 us
    ppermute x2, starting transfers between devices, passed_along(): return lax.ppermute(block, axis, route)  13.1 us
    pallas_call x2, Pallas kernels, feed_forward(): pl.pallas_call(feed_forward_kernel, out_shape=jax.ShapeDtypeStruct(tokens...  11 us
    ppermute x4, starting transfers between devices, to_other_core(): lax.ppermute(value, axis, [(place, place ^ 1) for place in range(lax.axis...  8 us
  transfers between devices with their start and end apart: 11, of which 7 were waited for; matrix products, arithmetic and copies ran while one was open for 0% of the time, Pallas kernels for 6%

profile of v3, /device:TPU:16, one launch (start us, length us, event | category | flops | bytes accessed | tf_op | source)
XLA Modules:
  0.0 167.8 jit_solution(6945412942266856204)
XLA Ops:
  0.0 3.6 %begin.1 = (bf16[6144,128]{1,0:T(8,128)(2,1)}, bf16[16,8,2048]{2,1,0:T(8,128)(2,1)}) custom-call(s32[2]{0:T(128)} %bitcast.11, bf16[8,2048]{1,0:T(8,128)(2,1)} %bitcast.7, f32[2,2048]{1,0:T(2,128)} %bitcast.9, bf16[2,2048,128]{2,1,0:T(8,128)(2,1)} %bitcast.14, bf16[2,2048,128]{2,1,0:T(8,128)(2,1)} %bitcast.16, bf16[2,128,2048]{2,1,0:T(8,128)(2,1)} %bitcast.18), custom_call_target="tpu_custom_call" | custom-call | flops 786432 | bytes 3145728 | tf_op jit(solution)/shard_map/begin/pallas_call | solution.py:147
  3.6 3.5 %collective-permute-start.1 = (bf16[6144,128]{1,0:T(8,128)(2,1)}, bf16[6144,128]{1,0:T(8,128)(2,1)}, u32[]{:S(2)}, u32[]{:S(2)}) collective-permute-start(bf16[6144,128]{1,0:T(8,128)(2,1)} %get-tuple-element.8.refs_0_), channel_id=1, source_target_pairs={{0,8},{1,3},{2,10},{3,1},{4,12},{5,7},{6,14},{7,5},{8,16},{9,11},{... | collective-permute-start | bytes 4718600 | tf_op jit(solution)/shard_map/ppermute | solution.py:42
  7.1 2.3 %collective-permute-start = (bf16[6144,128]{1,0:T(8,128)(2,1)}, bf16[6144,128]{1,0:T(8,128)(2,1)}, u32[]{:S(2)}, u32[]{:S(2)}) collective-permute-start(bf16[6144,128]{1,0:T(8,128)(2,1)} %get-tuple-element.8.refs_0_), channel_id=1, source_target_pairs={{0,1},{1,0},{2,3},{3,2},{4,5},{5,4},{6,7},{7,6},{8,9},{9,8},{10,11... | collective-permute-start | bytes 4718600 | tf_op jit(solution)/shard_map/ppermute | solution.py:36
  9.4 16.9 %collective-permute-done.1.refs_2_ = bf16[6144,128]{1,0:T(8,128)(2,1)} collective-permute-done((bf16[6144,128]{1,0:T(8,128)(2,1)}, bf16[6144,128]{1,0:T(8,128)(2,1)}, u32[]{:S(2)}, u32[]{:S(2)}) %collective-permute-start.1) | collective-permute-done | bytes 1572896 | tf_op jit(solution)/shard_map/ppermute | solution.py:42
  26.2 1.9 %collective-permute-start.2 = (bf16[6144,128]{1,0:T(8,128)(2,1)}, bf16[6144,128]{1,0:T(8,128)(2,1)}, u32[]{:S(2)}, u32[]{:S(2)}) collective-permute-start(bf16[6144,128]{1,0:T(8,128)(2,1)} %collective-permute-done.1.refs_2_), channel_id=1, source_target_pairs={{0,1},{1,0},{2,3},{3,2},{4,5},{5,4},{6,7},{7,6},{8,9},{9,8},{10,11... | collective-permute-start | bytes 4718600 | tf_op jit(solution)/shard_map/ppermute | solution.py:36
  28.1 14.5 %all-to-all-start = ((bf16[16,8,2048]{2,1,0:T(8,128)(2,1)}), bf16[16,8,2048]{2,1,0:T(8,128)(2,1)}, u32[]{:S(2)}, u32[]{:S(2)}) async-start(bf16[16,8,2048]{2,1,0:T(8,128)(2,1)} %get-tuple-element.7), calls=%async_computation | async-start | bytes 1048576 | tf_op jit(solution)/shard_map/all_to_all | solution.py:46
  42.7 3.3 %pack.1.refs_0_ = bf16[6144,128]{1,0:T(8,128)(2,1)} custom-call(s32[2]{0:T(128)} %bitcast.12, bf16[2,2048,128]{2,1,0:T(8,128)(2,1)} %bitcast.15, bf16[2,2048,128]{2,1,0:T(8,128)(2,1)} %bitcast.17, bf16[2,128,2048]{2,1,0:T(8,128)(2,1)} %bitcast.19), custom_call_target="tpu_custom_call" | custom-call | flops 786432 | bytes 3145728 | tf_op jit(solution)/shard_map/pack/pallas_call | solution.py:112
  45.9 0.0 copy-start.3
  46.0 0.0 copy-start
  46.0 3.1 %collective-permute-start.5 = (bf16[6144,128]{1,0:T(8,128)(2,1)}, bf16[6144,128]{1,0:T(8,128)(2,1)}, u32[]{:S(2)}, u32[]{:S(2)}) collective-permute-start(bf16[6144,128]{1,0:T(8,128)(2,1)} %pack.1.refs_0_), channel_id=1, source_target_pairs={{0,8},{1,3},{2,10},{3,1},{4,12},{5,7},{6,14},{7,5},{8,16},{9,11},{... | collective-permute-start | bytes 4718600 | tf_op jit(solution)/shard_map/ppermute | solution.py:42
  49.0 10.9 %all-to-all-done.tokens_ref = bf16[16,8,2048]{2,1,0:T(8,128)(2,1)} async-done(((bf16[16,8,2048]{2,1,0:T(8,128)(2,1)}), bf16[16,8,2048]{2,1,0:T(8,128)(2,1)}, u32[]{:S(2)}, u32[]{:S(2)}) %all-to-all-start) | async-done | bytes 524320 | tf_op jit(solution)/shard_map/all_to_all | solution.py:46
  60.0 0.0 collective-permute-done.refs_1_
  60.0 0.0 collective-permute-done.2.refs_3_
  60.0 5.5 %ffn.2 = bf16[16,8,2048]{2,1,0:T(8,128)(2,1)} custom-call(bf16[16,8,2048]{2,1,0:T(8,128)(2,1)} %all-to-all-done.tokens_ref, bf16[6144,128]{1,0:T(8,128)(2,1)} %get-tuple-element.8.refs_0_, bf16[6144,128]{1,0:T(8,128)(2,1)} %collective-permute-done.refs_1_, bf16[6144,128]{1,0:T(8,128)(2,1)} %collective-permute-done.1.refs_2_, ...), custom_call_target="tpu_custom_call" | custom-call | flops 805306368 | bytes 6291456 | tf_op jit(solution)/shard_map/ffn/pallas_call | solution.py:203
  65.5 0.0 copy-start.1
  65.5 0.0 copy-start.2
  65.5 5.5 %all-to-all-start.1 = ((bf16[16,8,2048]{2,1,0:T(8,128)(2,1)}), bf16[16,8,2048]{2,1,0:T(8,128)(2,1)S(1)}, u32[]{:S(2)}, u32[]{:S(2)}) async-start(bf16[16,8,2048]{2,1,0:T(8,128)(2,1)} %ffn.2), calls=%async_computation.1 | async-start | bytes 1048576 | tf_op jit(solution)/shard_map/all_to_all | solution.py:46
  71.0 0.0 copy-done.3
  71.0 1.9 %collective-permute-start.4 = (bf16[6144,128]{1,0:T(8,128)(2,1)S(1)}, bf16[6144,128]{1,0:T(8,128)(2,1)}, u32[]{:S(2)}, u32[]{:S(2)}) collective-permute-start(bf16[6144,128]{1,0:T(8,128)(2,1)S(1)} %copy-done.3), channel_id=1, source_target_pairs={{0,1},{1,0},{2,3},{3,2},{4,5},{5,4},{6,7},{7,6},{8,9},{9,8},{10,11... | collective-permute-start | bytes 4718600 | tf_op jit(solution)/shard_map/ppermute | solution.py:36
  73.0 9.4 %collective-permute-done.5.refs_2_ = bf16[6144,128]{1,0:T(8,128)(2,1)} collective-permute-done((bf16[6144,128]{1,0:T(8,128)(2,1)}, bf16[6144,128]{1,0:T(8,128)(2,1)}, u32[]{:S(2)}, u32[]{:S(2)}) %collective-permute-start.5) | collective-permute-done | bytes 1572896 | tf_op jit(solution)/shard_map/ppermute | solution.py:42
  82.3 1.9 %collective-permute-start.6 = (bf16[6144,128]{1,0:T(8,128)(2,1)}, bf16[6144,128]{1,0:T(8,128)(2,1)}, u32[]{:S(2)}, u32[]{:S(2)}) collective-permute-start(bf16[6144,128]{1,0:T(8,128)(2,1)} %collective-permute-done.5.refs_2_), channel_id=1, source_target_pairs={{0,1},{1,0},{2,3},{3,2},{4,5},{5,4},{6,7},{7,6},{8,9},{9,8},{10,11... | collective-permute-start | bytes 4718600 | tf_op jit(solution)/shard_map/ppermute | solution.py:36
  84.2 2.5 %all-to-all-done.1.parts_ref = bf16[16,8,2048]{2,1,0:T(8,128)(2,1)S(1)} async-done(((bf16[16,8,2048]{2,1,0:T(8,128)(2,1)}), bf16[16,8,2048]{2,1,0:T(8,128)(2,1)S(1)}, u32[]{:S(2)}, u32[]{:S(2)}) %all-to-all-start.1) | async-done | bytes 524320 | tf_op jit(solution)/shard_map/all_to_all | solution.py:46
  86.8 0.0 copy-done
  86.8 0.1 advance.2
  86.8 9.8 %collective-permute-start.3 = (bf16[8,2048]{1,0:T(8,128)(2,1)S(1)}, bf16[8,2048]{1,0:T(8,128)(2,1)S(1)}, u32[]{:S(2)}, u32[]{:S(2)}) collective-permute-start(bf16[8,2048]{1,0:T(8,128)(2,1)S(1)} %advance.2), channel_id=1, source_target_pairs={{704,0},{0,64},{64,128},{128,192},{192,256},{256,320},{320,384},{3... | collective-permute-start | bytes 98312 | tf_op jit(solution)/shard_map/ppermute | solution.py:19
  96.7 4.7 %collective-permute-done.3.refs_1_.rows_ref = bf16[8,2048]{1,0:T(8,128)(2,1)S(1)} collective-permute-done((bf16[8,2048]{1,0:T(8,128)(2,1)S(1)}, bf16[8,2048]{1,0:T(8,128)(2,1)S(1)}, u32[]{:S(2)}, u32[]{:S(2)}) %collective-permute-start.3) | collective-permute-done | bytes 32800 | tf_op jit(solution)/shard_map/ppermute | solution.py:19
  101.4 0.0 copy-done.1
  101.4 0.0 copy-done.2
  101.4 1.5 spread.1
  102.9 8.9 %all-to-all-start.2 = ((bf16[16,8,2048]{2,1,0:T(8,128)(2,1)}), bf16[16,8,2048]{2,1,0:T(8,128)(2,1)}, u32[]{:S(2)}, u32[]{:S(2)}) async-start(bf16[16,8,2048]{2,1,0:T(8,128)(2,1)} %spread.1), calls=%async_computation.2 | async-start | bytes 1048576 | tf_op jit(solution)/shard_map/all_to_all | solution.py:46
  111.8 0.0 collective-permute-done.4.refs_1_
  111.8 0.0 collective-permute-done.6.refs_3_
  111.9 16.8 %all-to-all-done.2.tokens_ref = bf16[16,8,2048]{2,1,0:T(8,128)(2,1)} async-done(((bf16[16,8,2048]{2,1,0:T(8,128)(2,1)}), bf16[16,8,2048]{2,1,0:T(8,128)(2,1)}, u32[]{:S(2)}, u32[]{:S(2)}) %all-to-all-start.2) | async-done | bytes 524320 | tf_op jit(solution)/shard_map/all_to_all | solution.py:46
  128.6 5.5 %ffn.3 = bf16[16,8,2048]{2,1,0:T(8,128)(2,1)} custom-call(bf16[16,8,2048]{2,1,0:T(8,128)(2,1)} %all-to-all-done.2.tokens_ref, bf16[6144,128]{1,0:T(8,128)(2,1)} %pack.1.refs_0_, bf16[6144,128]{1,0:T(8,128)(2,1)} %collective-permute-done.4.refs_1_, bf16[6144,128]{1,0:T(8,128)(2,1)} %collective-permute-done.5.refs_2_, ...), custom_call_target="tpu_custom_call" | custom-call | flops 805306368 | bytes 6291456 | tf_op jit(solution)/shard_map/ffn/pallas_call | solution.py:203
  134.1 21.1 %all_to_all.20.parts_ref = bf16[16,8,2048]{2,1,0:T(8,128)(2,1)S(1)} all-to-all(bf16[16,8,2048]{2,1,0:T(8,128)(2,1)} %ffn.3), channel_id=1, replica_groups={{0,4,10,14,16,20,26,30,32,36,42,46,48,52,58,62},{2,6,8,12,18,22,24,28,3..., dimensions={0} | all-to-all | bytes 1048576 | tf_op jit(solution)/shard_map/all_to_all | solution.py:46
  155.3 0.1 advance.3
  155.3 3.3 %collective-permute-start.7 = (bf16[8,2048]{1,0:T(8,128)(2,1)S(1)}, bf16[8,2048]{1,0:T(8,128)(2,1)S(1)}, u32[]{:S(2)}, u32[]{:S(2)}) collective-permute-start(bf16[8,2048]{1,0:T(8,128)(2,1)S(1)} %advance.3), channel_id=1, source_target_pairs={{704,0},{0,64},{64,128},{128,192},{192,256},{256,320},{320,384},{3... | collective-permute-start | bytes 98312 | tf_op jit(solution)/shard_map/ppermute | solution.py:19
  158.6 8.5 %collective-permute-done.7 = bf16[8,2048]{1,0:T(8,128)(2,1)S(1)} collective-permute-done((bf16[8,2048]{1,0:T(8,128)(2,1)S(1)}, bf16[8,2048]{1,0:T(8,128)(2,1)S(1)}, u32[]{:S(2)}, u32[]{:S(2)}) %collective-permute-start.7) | collective-permute-done | bytes 32800 | tf_op jit(solution)/shard_map/ppermute | solution.py:19
  167.2 0.6 copy.8
Async XLA Ops:
  3.6 22.6 %collective-permute-start.1 = (bf16[6144,128]{1,0:T(8,128)(2,1)}, bf16[6144,128]{1,0:T(8,128)(2,1)}, u32[]{:S(2)}, u32[]{:S(2)}) collective-permute-start(bf16[6144,128]{1,0:T(8,128)(2,1)} %get-tuple-element.8.refs_0_), channel_id=1, source_target_pairs={{0,8},{1,3},{2,10},{3,1},{4,12},{5,7},{6,14},{7,5},{8,16},{9,11},{... | collective-permute-start | bytes 4718600 | tf_op jit(solution)/shard_map/ppermute | solution.py:42
  7.1 52.9 %collective-permute-start = (bf16[6144,128]{1,0:T(8,128)(2,1)}, bf16[6144,128]{1,0:T(8,128)(2,1)}, u32[]{:S(2)}, u32[]{:S(2)}) collective-permute-start(bf16[6144,128]{1,0:T(8,128)(2,1)} %get-tuple-element.8.refs_0_), channel_id=1, source_target_pairs={{0,1},{1,0},{2,3},{3,2},{4,5},{5,4},{6,7},{7,6},{8,9},{9,8},{10,11... | collective-permute-start | bytes 4718600 | tf_op jit(solution)/shard_map/ppermute | solution.py:36
  26.2 33.8 %collective-permute-start.2 = (bf16[6144,128]{1,0:T(8,128)(2,1)}, bf16[6144,128]{1,0:T(8,128)(2,1)}, u32[]{:S(2)}, u32[]{:S(2)}) collective-permute-start(bf16[6144,128]{1,0:T(8,128)(2,1)} %collective-permute-done.1.refs_2_), channel_id=1, source_target_pairs={{0,1},{1,0},{2,3},{3,2},{4,5},{5,4},{6,7},{7,6},{8,9},{9,8},{10,11... | collective-permute-start | bytes 4718600 | tf_op jit(solution)/shard_map/ppermute | solution.py:36
  28.1 31.8 %all-to-all-start = ((bf16[16,8,2048]{2,1,0:T(8,128)(2,1)}), bf16[16,8,2048]{2,1,0:T(8,128)(2,1)}, u32[]{:S(2)}, u32[]{:S(2)}) async-start(bf16[16,8,2048]{2,1,0:T(8,128)(2,1)} %get-tuple-element.7), calls=%async_computation | async-start | bytes 1048576 | tf_op jit(solution)/shard_map/all_to_all | solution.py:46
  45.9 25.1 %copy-start.3 = (bf16[6144,128]{1,0:T(8,128)(2,1)S(1)}, bf16[6144,128]{1,0:T(8,128)(2,1)}, u32[]{:S(2)}) copy-start(bf16[6144,128]{1,0:T(8,128)(2,1)} %pack.1.refs_0_) | copy-start | bytes 4718596
  46.0 40.8 %copy-start = (bf16[1,8,2048]{2,1,0:T(8,128)(2,1)S(1)}, bf16[1,8,2048]{2,1,0:T(8,128)(2,1)}, u32[]{:S(2)}) copy-start(bf16[1,8,2048]{2,1,0:T(8,128)(2,1)} %param.6) | copy-start | bytes 98308
  46.0 36.4 %collective-permute-start.5 = (bf16[6144,128]{1,0:T(8,128)(2,1)}, bf16[6144,128]{1,0:T(8,128)(2,1)}, u32[]{:S(2)}, u32[]{:S(2)}) collective-permute-start(bf16[6144,128]{1,0:T(8,128)(2,1)} %pack.1.refs_0_), channel_id=1, source_target_pairs={{0,8},{1,3},{2,10},{3,1},{4,12},{5,7},{6,14},{7,5},{8,16},{9,11},{... | collective-permute-start | bytes 4718600 | tf_op jit(solution)/shard_map/ppermute | solution.py:42
  65.5 35.9 %copy-start.1 = (f32[1,2,2048]{2,1,0:T(2,128)S(1)}, f32[1,2,2048]{2,1,0:T(2,128)}, u32[]{:S(2)}) copy-start(f32[1,2,2048]{2,1,0:T(2,128)} %param.10) | copy-start | bytes 49156
  65.5 35.9 %copy-start.2 = (s32[2,1]{0,1:T(1,128)S(1)}, s32[2,1]{0,1:T(1,128)}, u32[]{:S(2)}) copy-start(s32[2,1]{0,1:T(1,128)} %param.11) | copy-start | bytes 28
  65.5 21.2 %all-to-all-start.1 = ((bf16[16,8,2048]{2,1,0:T(8,128)(2,1)}), bf16[16,8,2048]{2,1,0:T(8,128)(2,1)S(1)}, u32[]{:S(2)}, u32[]{:S(2)}) async-start(bf16[16,8,2048]{2,1,0:T(8,128)(2,1)} %ffn.2), calls=%async_computation.1 | async-start | bytes 1048576 | tf_op jit(solution)/shard_map/all_to_all | solution.py:46
  71.0 40.8 %collective-permute-start.4 = (bf16[6144,128]{1,0:T(8,128)(2,1)S(1)}, bf16[6144,128]{1,0:T(8,128)(2,1)}, u32[]{:S(2)}, u32[]{:S(2)}) collective-permute-start(bf16[6144,128]{1,0:T(8,128)(2,1)S(1)} %copy-done.3), channel_id=1, source_target_pairs={{0,1},{1,0},{2,3},{3,2},{4,5},{5,4},{6,7},{7,6},{8,9},{9,8},{10,11... | collective-permute-start | bytes 4718600 | tf_op jit(solution)/shard_map/ppermute | solution.py:36
  82.3 29.5 %collective-permute-start.6 = (bf16[6144,128]{1,0:T(8,128)(2,1)}, bf16[6144,128]{1,0:T(8,128)(2,1)}, u32[]{:S(2)}, u32[]{:S(2)}) collective-permute-start(bf16[6144,128]{1,0:T(8,128)(2,1)} %collective-permute-done.5.refs_2_), channel_id=1, source_target_pairs={{0,1},{1,0},{2,3},{3,2},{4,5},{5,4},{6,7},{7,6},{8,9},{9,8},{10,11... | collective-permute-start | bytes 4718600 | tf_op jit(solution)/shard_map/ppermute | solution.py:36
  86.8 14.6 %collective-permute-start.3 = (bf16[8,2048]{1,0:T(8,128)(2,1)S(1)}, bf16[8,2048]{1,0:T(8,128)(2,1)S(1)}, u32[]{:S(2)}, u32[]{:S(2)}) collective-permute-start(bf16[8,2048]{1,0:T(8,128)(2,1)S(1)} %advance.2), channel_id=1, source_target_pairs={{704,0},{0,64},{64,128},{128,192},{192,256},{256,320},{320,384},{3... | collective-permute-start | bytes 98312 | tf_op jit(solution)/shard_map/ppermute | solution.py:19
  102.9 25.7 %all-to-all-start.2 = ((bf16[16,8,2048]{2,1,0:T(8,128)(2,1)}), bf16[16,8,2048]{2,1,0:T(8,128)(2,1)}, u32[]{:S(2)}, u32[]{:S(2)}) async-start(bf16[16,8,2048]{2,1,0:T(8,128)(2,1)} %spread.1), calls=%async_computation.2 | async-start | bytes 1048576 | tf_op jit(solution)/shard_map/all_to_all | solution.py:46
  155.3 11.8 %collective-permute-start.7 = (bf16[8,2048]{1,0:T(8,128)(2,1)S(1)}, bf16[8,2048]{1,0:T(8,128)(2,1)S(1)}, u32[]{:S(2)}, u32[]{:S(2)}) collective-permute-start(bf16[8,2048]{1,0:T(8,128)(2,1)S(1)} %advance.3), channel_id=1, source_target_pairs={{704,0},{0,64},{64,128},{128,192},{192,256},{256,320},{320,384},{3... | collective-permute-start | bytes 98312 | tf_op jit(solution)/shard_map/ppermute | solution.py:19

commit v4 on v3

--- a/solution.py
+++ b/solution.py
@@ -165,26 +165,35 @@
     )(chosen, rows, gains, gate_weight, up_weight, down_weight)
 
 
-def feed_forward_kernel(tokens_ref, *refs):
+def feed_forward_kernel(tokens_ref, own_ref, *refs):
     count = (len(refs) - 2) // 2
-    sources, out_ref, packs, arrived = refs[:count], refs[count], refs[count + 1 : -1], refs[-1]
+    sources, out_ref, held, arrived = refs[:count], refs[count], refs[count + 1 : -1], refs[-1]
+    members, rows, width = tokens_ref.shape
+    parts = ((0, 2 * width), (2 * width, 3 * width))
     copies = [
-        pltpu.make_async_copy(source, slot, arrived.at[index])
-        for index, (source, slot) in enumerate(zip(sources, packs))
-    ]
-    for copy in copies:
-        copy.start()
-    members, rows, width = tokens_ref.shape
+        [
+            pltpu.make_async_copy(source.at[start:end], slot.at[start:end], arrived.at[part, index])
+            for index, (source, slot) in enumerate(zip(sources, held))
+        ]
+        for part, (start, end) in enumerate(parts)
+    ]
+    for part in copies:
+        for copy in part:
+            copy.start()
     tokens = tokens_ref[...].reshape(members * rows, width)
-    lanes = packs[0].shape[1]
+    packs = (own_ref, *held)
+    lanes = own_ref.shape[1]
     hidden = []
-    for copy, packed in zip(copies, packs):
-        copy.wait()
+    for index, packed in enumerate(packs):
+        if index:
+            copies[0][index - 1].wait()
         both = jnp.concatenate([packed[0:width], packed[width : 2 * width]], axis=1)
         value = jnp.dot(tokens, both, preferred_element_type=jnp.float32)
         gate_value, up_value = value[:, :lanes], value[:, lanes:]
         hidden.append((gate_value / (1.0 + jnp.exp(-gate_value)) * up_value).astype(tokens.dtype))
     hidden = jnp.concatenate(hidden, axis=1)
+    for copy in copies[1]:
+        copy.wait()
     for column in range(0, width // lanes, 2):
         slabs = []
         for step in range(2):
@@ -196,26 +205,26 @@
         )
 
 
-def feed_forward(tokens, packs):
+def feed_forward(tokens, own, others):
     members, rows, width = tokens.shape
-    lanes = packs[0].shape[1]
-    shards = len(packs)
+    lanes = own.shape[1]
+    shards = 1 + len(others)
     return pl.pallas_call(
         feed_forward_kernel,
         out_shape=jax.ShapeDtypeStruct(tokens.shape, tokens.dtype),
-        in_specs=[IN_VMEM] + [IN_HBM] * shards,
+        in_specs=[IN_VMEM, IN_VMEM] + [IN_HBM] * len(others),
         out_specs=IN_VMEM,
-        scratch_shapes=[pltpu.VMEM(pack.shape, pack.dtype) for pack in packs]
-        + [pltpu.SemaphoreType.DMA((shards,))],
+        scratch_shapes=[pltpu.VMEM(own.shape, own.dtype) for _ in others]
+        + [pltpu.SemaphoreType.DMA((2, len(others)))],
         cost_estimate=pl.CostEstimate(
             flops=6 * members * rows * width * lanes * shards,
             bytes_accessed=6 * width * lanes * shards,
             transcendentals=members * rows * lanes * shards,
         ),
-        compiler_params=room(62),
+        compiler_params=room(8),
         name="ffn",
         interpret=INTERPRET,
-    )(tokens, *packs)
+    )(tokens, own, *others)
 
 
 def advance_kernel(parts_ref, rows_ref, out_ref):
@@ -255,7 +264,7 @@
         tokens = exchange(copies, "dp", groups)
         own_pair = to_other_core(own, "dp")
         near_pair = to_other_core(near, "dp")
-        partial_value = feed_forward(tokens, (own, own_pair, near, near_pair))
+        partial_value = feed_forward(tokens, own, (own_pair, near, near_pair))
         parts = exchange(partial_value, "dp", groups)
         advanced = advance(parts, current)
         current = passed_along(advanced, "section", 1)

time: 169 us -> 166 us (0.982)
  Pallas kernels: 19.5 us -> 15.7 us
  waiting for transfers between devices: 69.8 us -> 67.4 us
  starting transfers between devices: 56.6 us -> 58.9 us
    pallas_call x2, Pallas kernels: 11 us -> 7.06 us  [feed_forward(): pl.pallas_call(feed_forward_kernel, out_shape=jax.ShapeDtypeStruct(tokens...]
    ppermute x2, starting transfers between devices: 13.1 us -> 14.9 us  [passed_along(): return lax.ppermute(block, axis, route)]
  transfers between devices with their start and end apart: 11 -> 11, of which waited for: 7 -> 7; matrix products, arithmetic and copies ran while one was open for 0% -> 0% of each run, Pallas kernels for 6% -> 5%
where the time goes in v4:
time: 166 us; the launch traced here: 165 us
  waiting for transfers between devices  67.4 us (41%)
  starting transfers between devices  58.9 us (35%)
  blocking collectives  21 us (13%)
  Pallas kernels  15.7 us (9%)
  local copies, waits for them, and re-layouts  2.04 us (1%)
    all_to_all x3, waiting for transfers between devices, exchange(): lax.all_to_all(blocks, axis, 0, 0, tiled=True, axis_index_groups=groups)  28.8 us
    all_to_all x3, starting transfers between devices, exchange(): lax.all_to_all(blocks, axis, 0, 0, tiled=True, axis_index_groups=groups)  28.8 us
    ppermute x2, waiting for transfers between devices, to_other_colour(): return lax.ppermute(value, axis, route)  26 us
    all_to_all x1, blocking collectives, exchange(): lax.all_to_all(blocks, axis, 0, 0, tiled=True, axis_index_groups=groups)  21 us
    ppermute x2, starting transfers between devices, passed_along(): return lax.ppermute(block, axis, route)  14.9 us
    ppermute x2, waiting for transfers between devices, passed_along(): return lax.ppermute(block, axis, route)  12.6 us
    ppermute x4, starting transfers between devices, to_other_core(): lax.ppermute(value, axis, [(place, place ^ 1) for place in range(lax.axis...  8 us
    ppermute x2, starting transfers between devices, to_other_colour(): return lax.ppermute(value, axis, route)  7.17 us
  transfers between devices with their start and end apart: 11, of which 7 were waited for; matrix products, arithmetic and copies ran while one was open for 0% of the time, Pallas kernels for 5%

profile of v4, /device:TPU:16, one launch (start us, length us, event | category | flops | bytes accessed | tf_op | source)
XLA Modules:
  0.0 165.1 jit_solution(6262841202337594685)
XLA Ops:
  0.0 3.7 %begin.1 = (bf16[6144,128]{1,0:T(8,128)(2,1)}, bf16[16,8,2048]{2,1,0:T(8,128)(2,1)}) custom-call(s32[2]{0:T(128)} %bitcast.11, bf16[8,2048]{1,0:T(8,128)(2,1)} %bitcast.7, f32[2,2048]{1,0:T(2,128)} %bitcast.9, bf16[2,2048,128]{2,1,0:T(8,128)(2,1)} %bitcast.14, bf16[2,2048,128]{2,1,0:T(8,128)(2,1)} %bitcast.16, bf16[2,128,2048]{2,1,0:T(8,128)(2,1)} %bitcast.18), custom_call_target="tpu_custom_call" | custom-call | flops 786432 | bytes 3145728 | tf_op jit(solution)/shard_map/begin/pallas_call | solution.py:147
  3.7 3.5 %collective-permute-start.1 = (bf16[6144,128]{1,0:T(8,128)(2,1)}, bf16[6144,128]{1,0:T(8,128)(2,1)}, u32[]{:S(2)}, u32[]{:S(2)}) collective-permute-start(bf16[6144,128]{1,0:T(8,128)(2,1)} %get-tuple-element.8.own_ref), channel_id=1, source_target_pairs={{0,8},{1,3},{2,10},{3,1},{4,12},{5,7},{6,14},{7,5},{8,16},{9,11},{... | collective-permute-start | bytes 4718600 | tf_op jit(solution)/shard_map/ppermute | solution.py:42
  7.2 2.3 %collective-permute-start = (bf16[6144,128]{1,0:T(8,128)(2,1)}, bf16[6144,128]{1,0:T(8,128)(2,1)}, u32[]{:S(2)}, u32[]{:S(2)}) collective-permute-start(bf16[6144,128]{1,0:T(8,128)(2,1)} %get-tuple-element.8.own_ref), channel_id=1, source_target_pairs={{0,1},{1,0},{2,3},{3,2},{4,5},{5,4},{6,7},{7,6},{8,9},{9,8},{10,11... | collective-permute-start | bytes 4718600 | tf_op jit(solution)/shard_map/ppermute | solution.py:36
  9.4 16.9 %collective-permute-done.1.refs_1_ = bf16[6144,128]{1,0:T(8,128)(2,1)} collective-permute-done((bf16[6144,128]{1,0:T(8,128)(2,1)}, bf16[6144,128]{1,0:T(8,128)(2,1)}, u32[]{:S(2)}, u32[]{:S(2)}) %collective-permute-start.1) | collective-permute-done | bytes 1572896 | tf_op jit(solution)/shard_map/ppermute | solution.py:42
  26.3 1.9 %collective-permute-start.2 = (bf16[6144,128]{1,0:T(8,128)(2,1)}, bf16[6144,128]{1,0:T(8,128)(2,1)}, u32[]{:S(2)}, u32[]{:S(2)}) collective-permute-start(bf16[6144,128]{1,0:T(8,128)(2,1)} %collective-permute-done.1.refs_1_), channel_id=1, source_target_pairs={{0,1},{1,0},{2,3},{3,2},{4,5},{5,4},{6,7},{7,6},{8,9},{9,8},{10,11... | collective-permute-start | bytes 4718600 | tf_op jit(solution)/shard_map/ppermute | solution.py:36
  28.2 13.9 %all-to-all-start = ((bf16[16,8,2048]{2,1,0:T(8,128)(2,1)}), bf16[16,8,2048]{2,1,0:T(8,128)(2,1)S(1)}, u32[]{:S(2)}, u32[]{:S(2)}) async-start(bf16[16,8,2048]{2,1,0:T(8,128)(2,1)} %get-tuple-element.7), calls=%async_computation | async-start | bytes 1048576 | tf_op jit(solution)/shard_map/all_to_all | solution.py:46
  42.1 0.0 copy-start.2
  42.2 3.4 %pack.1.own_ref = bf16[6144,128]{1,0:T(8,128)(2,1)} custom-call(s32[2]{0:T(128)} %bitcast.12, bf16[2,2048,128]{2,1,0:T(8,128)(2,1)} %bitcast.15, bf16[2,2048,128]{2,1,0:T(8,128)(2,1)} %bitcast.17, bf16[2,128,2048]{2,1,0:T(8,128)(2,1)} %bitcast.19), custom_call_target="tpu_custom_call" | custom-call | flops 786432 | bytes 3145728 | tf_op jit(solution)/shard_map/pack/pallas_call | solution.py:112
  45.5 0.0 copy-start
  45.5 3.7 %collective-permute-start.5 = (bf16[6144,128]{1,0:T(8,128)(2,1)}, bf16[6144,128]{1,0:T(8,128)(2,1)}, u32[]{:S(2)}, u32[]{:S(2)}) collective-permute-start(bf16[6144,128]{1,0:T(8,128)(2,1)} %pack.1.own_ref), channel_id=1, source_target_pairs={{0,8},{1,3},{2,10},{3,1},{4,12},{5,7},{6,14},{7,5},{8,16},{9,11},{... | collective-permute-start | bytes 4718600 | tf_op jit(solution)/shard_map/ppermute | solution.py:42
  49.2 10.0 %all-to-all-done.tokens_ref = bf16[16,8,2048]{2,1,0:T(8,128)(2,1)S(1)} async-done(((bf16[16,8,2048]{2,1,0:T(8,128)(2,1)}), bf16[16,8,2048]{2,1,0:T(8,128)(2,1)S(1)}, u32[]{:S(2)}, u32[]{:S(2)}) %all-to-all-start) | async-done | bytes 524320 | tf_op jit(solution)/shard_map/all_to_all | solution.py:46
  59.3 0.0 collective-permute-done.refs_0_
  59.3 0.0 collective-permute-done.2.refs_2_
  59.3 0.0 copy-start.1
  59.3 1.4 copy-done.1
  60.7 4.0 %ffn.2 = bf16[16,8,2048]{2,1,0:T(8,128)(2,1)} custom-call(bf16[16,8,2048]{2,1,0:T(8,128)(2,1)S(1)} %all-to-all-done.tokens_ref, bf16[6144,128]{1,0:T(8,128)(2,1)S(1)} %copy-done.1, bf16[6144,128]{1,0:T(8,128)(2,1)} %collective-permute-done.refs_0_, bf16[6144,128]{1,0:T(8,128)(2,1)} %collective-permute-done.1.refs_1_, ...), custom_call_target="tpu_custom_call" | custom-call | flops 805306368 | bytes 6291456 | tf_op jit(solution)/shard_map/ffn/pallas_call | solution.py:212
  64.7 0.0 copy-start.3
  64.7 0.0 copy-start.4
  64.7 5.9 %all-to-all-start.1 = ((bf16[16,8,2048]{2,1,0:T(8,128)(2,1)}), bf16[16,8,2048]{2,1,0:T(8,128)(2,1)S(1)}, u32[]{:S(2)}, u32[]{:S(2)}) async-start(bf16[16,8,2048]{2,1,0:T(8,128)(2,1)} %ffn.2), calls=%async_computation.1 | async-start | bytes 1048576 | tf_op jit(solution)/shard_map/all_to_all | solution.py:46
  70.7 0.0 copy-done
  70.7 1.9 %collective-permute-start.4 = (bf16[6144,128]{1,0:T(8,128)(2,1)S(1)}, bf16[6144,128]{1,0:T(8,128)(2,1)}, u32[]{:S(2)}, u32[]{:S(2)}) collective-permute-start(bf16[6144,128]{1,0:T(8,128)(2,1)S(1)} %copy-done), channel_id=1, source_target_pairs={{0,1},{1,0},{2,3},{3,2},{4,5},{5,4},{6,7},{7,6},{8,9},{9,8},{10,11... | collective-permute-start | bytes 4718600 | tf_op jit(solution)/shard_map/ppermute | solution.py:36
  72.6 9.1 %collective-permute-done.5.refs_1_ = bf16[6144,128]{1,0:T(8,128)(2,1)} collective-permute-done((bf16[6144,128]{1,0:T(8,128)(2,1)}, bf16[6144,128]{1,0:T(8,128)(2,1)}, u32[]{:S(2)}, u32[]{:S(2)}) %collective-permute-start.5) | collective-permute-done | bytes 1572896 | tf_op jit(solution)/shard_map/ppermute | solution.py:42
  81.7 1.9 %collective-permute-start.6 = (bf16[6144,128]{1,0:T(8,128)(2,1)}, bf16[6144,128]{1,0:T(8,128)(2,1)}, u32[]{:S(2)}, u32[]{:S(2)}) collective-permute-start(bf16[6144,128]{1,0:T(8,128)(2,1)} %collective-permute-done.5.refs_1_), channel_id=1, source_target_pairs={{0,1},{1,0},{2,3},{3,2},{4,5},{5,4},{6,7},{7,6},{8,9},{9,8},{10,11... | collective-permute-start | bytes 4718600 | tf_op jit(solution)/shard_map/ppermute | solution.py:36
  83.6 2.1 %all-to-all-done.1.parts_ref = bf16[16,8,2048]{2,1,0:T(8,128)(2,1)S(1)} async-done(((bf16[16,8,2048]{2,1,0:T(8,128)(2,1)}), bf16[16,8,2048]{2,1,0:T(8,128)(2,1)S(1)}, u32[]{:S(2)}, u32[]{:S(2)}) %all-to-all-start.1) | async-done | bytes 524320 | tf_op jit(solution)/shard_map/all_to_all | solution.py:46
  85.7 0.0 copy-done.2
  85.7 0.1 advance.2
  85.8 11.1 %collective-permute-start.3 = (bf16[8,2048]{1,0:T(8,128)(2,1)S(1)}, bf16[8,2048]{1,0:T(8,128)(2,1)S(1)}, u32[]{:S(2)}, u32[]{:S(2)}) collective-permute-start(bf16[8,2048]{1,0:T(8,128)(2,1)S(1)} %advance.2), channel_id=1, source_target_pairs={{704,0},{0,64},{64,128},{128,192},{192,256},{256,320},{320,384},{3... | collective-permute-start | bytes 98312 | tf_op jit(solution)/shard_map/ppermute | solution.py:19
  97.0 4.5 %collective-permute-done.3.refs_1_.rows_ref = bf16[8,2048]{1,0:T(8,128)(2,1)S(1)} collective-permute-done((bf16[8,2048]{1,0:T(8,128)(2,1)S(1)}, bf16[8,2048]{1,0:T(8,128)(2,1)S(1)}, u32[]{:S(2)}, u32[]{:S(2)}) %collective-permute-start.3) | collective-permute-done | bytes 32800 | tf_op jit(solution)/shard_map/ppermute | solution.py:19
  101.5 0.0 copy-done.3
  101.5 0.0 copy-done.4
  101.5 1.5 spread.1
  103.0 8.9 %all-to-all-start.2 = ((bf16[16,8,2048]{2,1,0:T(8,128)(2,1)}), bf16[16,8,2048]{2,1,0:T(8,128)(2,1)S(1)}, u32[]{:S(2)}, u32[]{:S(2)}) async-start(bf16[16,8,2048]{2,1,0:T(8,128)(2,1)} %spread.1), calls=%async_computation.2 | async-start | bytes 1048576 | tf_op jit(solution)/shard_map/all_to_all | solution.py:46
  111.9 0.0 collective-permute-done.4.refs_0_
  111.9 0.0 collective-permute-done.6.refs_2_
  111.9 16.6 %all-to-all-done.2.tokens_ref = bf16[16,8,2048]{2,1,0:T(8,128)(2,1)S(1)} async-done(((bf16[16,8,2048]{2,1,0:T(8,128)(2,1)}), bf16[16,8,2048]{2,1,0:T(8,128)(2,1)S(1)}, u32[]{:S(2)}, u32[]{:S(2)}) %all-to-all-start.2) | async-done | bytes 524320 | tf_op jit(solution)/shard_map/all_to_all | solution.py:46
  128.6 3.0 %ffn.3 = bf16[16,8,2048]{2,1,0:T(8,128)(2,1)S(1)} custom-call(bf16[16,8,2048]{2,1,0:T(8,128)(2,1)S(1)} %all-to-all-done.2.tokens_ref, bf16[6144,128]{1,0:T(8,128)(2,1)S(1)} %copy-done, bf16[6144,128]{1,0:T(8,128)(2,1)} %collective-permute-done.4.refs_0_, bf16[6144,128]{1,0:T(8,128)(2,1)} %collective-permute-done.5.refs_1_, ...), custom_call_target="tpu_custom_call" | custom-call | flops 805306368 | bytes 6291456 | tf_op jit(solution)/shard_map/ffn/pallas_call | solution.py:212
  131.6 21.0 %all_to_all.20.parts_ref = bf16[16,8,2048]{2,1,0:T(8,128)(2,1)S(1)} all-to-all(bf16[16,8,2048]{2,1,0:T(8,128)(2,1)S(1)} %ffn.3), channel_id=1, replica_groups={{0,4,10,14,16,20,26,30,32,36,42,46,48,52,58,62},{2,6,8,12,18,22,24,28,3..., dimensions={0} | all-to-all | bytes 1048576 | tf_op jit(solution)/shard_map/all_to_all | solution.py:46
  152.6 0.1 advance.3
  152.7 3.8 %collective-permute-start.7 = (bf16[8,2048]{1,0:T(8,128)(2,1)S(1)}, bf16[8,2048]{1,0:T(8,128)(2,1)S(1)}, u32[]{:S(2)}, u32[]{:S(2)}) collective-permute-start(bf16[8,2048]{1,0:T(8,128)(2,1)S(1)} %advance.3), channel_id=1, source_target_pairs={{704,0},{0,64},{64,128},{128,192},{192,256},{256,320},{320,384},{3... | collective-permute-start | bytes 98312 | tf_op jit(solution)/shard_map/ppermute | solution.py:19
  156.4 8.0 %collective-permute-done.7 = bf16[8,2048]{1,0:T(8,128)(2,1)S(1)} collective-permute-done((bf16[8,2048]{1,0:T(8,128)(2,1)S(1)}, bf16[8,2048]{1,0:T(8,128)(2,1)S(1)}, u32[]{:S(2)}, u32[]{:S(2)}) %collective-permute-start.7) | collective-permute-done | bytes 32800 | tf_op jit(solution)/shard_map/ppermute | solution.py:19
  164.5 0.6 copy.8
Async XLA Ops:
  3.7 22.6 %collective-permute-start.1 = (bf16[6144,128]{1,0:T(8,128)(2,1)}, bf16[6144,128]{1,0:T(8,128)(2,1)}, u32[]{:S(2)}, u32[]{:S(2)}) collective-permute-start(bf16[6144,128]{1,0:T(8,128)(2,1)} %get-tuple-element.8.own_ref), channel_id=1, source_target_pairs={{0,8},{1,3},{2,10},{3,1},{4,12},{5,7},{6,14},{7,5},{8,16},{9,11},{... | collective-permute-start | bytes 4718600 | tf_op jit(solution)/shard_map/ppermute | solution.py:42
  7.2 52.1 %collective-permute-start = (bf16[6144,128]{1,0:T(8,128)(2,1)}, bf16[6144,128]{1,0:T(8,128)(2,1)}, u32[]{:S(2)}, u32[]{:S(2)}) collective-permute-start(bf16[6144,128]{1,0:T(8,128)(2,1)} %get-tuple-element.8.own_ref), channel_id=1, source_target_pairs={{0,1},{1,0},{2,3},{3,2},{4,5},{5,4},{6,7},{7,6},{8,9},{9,8},{10,11... | collective-permute-start | bytes 4718600 | tf_op jit(solution)/shard_map/ppermute | solution.py:36
  26.3 33.0 %collective-permute-start.2 = (bf16[6144,128]{1,0:T(8,128)(2,1)}, bf16[6144,128]{1,0:T(8,128)(2,1)}, u32[]{:S(2)}, u32[]{:S(2)}) collective-permute-start(bf16[6144,128]{1,0:T(8,128)(2,1)} %collective-permute-done.1.refs_1_), channel_id=1, source_target_pairs={{0,1},{1,0},{2,3},{3,2},{4,5},{5,4},{6,7},{7,6},{8,9},{9,8},{10,11... | collective-permute-start | bytes 4718600 | tf_op jit(solution)/shard_map/ppermute | solution.py:36
  28.2 31.0 %all-to-all-start = ((bf16[16,8,2048]{2,1,0:T(8,128)(2,1)}), bf16[16,8,2048]{2,1,0:T(8,128)(2,1)S(1)}, u32[]{:S(2)}, u32[]{:S(2)}) async-start(bf16[16,8,2048]{2,1,0:T(8,128)(2,1)} %get-tuple-element.7), calls=%async_computation | async-start | bytes 1048576 | tf_op jit(solution)/shard_map/all_to_all | solution.py:46
  42.1 43.6 %copy-start.2 = (bf16[1,8,2048]{2,1,0:T(8,128)(2,1)S(1)}, bf16[1,8,2048]{2,1,0:T(8,128)(2,1)}, u32[]{:S(2)}) copy-start(bf16[1,8,2048]{2,1,0:T(8,128)(2,1)} %param.6) | copy-start | bytes 98308
  45.5 25.1 %copy-start = (bf16[6144,128]{1,0:T(8,128)(2,1)S(1)}, bf16[6144,128]{1,0:T(8,128)(2,1)}, u32[]{:S(2)}) copy-start(bf16[6144,128]{1,0:T(8,128)(2,1)} %pack.1.own_ref) | copy-start | bytes 4718596
  45.5 36.2 %collective-permute-start.5 = (bf16[6144,128]{1,0:T(8,128)(2,1)}, bf16[6144,128]{1,0:T(8,128)(2,1)}, u32[]{:S(2)}, u32[]{:S(2)}) collective-permute-start(bf16[6144,128]{1,0:T(8,128)(2,1)} %pack.1.own_ref), channel_id=1, source_target_pairs={{0,8},{1,3},{2,10},{3,1},{4,12},{5,7},{6,14},{7,5},{8,16},{9,11},{... | collective-permute-start | bytes 4718600 | tf_op jit(solution)/shard_map/ppermute | solution.py:42
  59.3 1.4 copy-start.1
  64.7 36.8 %copy-start.3 = (f32[1,2,2048]{2,1,0:T(2,128)S(1)}, f32[1,2,2048]{2,1,0:T(2,128)}, u32[]{:S(2)}) copy-start(f32[1,2,2048]{2,1,0:T(2,128)} %param.10) | copy-start | bytes 49156
  64.7 36.8 %copy-start.4 = (s32[2,1]{0,1:T(1,128)S(1)}, s32[2,1]{0,1:T(1,128)}, u32[]{:S(2)}) copy-start(s32[2,1]{0,1:T(1,128)} %param.11) | copy-start | bytes 28
  64.7 21.0 %all-to-all-start.1 = ((bf16[16,8,2048]{2,1,0:T(8,128)(2,1)}), bf16[16,8,2048]{2,1,0:T(8,128)(2,1)S(1)}, u32[]{:S(2)}, u32[]{:S(2)}) async-start(bf16[16,8,2048]{2,1,0:T(8,128)(2,1)} %ffn.2), calls=%async_computation.1 | async-start | bytes 1048576 | tf_op jit(solution)/shard_map/all_to_all | solution.py:46
  70.7 41.3 %collective-permute-start.4 = (bf16[6144,128]{1,0:T(8,128)(2,1)S(1)}, bf16[6144,128]{1,0:T(8,128)(2,1)}, u32[]{:S(2)}, u32[]{:S(2)}) collective-permute-start(bf16[6144,128]{1,0:T(8,128)(2,1)S(1)} %copy-done), channel_id=1, source_target_pairs={{0,1},{1,0},{2,3},{3,2},{4,5},{5,4},{6,7},{7,6},{8,9},{9,8},{10,11... | collective-permute-start | bytes 4718600 | tf_op jit(solution)/shard_map/ppermute | solution.py:36
  81.7 30.2 %collective-permute-start.6 = (bf16[6144,128]{1,0:T(8,128)(2,1)}, bf16[6144,128]{1,0:T(8,128)(2,1)}, u32[]{:S(2)}, u32[]{:S(2)}) collective-permute-start(bf16[6144,128]{1,0:T(8,128)(2,1)} %collective-permute-done.5.refs_1_), channel_id=1, source_target_pairs={{0,1},{1,0},{2,3},{3,2},{4,5},{5,4},{6,7},{7,6},{8,9},{9,8},{10,11... | collective-permute-start | bytes 4718600 | tf_op jit(solution)/shard_map/ppermute | solution.py:36
  85.8 15.7 %collective-permute-start.3 = (bf16[8,2048]{1,0:T(8,128)(2,1)S(1)}, bf16[8,2048]{1,0:T(8,128)(2,1)S(1)}, u32[]{:S(2)}, u32[]{:S(2)}) collective-permute-start(bf16[8,2048]{1,0:T(8,128)(2,1)S(1)} %advance.2), channel_id=1, source_target_pairs={{704,0},{0,64},{64,128},{128,192},{192,256},{256,320},{320,384},{3... | collective-permute-start | bytes 98312 | tf_op jit(solution)/shard_map/ppermute | solution.py:19
  103.0 25.6 %all-to-all-start.2 = ((bf16[16,8,2048]{2,1,0:T(8,128)(2,1)}), bf16[16,8,2048]{2,1,0:T(8,128)(2,1)S(1)}, u32[]{:S(2)}, u32[]{:S(2)}) async-start(bf16[16,8,2048]{2,1,0:T(8,128)(2,1)} %spread.1), calls=%async_computation.2 | async-start | bytes 1048576 | tf_op jit(solution)/shard_map/all_to_all | solution.py:46
  152.7 11.8 %collective-permute-start.7 = (bf16[8,2048]{1,0:T(8,128)(2,1)S(1)}, bf16[8,2048]{1,0:T(8,128)(2,1)S(1)}, u32[]{:S(2)}, u32[]{:S(2)}) collective-permute-start(bf16[8,2048]{1,0:T(8,128)(2,1)S(1)} %advance.3), channel_id=1, source_target_pairs={{704,0},{0,64},{64,128},{128,192},{192,256},{256,320},{320,384},{3... | collective-permute-start | bytes 98312 | tf_op jit(solution)/shard_map/ppermute | solution.py:19

commit v5 on v4

--- a/solution.py
+++ b/solution.py
@@ -36,9 +36,9 @@
     return lax.ppermute(value, axis, [(place, place ^ 1) for place in range(lax.axis_size(axis))])
 
 
-def to_other_colour(value, axis):
+def to_other_colour(value, axis, step):
     size = lax.axis_size(axis)
-    route = [(place, place ^ 2 if place & 1 else (place + 8) % size) for place in range(size)]
+    route = [(place, place ^ 2 if place & 1 else (place + 8 * step) % size) for place in range(size)]
     return lax.ppermute(value, axis, route)
 
 
@@ -260,7 +260,7 @@
         else:
             own = pack(tick, chosen, *weights)
             copies = spread(tick, chosen, current, norm_gain[0], members)
-        near = to_other_colour(own, "dp")
+        near = to_other_colour(own, "dp", 1 if tick else -1)
         tokens = exchange(copies, "dp", groups)
         own_pair = to_other_core(own, "dp")
         near_pair = to_other_core(near, "dp")

time: 166 us -> 165 us (level)
  no operation moved by 1% of the time
where the time goes in v5:
time: 165 us; the launch traced here: 164 us
  waiting for transfers between devices  67.6 us (41%)
  starting transfers between devices  57.7 us (35%)
  blocking collectives  20.4 us (12%)
  Pallas kernels  15.7 us (10%)
  local copies, waits for them, and re-layouts  2.04 us (1%)
    all_to_all x3, waiting for transfers between devices, exchange(): lax.all_to_all(blocks, axis, 0, 0, tiled=True, axis_index_groups=groups)  28.7 us
    all_to_all x3, starting transfers between devices, exchange(): lax.all_to_all(blocks, axis, 0, 0, tiled=True, axis_index_groups=groups)  27.7 us
    ppermute x2, waiting for transfers between devices, to_other_colour(): return lax.ppermute(value, axis, route)  26 us
    all_to_all x1, blocking collectives, exchange(): lax.all_to_all(blocks, axis, 0, 0, tiled=True, axis_index_groups=groups)  20.4 us
    ppermute x2, starting transfers between devices, passed_along(): return lax.ppermute(block, axis, route)  14.9 us
    ppermute x2, waiting for transfers between devices, passed_along(): return lax.ppermute(block, axis, route)  13 us
    ppermute x4, starting transfers between devices, to_other_core(): lax.ppermute(value, axis, [(place, place ^ 1) for place in range(lax.axis...  9.13 us
    pallas_call x2, Pallas kernels, feed_forward(): pl.pallas_call(feed_forward_kernel, out_shape=jax.ShapeDtypeStruct(tokens...  7.06 us
  transfers between devices with their start and end apart: 11, of which 7 were waited for; matrix products, arithmetic and copies ran while one was open for 0% of the time, Pallas kernels for 5%

profile of v5, /device:TPU:16, one launch (start us, length us, event | category | flops | bytes accessed | tf_op | source)
XLA Modules:
  0.0 163.7 jit_solution(10822637020255195654)
XLA Ops:
  0.0 3.7 %begin.1 = (bf16[6144,128]{1,0:T(8,128)(2,1)}, bf16[16,8,2048]{2,1,0:T(8,128)(2,1)}) custom-call(s32[2]{0:T(128)} %bitcast.11, bf16[8,2048]{1,0:T(8,128)(2,1)} %bitcast.7, f32[2,2048]{1,0:T(2,128)} %bitcast.9, bf16[2,2048,128]{2,1,0:T(8,128)(2,1)} %bitcast.14, bf16[2,2048,128]{2,1,0:T(8,128)(2,1)} %bitcast.16, bf16[2,128,2048]{2,1,0:T(8,128)(2,1)} %bitcast.18), custom_call_target="tpu_custom_call" | custom-call | flops 786432 | bytes 3145728 | tf_op jit(solution)/shard_map/begin/pallas_call | solution.py:147
  3.7 2.4 %collective-permute-start.1 = (bf16[6144,128]{1,0:T(8,128)(2,1)}, bf16[6144,128]{1,0:T(8,128)(2,1)}, u32[]{:S(2)}, u32[]{:S(2)}) collective-permute-start(bf16[6144,128]{1,0:T(8,128)(2,1)} %get-tuple-element.8.own_ref), channel_id=1, source_target_pairs={{0,56},{1,3},{2,58},{3,1},{4,60},{5,7},{6,62},{7,5},{8,0},{9,11},{... | collective-permute-start | bytes 4718600 | tf_op jit(solution)/shard_map/ppermute | solution.py:42
  6.0 3.4 %collective-permute-start = (bf16[6144,128]{1,0:T(8,128)(2,1)}, bf16[6144,128]{1,0:T(8,128)(2,1)}, u32[]{:S(2)}, u32[]{:S(2)}) collective-permute-start(bf16[6144,128]{1,0:T(8,128)(2,1)} %get-tuple-element.8.own_ref), channel_id=1, source_target_pairs={{0,1},{1,0},{2,3},{3,2},{4,5},{5,4},{6,7},{7,6},{8,9},{9,8},{10,11... | collective-permute-start | bytes 4718600 | tf_op jit(solution)/shard_map/ppermute | solution.py:36
  9.4 16.9 %collective-permute-done.1.refs_1_ = bf16[6144,128]{1,0:T(8,128)(2,1)} collective-permute-done((bf16[6144,128]{1,0:T(8,128)(2,1)}, bf16[6144,128]{1,0:T(8,128)(2,1)}, u32[]{:S(2)}, u32[]{:S(2)}) %collective-permute-start.1) | collective-permute-done | bytes 1572896 | tf_op jit(solution)/shard_map/ppermute | solution.py:42
  26.3 1.9 %collective-permute-start.2 = (bf16[6144,128]{1,0:T(8,128)(2,1)}, bf16[6144,128]{1,0:T(8,128)(2,1)}, u32[]{:S(2)}, u32[]{:S(2)}) collective-permute-start(bf16[6144,128]{1,0:T(8,128)(2,1)} %collective-permute-done.1.refs_1_), channel_id=1, source_target_pairs={{0,1},{1,0},{2,3},{3,2},{4,5},{5,4},{6,7},{7,6},{8,9},{9,8},{10,11... | collective-permute-start | bytes 4718600 | tf_op jit(solution)/shard_map/ppermute | solution.py:36
  28.2 12.7 %all-to-all-start = ((bf16[16,8,2048]{2,1,0:T(8,128)(2,1)}), bf16[16,8,2048]{2,1,0:T(8,128)(2,1)S(1)}, u32[]{:S(2)}, u32[]{:S(2)}) async-start(bf16[16,8,2048]{2,1,0:T(8,128)(2,1)} %get-tuple-element.7), calls=%async_computation | async-start | bytes 1048576 | tf_op jit(solution)/shard_map/all_to_all | solution.py:46
  40.9 0.0 copy-start.2
  40.9 3.4 %pack.1.own_ref = bf16[6144,128]{1,0:T(8,128)(2,1)} custom-call(s32[2]{0:T(128)} %bitcast.12, bf16[2,2048,128]{2,1,0:T(8,128)(2,1)} %bitcast.15, bf16[2,2048,128]{2,1,0:T(8,128)(2,1)} %bitcast.17, bf16[2,128,2048]{2,1,0:T(8,128)(2,1)} %bitcast.19), custom_call_target="tpu_custom_call" | custom-call | flops 786432 | bytes 3145728 | tf_op jit(solution)/shard_map/pack/pallas_call | solution.py:112
  44.3 0.0 copy-start
  44.3 3.7 %collective-permute-start.5 = (bf16[6144,128]{1,0:T(8,128)(2,1)}, bf16[6144,128]{1,0:T(8,128)(2,1)}, u32[]{:S(2)}, u32[]{:S(2)}) collective-permute-start(bf16[6144,128]{1,0:T(8,128)(2,1)} %pack.1.own_ref), channel_id=1, source_target_pairs={{0,8},{1,3},{2,10},{3,1},{4,12},{5,7},{6,14},{7,5},{8,16},{9,11},{... | collective-permute-start | bytes 4718600 | tf_op jit(solution)/shard_map/ppermute | solution.py:42
  48.0 10.0 %all-to-all-done.tokens_ref = bf16[16,8,2048]{2,1,0:T(8,128)(2,1)S(1)} async-done(((bf16[16,8,2048]{2,1,0:T(8,128)(2,1)}), bf16[16,8,2048]{2,1,0:T(8,128)(2,1)S(1)}, u32[]{:S(2)}, u32[]{:S(2)}) %all-to-all-start) | async-done | bytes 524320 | tf_op jit(solution)/shard_map/all_to_all | solution.py:46
  58.0 0.0 collective-permute-done.refs_0_
  58.1 0.0 collective-permute-done.2.refs_2_
  58.1 0.0 copy-start.1
  58.1 1.4 copy-done.1
  59.5 4.0 %ffn.2 = bf16[16,8,2048]{2,1,0:T(8,128)(2,1)} custom-call(bf16[16,8,2048]{2,1,0:T(8,128)(2,1)S(1)} %all-to-all-done.tokens_ref, bf16[6144,128]{1,0:T(8,128)(2,1)S(1)} %copy-done.1, bf16[6144,128]{1,0:T(8,128)(2,1)} %collective-permute-done.refs_0_, bf16[6144,128]{1,0:T(8,128)(2,1)} %collective-permute-done.1.refs_1_, ...), custom_call_target="tpu_custom_call" | custom-call | flops 805306368 | bytes 6291456 | tf_op jit(solution)/shard_map/ffn/pallas_call | solution.py:212
  63.5 0.0 copy-start.3
  63.5 0.0 copy-start.4
  63.5 5.9 %all-to-all-start.1 = ((bf16[16,8,2048]{2,1,0:T(8,128)(2,1)}), bf16[16,8,2048]{2,1,0:T(8,128)(2,1)S(1)}, u32[]{:S(2)}, u32[]{:S(2)}) async-start(bf16[16,8,2048]{2,1,0:T(8,128)(2,1)} %ffn.2), calls=%async_computation.1 | async-start | bytes 1048576 | tf_op jit(solution)/shard_map/all_to_all | solution.py:46
  69.4 0.0 copy-done
  69.5 1.9 %collective-permute-start.4 = (bf16[6144,128]{1,0:T(8,128)(2,1)S(1)}, bf16[6144,128]{1,0:T(8,128)(2,1)}, u32[]{:S(2)}, u32[]{:S(2)}) collective-permute-start(bf16[6144,128]{1,0:T(8,128)(2,1)S(1)} %copy-done), channel_id=1, source_target_pairs={{0,1},{1,0},{2,3},{3,2},{4,5},{5,4},{6,7},{7,6},{8,9},{9,8},{10,11... | collective-permute-start | bytes 4718600 | tf_op jit(solution)/shard_map/ppermute | solution.py:36
  71.4 9.1 %collective-permute-done.5.refs_1_ = bf16[6144,128]{1,0:T(8,128)(2,1)} collective-permute-done((bf16[6144,128]{1,0:T(8,128)(2,1)}, bf16[6144,128]{1,0:T(8,128)(2,1)}, u32[]{:S(2)}, u32[]{:S(2)}) %collective-permute-start.5) | collective-permute-done | bytes 1572896 | tf_op jit(solution)/shard_map/ppermute | solution.py:42
  80.5 1.9 %collective-permute-start.6 = (bf16[6144,128]{1,0:T(8,128)(2,1)}, bf16[6144,128]{1,0:T(8,128)(2,1)}, u32[]{:S(2)}, u32[]{:S(2)}) collective-permute-start(bf16[6144,128]{1,0:T(8,128)(2,1)} %collective-permute-done.5.refs_1_), channel_id=1, source_target_pairs={{0,1},{1,0},{2,3},{3,2},{4,5},{5,4},{6,7},{7,6},{8,9},{9,8},{10,11... | collective-permute-start | bytes 4718600 | tf_op jit(solution)/shard_map/ppermute | solution.py:36
  82.4 2.1 %all-to-all-done.1.parts_ref = bf16[16,8,2048]{2,1,0:T(8,128)(2,1)S(1)} async-done(((bf16[16,8,2048]{2,1,0:T(8,128)(2,1)}), bf16[16,8,2048]{2,1,0:T(8,128)(2,1)S(1)}, u32[]{:S(2)}, u32[]{:S(2)}) %all-to-all-start.1) | async-done | bytes 524320 | tf_op jit(solution)/shard_map/all_to_all | solution.py:46
  84.5 0.0 copy-done.2
  84.5 0.1 advance.2
  84.6 10.3 %collective-permute-start.3 = (bf16[8,2048]{1,0:T(8,128)(2,1)S(1)}, bf16[8,2048]{1,0:T(8,128)(2,1)S(1)}, u32[]{:S(2)}, u32[]{:S(2)}) collective-permute-start(bf16[8,2048]{1,0:T(8,128)(2,1)S(1)} %advance.2), channel_id=1, source_target_pairs={{704,0},{0,64},{64,128},{128,192},{192,256},{256,320},{320,384},{3... | collective-permute-start | bytes 98312 | tf_op jit(solution)/shard_map/ppermute | solution.py:19
  94.9 5.4 %collective-permute-done.3.refs_1_.rows_ref = bf16[8,2048]{1,0:T(8,128)(2,1)S(1)} collective-permute-done((bf16[8,2048]{1,0:T(8,128)(2,1)S(1)}, bf16[8,2048]{1,0:T(8,128)(2,1)S(1)}, u32[]{:S(2)}, u32[]{:S(2)}) %collective-permute-start.3) | collective-permute-done | bytes 32800 | tf_op jit(solution)/shard_map/ppermute | solution.py:19
  100.3 0.0 copy-done.3
  100.3 0.0 copy-done.4
  100.3 1.5 spread.1
  101.8 9.0 %all-to-all-start.2 = ((bf16[16,8,2048]{2,1,0:T(8,128)(2,1)}), bf16[16,8,2048]{2,1,0:T(8,128)(2,1)S(1)}, u32[]{:S(2)}, u32[]{:S(2)}) async-start(bf16[16,8,2048]{2,1,0:T(8,128)(2,1)} %spread.1), calls=%async_computation.2 | async-start | bytes 1048576 | tf_op jit(solution)/shard_map/all_to_all | solution.py:46
  110.8 0.0 collective-permute-done.4.refs_0_
  110.8 0.0 collective-permute-done.6.refs_2_
  110.9 16.5 %all-to-all-done.2.tokens_ref = bf16[16,8,2048]{2,1,0:T(8,128)(2,1)S(1)} async-done(((bf16[16,8,2048]{2,1,0:T(8,128)(2,1)}), bf16[16,8,2048]{2,1,0:T(8,128)(2,1)S(1)}, u32[]{:S(2)}, u32[]{:S(2)}) %all-to-all-start.2) | async-done | bytes 524320 | tf_op jit(solution)/shard_map/all_to_all | solution.py:46
  127.3 3.0 %ffn.3 = bf16[16,8,2048]{2,1,0:T(8,128)(2,1)S(1)} custom-call(bf16[16,8,2048]{2,1,0:T(8,128)(2,1)S(1)} %all-to-all-done.2.tokens_ref, bf16[6144,128]{1,0:T(8,128)(2,1)S(1)} %copy-done, bf16[6144,128]{1,0:T(8,128)(2,1)} %collective-permute-done.4.refs_0_, bf16[6144,128]{1,0:T(8,128)(2,1)} %collective-permute-done.5.refs_1_, ...), custom_call_target="tpu_custom_call" | custom-call | flops 805306368 | bytes 6291456 | tf_op jit(solution)/shard_map/ffn/pallas_call | solution.py:212
  130.4 20.4 %all_to_all.20.parts_ref = bf16[16,8,2048]{2,1,0:T(8,128)(2,1)S(1)} all-to-all(bf16[16,8,2048]{2,1,0:T(8,128)(2,1)S(1)} %ffn.3), channel_id=1, replica_groups={{0,4,10,14,16,20,26,30,32,36,42,46,48,52,58,62},{2,6,8,12,18,22,24,28,3..., dimensions={0} | all-to-all | bytes 1048576 | tf_op jit(solution)/shard_map/all_to_all | solution.py:46
  150.8 0.1 advance.3
  150.9 4.6 %collective-permute-start.7 = (bf16[8,2048]{1,0:T(8,128)(2,1)S(1)}, bf16[8,2048]{1,0:T(8,128)(2,1)S(1)}, u32[]{:S(2)}, u32[]{:S(2)}) collective-permute-start(bf16[8,2048]{1,0:T(8,128)(2,1)S(1)} %advance.3), channel_id=1, source_target_pairs={{704,0},{0,64},{64,128},{128,192},{192,256},{256,320},{320,384},{3... | collective-permute-start | bytes 98312 | tf_op jit(solution)/shard_map/ppermute | solution.py:19
  155.5 7.6 %collective-permute-done.7 = bf16[8,2048]{1,0:T(8,128)(2,1)S(1)} collective-permute-done((bf16[8,2048]{1,0:T(8,128)(2,1)S(1)}, bf16[8,2048]{1,0:T(8,128)(2,1)S(1)}, u32[]{:S(2)}, u32[]{:S(2)}) %collective-permute-start.7) | collective-permute-done | bytes 32800 | tf_op jit(solution)/shard_map/ppermute | solution.py:19
  163.1 0.6 copy.8
Async XLA Ops:
  3.7 22.6 %collective-permute-start.1 = (bf16[6144,128]{1,0:T(8,128)(2,1)}, bf16[6144,128]{1,0:T(8,128)(2,1)}, u32[]{:S(2)}, u32[]{:S(2)}) collective-permute-start(bf16[6144,128]{1,0:T(8,128)(2,1)} %get-tuple-element.8.own_ref), channel_id=1, source_target_pairs={{0,56},{1,3},{2,58},{3,1},{4,60},{5,7},{6,62},{7,5},{8,0},{9,11},{... | collective-permute-start | bytes 4718600 | tf_op jit(solution)/shard_map/ppermute | solution.py:42
  6.0 52.0 %collective-permute-start = (bf16[6144,128]{1,0:T(8,128)(2,1)}, bf16[6144,128]{1,0:T(8,128)(2,1)}, u32[]{:S(2)}, u32[]{:S(2)}) collective-permute-start(bf16[6144,128]{1,0:T(8,128)(2,1)} %get-tuple-element.8.own_ref), channel_id=1, source_target_pairs={{0,1},{1,0},{2,3},{3,2},{4,5},{5,4},{6,7},{7,6},{8,9},{9,8},{10,11... | collective-permute-start | bytes 4718600 | tf_op jit(solution)/shard_map/ppermute | solution.py:36
  26.3 31.7 %collective-permute-start.2 = (bf16[6144,128]{1,0:T(8,128)(2,1)}, bf16[6144,128]{1,0:T(8,128)(2,1)}, u32[]{:S(2)}, u32[]{:S(2)}) collective-permute-start(bf16[6144,128]{1,0:T(8,128)(2,1)} %collective-permute-done.1.refs_1_), channel_id=1, source_target_pairs={{0,1},{1,0},{2,3},{3,2},{4,5},{5,4},{6,7},{7,6},{8,9},{9,8},{10,11... | collective-permute-start | bytes 4718600 | tf_op jit(solution)/shard_map/ppermute | solution.py:36
  28.2 29.8 %all-to-all-start = ((bf16[16,8,2048]{2,1,0:T(8,128)(2,1)}), bf16[16,8,2048]{2,1,0:T(8,128)(2,1)S(1)}, u32[]{:S(2)}, u32[]{:S(2)}) async-start(bf16[16,8,2048]{2,1,0:T(8,128)(2,1)} %get-tuple-element.7), calls=%async_computation | async-start | bytes 1048576 | tf_op jit(solution)/shard_map/all_to_all | solution.py:46
  40.9 43.6 %copy-start.2 = (bf16[1,8,2048]{2,1,0:T(8,128)(2,1)S(1)}, bf16[1,8,2048]{2,1,0:T(8,128)(2,1)}, u32[]{:S(2)}) copy-start(bf16[1,8,2048]{2,1,0:T(8,128)(2,1)} %param.6) | copy-start | bytes 98308
  44.3 25.1 %copy-start = (bf16[6144,128]{1,0:T(8,128)(2,1)S(1)}, bf16[6144,128]{1,0:T(8,128)(2,1)}, u32[]{:S(2)}) copy-start(bf16[6144,128]{1,0:T(8,128)(2,1)} %pack.1.own_ref) | copy-start | bytes 4718596
  44.3 36.2 %collective-permute-start.5 = (bf16[6144,128]{1,0:T(8,128)(2,1)}, bf16[6144,128]{1,0:T(8,128)(2,1)}, u32[]{:S(2)}, u32[]{:S(2)}) collective-permute-start(bf16[6144,128]{1,0:T(8,128)(2,1)} %pack.1.own_ref), channel_id=1, source_target_pairs={{0,8},{1,3},{2,10},{3,1},{4,12},{5,7},{6,14},{7,5},{8,16},{9,11},{... | collective-permute-start | bytes 4718600 | tf_op jit(solution)/shard_map/ppermute | solution.py:42
  58.1 1.4 copy-start.1
  63.5 36.8 %copy-start.3 = (f32[1,2,2048]{2,1,0:T(2,128)S(1)}, f32[1,2,2048]{2,1,0:T(2,128)}, u32[]{:S(2)}) copy-start(f32[1,2,2048]{2,1,0:T(2,128)} %param.10) | copy-start | bytes 49156
  63.5 36.8 %copy-start.4 = (s32[2,1]{0,1:T(1,128)S(1)}, s32[2,1]{0,1:T(1,128)}, u32[]{:S(2)}) copy-start(s32[2,1]{0,1:T(1,128)} %param.11) | copy-start | bytes 28
  63.5 21.0 %all-to-all-start.1 = ((bf16[16,8,2048]{2,1,0:T(8,128)(2,1)}), bf16[16,8,2048]{2,1,0:T(8,128)(2,1)S(1)}, u32[]{:S(2)}, u32[]{:S(2)}) async-start(bf16[16,8,2048]{2,1,0:T(8,128)(2,1)} %ffn.2), calls=%async_computation.1 | async-start | bytes 1048576 | tf_op jit(solution)/shard_map/all_to_all | solution.py:46
  69.5 41.4 %collective-permute-start.4 = (bf16[6144,128]{1,0:T(8,128)(2,1)S(1)}, bf16[6144,128]{1,0:T(8,128)(2,1)}, u32[]{:S(2)}, u32[]{:S(2)}) collective-permute-start(bf16[6144,128]{1,0:T(8,128)(2,1)S(1)} %copy-done), channel_id=1, source_target_pairs={{0,1},{1,0},{2,3},{3,2},{4,5},{5,4},{6,7},{7,6},{8,9},{9,8},{10,11... | collective-permute-start | bytes 4718600 | tf_op jit(solution)/shard_map/ppermute | solution.py:36
  80.5 30.4 %collective-permute-start.6 = (bf16[6144,128]{1,0:T(8,128)(2,1)}, bf16[6144,128]{1,0:T(8,128)(2,1)}, u32[]{:S(2)}, u32[]{:S(2)}) collective-permute-start(bf16[6144,128]{1,0:T(8,128)(2,1)} %collective-permute-done.5.refs_1_), channel_id=1, source_target_pairs={{0,1},{1,0},{2,3},{3,2},{4,5},{5,4},{6,7},{7,6},{8,9},{9,8},{10,11... | collective-permute-start | bytes 4718600 | tf_op jit(solution)/shard_map/ppermute | solution.py:36
  84.6 15.7 %collective-permute-start.3 = (bf16[8,2048]{1,0:T(8,128)(2,1)S(1)}, bf16[8,2048]{1,0:T(8,128)(2,1)S(1)}, u32[]{:S(2)}, u32[]{:S(2)}) collective-permute-start(bf16[8,2048]{1,0:T(8,128)(2,1)S(1)} %advance.2), channel_id=1, source_target_pairs={{704,0},{0,64},{64,128},{128,192},{192,256},{256,320},{320,384},{3... | collective-permute-start | bytes 98312 | tf_op jit(solution)/shard_map/ppermute | solution.py:19
  101.8 25.5 %all-to-all-start.2 = ((bf16[16,8,2048]{2,1,0:T(8,128)(2,1)}), bf16[16,8,2048]{2,1,0:T(8,128)(2,1)S(1)}, u32[]{:S(2)}, u32[]{:S(2)}) async-start(bf16[16,8,2048]{2,1,0:T(8,128)(2,1)} %spread.1), calls=%async_computation.2 | async-start | bytes 1048576 | tf_op jit(solution)/shard_map/all_to_all | solution.py:46
  150.9 12.2 %collective-permute-start.7 = (bf16[8,2048]{1,0:T(8,128)(2,1)S(1)}, bf16[8,2048]{1,0:T(8,128)(2,1)S(1)}, u32[]{:S(2)}, u32[]{:S(2)}) collective-permute-start(bf16[8,2048]{1,0:T(8,128)(2,1)S(1)} %advance.3), channel_id=1, source_target_pairs={{704,0},{0,64},{64,128},{128,192},{192,256},{256,320},{320,384},{3... | collective-permute-start | bytes 98312 | tf_op jit(solution)/shard_map/ppermute | solution.py:19

commit v6 on v5

v6 whole, which is shorter than its diff:
```python
import jax
import jax.numpy as jnp
from jax import lax
from jax.experimental import pallas as pl
from jax.experimental.pallas import tpu as pltpu
from jax.sharding import PartitionSpec as P


TICKS = 2
INTERPRET = False


epsilon = 0.5


def passed_along(block, axis, distance):
    devices = range(lax.axis_size(axis))
    route = [((i - distance) % len(devices), i) for i in devices]
    return lax.ppermute(block, axis, route)


def colour(place):
    return (place >> 1 ^ place >> 3) & 1


def same_kind(axis):
    size = lax.axis_size(axis)
    return [
        [place for place in range(size) if place & 1 == core and colour(place) == shade]
        for core in range(2)
        for shade in range(2)
    ]


def to_other_core(value, axis):
    return lax.ppermute(value, axis, [(place, place ^ 1) for place in range(lax.axis_size(axis))])


def to_other_colour(value, axis, step):
    size = lax.axis_size(axis)
    route = [(place, place ^ 2 if place & 1 else (place + 8 * step) % size) for place in range(size)]
    return lax.ppermute(value, axis, route)


def exchange(blocks, axis, groups):
    return lax.all_to_all(blocks, axis, 0, 0, tiled=True, axis_index_groups=groups)


def room(mebibytes):
    return pltpu.CompilerParams(vmem_limit_bytes=mebibytes << 20)


def spread_kernel(tick, chosen_ref, rows_ref, gain_ref, copies_ref):
    widened = rows_ref[...].astype(jnp.float32)
    squares = jnp.mean(widened * widened, axis=-1, keepdims=True)
    gain_row = gain_ref[pl.ds(chosen_ref[tick], 1), :]
    normed = (widened * lax.rsqrt(squares + epsilon) * gain_row).astype(copies_ref.dtype)
    for member in range(copies_ref.shape[0]):
        copies_ref[member] = normed


def spread(tick, repeat_index, rows, gains, members):
    count, width = rows.shape
    return pl.pallas_call(
        lambda *refs: spread_kernel(tick, *refs),
        out_shape=jax.ShapeDtypeStruct((members, count, width), rows.dtype),
        in_specs=[
            pl.BlockSpec(memory_space=pltpu.SMEM),
            pl.BlockSpec(memory_space=pltpu.VMEM),
            pl.BlockSpec(memory_space=pltpu.VMEM),
        ],
        out_specs=pl.BlockSpec(memory_space=pltpu.VMEM),
        cost_estimate=pl.CostEstimate(flops=8 * count * width, bytes_accessed=2 * members * count * width, transcendentals=8),
        compiler_params=room(4),
        name="spread",
        interpret=INTERPRET,
    )(repeat_index, rows, gains)


def slab_loads(chosen, sources, slabs, arrived):
    return [
        pltpu.make_async_copy(source.at[chosen], slab, arrived.at[index])
        for index, (source, slab) in enumerate(zip(sources, slabs))
    ]


def store_halves(gate_ref, up_ref, down_ref, half_refs):
    width, lanes = gate_ref.shape
    units = lanes // 2
    gate_value = gate_ref[...].astype(jnp.float32)
    up_value = up_ref[...].astype(jnp.float32)
    first = lax.broadcasted_iota(jnp.int32, (width, lanes), 1) < units
    mixed = (
        jnp.where(first, gate_value, pltpu.roll(up_value, units, 1)),
        jnp.where(first, pltpu.roll(gate_value, units, 1), up_value),
    )
    for half, half_ref in enumerate(half_refs):
        half_ref[0:width] = mixed[half].astype(half_ref.dtype)
        for column in range(width // lanes):
            start = width + column * units
            half_ref[start : start + units] = down_ref[
                half * units : (half + 1) * units, column * lanes : (column + 1) * lanes
            ]


def pack_kernel(tick, chosen_ref, gate_hbm, up_hbm, down_hbm, packed_ref, *scratch):
    slabs, arrived = scratch[:-1], scratch[-1]
    loads = slab_loads(chosen_ref[tick], (gate_hbm, up_hbm, down_hbm), slabs, arrived)
    for load in loads:
        load.start()
    for load in loads:
        load.wait()
    store_halves(*slabs, halves_in(packed_ref, slabs[0].shape[0]))


def halves_in(ref, width):
    size = width + width // 2
    return [ref.at[start : start + size] for start in range(0, ref.shape[0], size)]


IN_HBM = pl.BlockSpec(memory_space=pltpu.HBM)
IN_VMEM = pl.BlockSpec(memory_space=pltpu.VMEM)
IN_SMEM = pl.BlockSpec(memory_space=pltpu.SMEM)


def halves_of(weight):
    _, width, lanes = weight.shape
    half = jax.ShapeDtypeStruct((width + width // 2, lanes), weight.dtype)
    return half, half


def slabs_of(*weights):
    return [pltpu.VMEM(weight.shape[1:], weight.dtype) for weight in weights]


def pack(tick, chosen, *weights):
    size = weights[0].shape[1] * weights[0].shape[2]
    return pl.pallas_call(
        lambda *refs: pack_kernel(tick, *refs),
        out_shape=jax.ShapeDtypeStruct((3 * weights[0].shape[1], weights[0].shape[2]), weights[0].dtype),
        in_specs=[IN_SMEM, IN_HBM, IN_HBM, IN_HBM],
        out_specs=IN_VMEM,
        scratch_shapes=slabs_of(*weights) + [pltpu.SemaphoreType.DMA((3,))],
        cost_estimate=pl.CostEstimate(flops=6 * size, bytes_accessed=12 * size, transcendentals=0),
        compiler_params=room(60),
        name="pack",
        interpret=INTERPRET,
    )(chosen, *weights)


def begin_kernel(
    chosen_ref, rows_hbm, gain_hbm, gate_hbm, up_hbm, down_hbm, first_ref, second_ref, copies_ref, *scratch
):
    slabs, (rows_ref, gain_ref, arrived, loaded) = scratch[:3], scratch[3:]
    early = [
        pltpu.make_async_copy(rows_hbm, rows_ref, loaded.at[0]),
        pltpu.make_async_copy(gain_hbm, gain_ref, loaded.at[1]),
    ]
    for load in early:
        load.start()
    loads = slab_loads(chosen_ref[0], (gate_hbm, up_hbm, down_hbm), slabs, arrived)
    for load in loads:
        load.start()
    for load in early:
        load.wait()
    spread_kernel(0, chosen_ref, rows_ref, gain_ref, copies_ref)
    for load in loads:
        load.wait()
    store_halves(*slabs, (first_ref, second_ref))


def begin(chosen, rows, gains, weights, members):
    size = weights[0].shape[1] * weights[0].shape[2]
    return pl.pallas_call(
        begin_kernel,
        out_shape=(*halves_of(weights[0]), jax.ShapeDtypeStruct((members, *rows.shape), rows.dtype)),
        in_specs=[IN_SMEM] + [IN_HBM] * 5,
        out_specs=(IN_VMEM,) * 3,
        scratch_shapes=slabs_of(*weights)
        + [
            pltpu.VMEM(rows.shape, rows.dtype),
            pltpu.VMEM(gains.shape, gains.dtype),
            pltpu.SemaphoreType.DMA((3,)),
            pltpu.SemaphoreType.DMA((2,)),
        ],
        cost_estimate=pl.CostEstimate(flops=6 * size, bytes_accessed=12 * size, transcendentals=8),
        compiler_params=room(60),
        name="begin",
        interpret=INTERPRET,
    )(chosen, rows, gains, *weights)


def feed_forward_kernel(owned, tokens_ref, *refs):
    own, refs = refs[:owned], refs[owned:]
    count = (len(refs) - 2) // 2
    sources, out_ref, held, arrived = refs[:count], refs[count], refs[count + 1 : -1], refs[-1]
    members, rows, width = tokens_ref.shape

    def split(refs):
        return [half for ref in refs for half in halves_in(ref, width)]

    parts = ((0, width), (width, width + width // 2))
    copies = [
        [
            pltpu.make_async_copy(source.at[start:end], slot.at[start:end], arrived.at[part, index])
            for index, (source, slot) in enumerate(zip(split(sources), split(held)))
        ]
        for part, (start, end) in enumerate(parts)
    ]
    for part in copies:
        for copy in part:
            copy.start()
    tokens = tokens_ref[...].reshape(members * rows, width)
    halves = split(own) + split(held)
    lanes = own[0].shape[1]
    units = lanes // 2
    first = lax.broadcasted_iota(jnp.int32, (members * rows, lanes), 1) < units
    hidden = []
    for index in range(0, len(halves), 2):
        if index:
            copies[0][index - 2].wait()
            copies[0][index - 1].wait()
        both = jnp.concatenate([halves[index][0:width], halves[index + 1][0:width]], axis=1)
        value = jnp.dot(tokens, both, preferred_element_type=jnp.float32)
        left, right = value[:, :lanes], value[:, lanes:]
        gate_value = jnp.where(first, left, pltpu.roll(right, units, 1))
        up_value = jnp.where(first, pltpu.roll(left, units, 1), right)
        hidden.append((gate_value / (1.0 + jnp.exp(-gate_value)) * up_value).astype(tokens.dtype))
    hidden = jnp.concatenate(hidden, axis=1)
    for copy in copies[1]:
        copy.wait()
    for column in range(0, width // lanes, 2):
        slabs = []
        for step in range(2):
            start = width + (column + step) * units
            slabs.append(jnp.concatenate([half[start : start + units] for half in halves], axis=0))
        value = jnp.dot(hidden, jnp.concatenate(slabs, axis=1), preferred_element_type=jnp.float32)
        out_ref[:, :, column * lanes : (column + 2) * lanes] = value.astype(out_ref.dtype).reshape(
            members, rows, 2 * lanes
        )


def feed_forward(tokens, own, others):
    members, rows, width = tokens.shape
    lanes = own[0].shape[1]
    halves = 8
    return pl.pallas_call(
        lambda *refs: feed_forward_kernel(len(own), *refs),
        out_shape=jax.ShapeDtypeStruct(tokens.shape, tokens.dtype),
        in_specs=[IN_VMEM] * (1 + len(own)) + [IN_HBM] * len(others),
        out_specs=IN_VMEM,
        scratch_shapes=[pltpu.VMEM(other.shape, other.dtype) for other in others]
        + [pltpu.SemaphoreType.DMA((2, halves - 2))],
        cost_estimate=pl.CostEstimate(
            flops=3 * members * rows * width * lanes * halves,
            bytes_accessed=3 * width * lanes * halves,
            transcendentals=members * rows * lanes * halves // 2,
        ),
        compiler_params=room(8),
        name="ffn",
        interpret=INTERPRET,
    )(tokens, *own, *others)


def advance_kernel(parts_ref, rows_ref, out_ref):
    total = rows_ref[...].astype(jnp.float32)
    output = parts_ref[0].astype(jnp.float32)
    for member in range(1, parts_ref.shape[0]):
        output = output + parts_ref[member].astype(jnp.float32)
    out_ref[...] = (total + output).astype(out_ref.dtype)


def advance(parts, rows):
    return pl.pallas_call(
        advance_kernel,
        out_shape=jax.ShapeDtypeStruct(rows.shape, rows.dtype),
        in_specs=[pl.BlockSpec(memory_space=pltpu.VMEM)] * 2,
        out_specs=pl.BlockSpec(memory_space=pltpu.VMEM),
        cost_estimate=pl.CostEstimate(flops=parts.size, bytes_accessed=2 * parts.size, transcendentals=0),
        compiler_params=room(4),
        name="advance",
        interpret=INTERPRET,
    )(parts, rows)


def on_device(buffer, gate_weight, up_weight, down_weight, norm_gain, repeat_index):
    current = buffer[0]
    chosen = repeat_index.reshape(TICKS)
    weights = (gate_weight[0], up_weight[0], down_weight[0])
    groups = same_kind("dp")
    members = len(groups[0])
    for tick in range(TICKS):
        if tick == 0:
            *own, copies = begin(chosen, current, norm_gain[0], weights, members)
        else:
            own = [pack(tick, chosen, *weights)]
            copies = spread(tick, chosen, current, norm_gain[0], members)
        near, pair, far = [], [], []
        for index, packed in enumerate(own):
            near.append(to_other_colour(packed, "dp", 1 if tick or index else -1))
            pair.append(to_other_core(packed, "dp"))
            far.append(to_other_core(near[-1], "dp"))
        tokens = exchange(copies, "dp", groups)
        partial_value = feed_forward(tokens, own, (*pair, *near, *far))
        parts = exchange(partial_value, "dp", groups)
        advanced = advance(parts, current)
        current = passed_along(advanced, "section", 1)
    return current[None]


def solution(mesh):
    placed = (
        P("section", "dp", None),
        P("section", None, None, "dp"),
        P("section", None, None, "dp"),
        P("section", None, "dp", None),
        P("section", None, None),
        P(None, "section"),
    )
    return jax.shard_map(
        on_device, mesh=mesh, in_specs=placed, out_specs=P("section", "dp", None), check_vma=False
    )
```

time: 165 us -> 160 us (0.970)
  the two profiles are of different devices: /device:TPU:16 before, /device:TPU:56 now
where the time goes in v6:
time: 160 us; the launch traced here: 157 us
  waiting for transfers between devices  59 us (37%)
  starting transfers between devices  57.6 us (36%)
  blocking collectives  21 us (13%)
  Pallas kernels  17.2 us (11%)
  local copies, waits for them, and re-layouts  1.77 us (1%)
    ppermute x3, waiting for transfers between devices, to_other_colour(): return lax.ppermute(value, axis, route)  24.8 us
    all_to_all x3, starting transfers between devices, exchange(): lax.all_to_all(blocks, axis, 0, 0, tiled=True, axis_index_groups=groups)  23.3 us
    all_to_all x1, blocking collectives, exchange(): lax.all_to_all(blocks, axis, 0, 0, tiled=True, axis_index_groups=groups)  21 us
    ppermute x2, waiting for transfers between devices, passed_along(): return lax.ppermute(block, axis, route)  19.8 us
    ppermute x3, starting transfers between devices, to_other_colour(): return lax.ppermute(value, axis, route)  18.3 us
    all_to_all x3, waiting for transfers between devices, exchange(): lax.all_to_all(blocks, axis, 0, 0, tiled=True, axis_index_groups=groups)  14.3 us
    ppermute x6, starting transfers between devices, to_other_core(): lax.ppermute(value, axis, [(place, place ^ 1) for place in range(lax.axis...  12.1 us
    pallas_call x2, Pallas kernels, feed_forward(): pl.pallas_call(lambda *refs: feed_forward_kernel(len(own), *refs), out_sh...  7.97 us
  transfers between devices with their start and end apart: 14, of which 6 were waited for; matrix products, arithmetic and copies ran while one was open for 0% of the time, Pallas kernels for 6%

profile of v6, /device:TPU:56, one launch (start us, length us, event | category | flops | bytes accessed | tf_op | source)
XLA Modules:
  0.0 156.7 jit_solution(4525385995497528527)
XLA Ops:
  0.0 3.9 %begin.1 = (bf16[3072,128]{1,0:T(8,128)(2,1)}, bf16[3072,128]{1,0:T(8,128)(2,1)}, bf16[16,8,2048]{2,1,0:T(8,128)(2,1)}) custom-call(s32[2]{0:T(128)} %bitcast.11, bf16[8,2048]{1,0:T(8,128)(2,1)} %bitcast.7, f32[2,2048]{1,0:T(2,128)} %bitcast.9, bf16[2,2048,128]{2,1,0:T(8,128)(2,1)} %bitcast.14, bf16[2,2048,128]{2,1,0:T(8,128)(2,1)} %bitcast.16, ...), custom_call_target="tpu_custom_call" | custom-call | flops 1572864 | bytes 3145728 | tf_op jit(solution)/shard_map/begin/pallas_call | solution.py:174
  3.9 3.3 %collective-permute-start.2 = (bf16[3072,128]{1,0:T(8,128)(2,1)}, bf16[3072,128]{1,0:T(8,128)(2,1)}, u32[]{:S(2)}, u32[]{:S(2)}) collective-permute-start(bf16[3072,128]{1,0:T(8,128)(2,1)} %get-tuple-element.9.refs_1_), channel_id=1, source_target_pairs={{0,56},{1,3},{2,58},{3,1},{4,60},{5,7},{6,62},{7,5},{8,0},{9,11},{... | collective-permute-start | bytes 2359304 | tf_op jit(solution)/shard_map/ppermute | solution.py:42
  7.1 9.3 %collective-permute-start.3 = (bf16[3072,128]{1,0:T(8,128)(2,1)}, bf16[3072,128]{1,0:T(8,128)(2,1)}, u32[]{:S(2)}, u32[]{:S(2)}) collective-permute-start(bf16[3072,128]{1,0:T(8,128)(2,1)} %get-tuple-element.10.refs_2_), channel_id=1, source_target_pairs={{0,8},{1,3},{2,10},{3,1},{4,12},{5,7},{6,14},{7,5},{8,16},{9,11},{... | collective-permute-start | bytes 2359304 | tf_op jit(solution)/shard_map/ppermute | solution.py:42
  16.5 5.6 %all-to-all-start = ((bf16[16,8,2048]{2,1,0:T(8,128)(2,1)}), bf16[16,8,2048]{2,1,0:T(8,128)(2,1)S(1)}, u32[]{:S(2)}, u32[]{:S(2)}) async-start(bf16[16,8,2048]{2,1,0:T(8,128)(2,1)} %get-tuple-element.8), calls=%async_computation | async-start | bytes 1048576 | tf_op jit(solution)/shard_map/all_to_all | solution.py:46
  22.1 2.1 %collective-permute-start = (bf16[3072,128]{1,0:T(8,128)(2,1)}, bf16[3072,128]{1,0:T(8,128)(2,1)}, u32[]{:S(2)}, u32[]{:S(2)}) collective-permute-start(bf16[3072,128]{1,0:T(8,128)(2,1)} %get-tuple-element.9.refs_1_), channel_id=1, source_target_pairs={{0,1},{1,0},{2,3},{3,2},{4,5},{5,4},{6,7},{7,6},{8,9},{9,8},{10,11... | collective-permute-start | bytes 2359304 | tf_op jit(solution)/shard_map/ppermute | solution.py:36
  24.1 2.4 %collective-permute-start.1 = (bf16[3072,128]{1,0:T(8,128)(2,1)}, bf16[3072,128]{1,0:T(8,128)(2,1)}, u32[]{:S(2)}, u32[]{:S(2)}) collective-permute-start(bf16[3072,128]{1,0:T(8,128)(2,1)} %get-tuple-element.10.refs_2_), channel_id=1, source_target_pairs={{0,1},{1,0},{2,3},{3,2},{4,5},{5,4},{6,7},{7,6},{8,9},{9,8},{10,11... | collective-permute-start | bytes 2359304 | tf_op jit(solution)/shard_map/ppermute | solution.py:36
  26.5 3.9 %collective-permute-done.2.refs_5_ = bf16[3072,128]{1,0:T(8,128)(2,1)} collective-permute-done((bf16[3072,128]{1,0:T(8,128)(2,1)}, bf16[3072,128]{1,0:T(8,128)(2,1)}, u32[]{:S(2)}, u32[]{:S(2)}) %collective-permute-start.2) | collective-permute-done | bytes 786464 | tf_op jit(solution)/shard_map/ppermute | solution.py:42
  30.4 1.9 %collective-permute-start.4 = (bf16[3072,128]{1,0:T(8,128)(2,1)}, bf16[3072,128]{1,0:T(8,128)(2,1)}, u32[]{:S(2)}, u32[]{:S(2)}) collective-permute-start(bf16[3072,128]{1,0:T(8,128)(2,1)} %collective-permute-done.2.refs_5_), channel_id=1, source_target_pairs={{0,1},{1,0},{2,3},{3,2},{4,5},{5,4},{6,7},{7,6},{8,9},{9,8},{10,11... | collective-permute-start | bytes 2359304 | tf_op jit(solution)/shard_map/ppermute | solution.py:36
  32.4 4.8 %collective-permute-done.3.refs_6_ = bf16[3072,128]{1,0:T(8,128)(2,1)} collective-permute-done((bf16[3072,128]{1,0:T(8,128)(2,1)}, bf16[3072,128]{1,0:T(8,128)(2,1)}, u32[]{:S(2)}, u32[]{:S(2)}) %collective-permute-start.3) | collective-permute-done | bytes 786464 | tf_op jit(solution)/shard_map/ppermute | solution.py:42
  37.2 1.9 %collective-permute-start.5 = (bf16[3072,128]{1,0:T(8,128)(2,1)}, bf16[3072,128]{1,0:T(8,128)(2,1)}, u32[]{:S(2)}, u32[]{:S(2)}) collective-permute-start(bf16[3072,128]{1,0:T(8,128)(2,1)} %collective-permute-done.3.refs_6_), channel_id=1, source_target_pairs={{0,1},{1,0},{2,3},{3,2},{4,5},{5,4},{6,7},{7,6},{8,9},{9,8},{10,11... | collective-permute-start | bytes 2359304 | tf_op jit(solution)/shard_map/ppermute | solution.py:36
  39.1 0.0 copy-start.3
  39.1 3.7 %pack.1.refs_1_ = bf16[6144,128]{1,0:T(8,128)(2,1)} custom-call(s32[2]{0:T(128)} %bitcast.12, bf16[2,2048,128]{2,1,0:T(8,128)(2,1)} %bitcast.15, bf16[2,2048,128]{2,1,0:T(8,128)(2,1)} %bitcast.17, bf16[2,128,2048]{2,1,0:T(8,128)(2,1)} %bitcast.19), custom_call_target="tpu_custom_call" | custom-call | flops 1572864 | bytes 3145728 | tf_op jit(solution)/shard_map/pack/pallas_call | solution.py:138
  42.9 0.0 copy-start
  42.9 5.7 %collective-permute-start.8 = (bf16[6144,128]{1,0:T(8,128)(2,1)}, bf16[6144,128]{1,0:T(8,128)(2,1)}, u32[]{:S(2)}, u32[]{:S(2)}) collective-permute-start(bf16[6144,128]{1,0:T(8,128)(2,1)} %pack.1.refs_1_), channel_id=1, source_target_pairs={{0,8},{1,3},{2,10},{3,1},{4,12},{5,7},{6,14},{7,5},{8,16},{9,11},{... | collective-permute-start | bytes 4718600 | tf_op jit(solution)/shard_map/ppermute | solution.py:42
  48.6 0.0 collective-permute-done.refs_3_
  48.6 0.0 collective-permute-done.1.refs_4_
  48.6 0.0 all-to-all-done.refs_0_
  48.6 0.0 collective-permute-done.4.refs_7_
  48.6 0.0 collective-permute-done.5.refs_8_
  48.6 0.0 copy-done.1
  48.6 0.0 copy-start.2
  48.6 1.1 copy-done.2
  49.8 4.4 %ffn.2 = bf16[16,8,2048]{2,1,0:T(8,128)(2,1)} custom-call(bf16[16,8,2048]{2,1,0:T(8,128)(2,1)S(1)} %all-to-all-done.refs_0_, bf16[3072,128]{1,0:T(8,128)(2,1)S(1)} %copy-done.1, bf16[3072,128]{1,0:T(8,128)(2,1)S(1)} %copy-done.2, bf16[3072,128]{1,0:T(8,128)(2,1)} %collective-permute-done.refs_3_, bf16[3072,128]{1,0:T(8,128)(2,1)} %collective-permute-done.1.refs_4_, ...), custom_call_target="tpu_custom_call" | custom-call | flops 805306368 | bytes 6291456 | tf_op jit(solution)/shard_map/ffn/pallas_call | solution.py:247
  54.2 0.0 copy-start.4
  54.2 0.0 copy-start.5
  54.2 5.4 %all-to-all-start.1 = ((bf16[16,8,2048]{2,1,0:T(8,128)(2,1)}), bf16[16,8,2048]{2,1,0:T(8,128)(2,1)S(1)}, u32[]{:S(2)}, u32[]{:S(2)}) async-start(bf16[16,8,2048]{2,1,0:T(8,128)(2,1)} %ffn.2), calls=%async_computation.1 | async-start | bytes 1048576 | tf_op jit(solution)/shard_map/all_to_all | solution.py:46
  59.6 0.0 copy-done
  59.7 1.9 %collective-permute-start.7 = (bf16[6144,128]{1,0:T(8,128)(2,1)S(1)}, bf16[6144,128]{1,0:T(8,128)(2,1)}, u32[]{:S(2)}, u32[]{:S(2)}) collective-permute-start(bf16[6144,128]{1,0:T(8,128)(2,1)S(1)} %copy-done), channel_id=1, source_target_pairs={{0,1},{1,0},{2,3},{3,2},{4,5},{5,4},{6,7},{7,6},{8,9},{9,8},{10,11... | collective-permute-start | bytes 4718600 | tf_op jit(solution)/shard_map/ppermute | solution.py:36
  61.6 16.1 %collective-permute-done.8.refs_3_ = bf16[6144,128]{1,0:T(8,128)(2,1)} collective-permute-done((bf16[6144,128]{1,0:T(8,128)(2,1)}, bf16[6144,128]{1,0:T(8,128)(2,1)}, u32[]{:S(2)}, u32[]{:S(2)}) %collective-permute-start.8) | collective-permute-done | bytes 1572896 | tf_op jit(solution)/shard_map/ppermute | solution.py:42
  77.7 1.9 %collective-permute-start.9 = (bf16[6144,128]{1,0:T(8,128)(2,1)}, bf16[6144,128]{1,0:T(8,128)(2,1)}, u32[]{:S(2)}, u32[]{:S(2)}) collective-permute-start(bf16[6144,128]{1,0:T(8,128)(2,1)} %collective-permute-done.8.refs_3_), channel_id=1, source_target_pairs={{0,1},{1,0},{2,3},{3,2},{4,5},{5,4},{6,7},{7,6},{8,9},{9,8},{10,11... | collective-permute-start | bytes 4718600 | tf_op jit(solution)/shard_map/ppermute | solution.py:36
  79.6 0.0 all-to-all-done.1.parts_ref
  79.6 0.0 copy-done.3
  79.6 0.1 advance.2
  79.7 1.9 %collective-permute-start.6 = (bf16[8,2048]{1,0:T(8,128)(2,1)S(1)}, bf16[8,2048]{1,0:T(8,128)(2,1)S(1)}, u32[]{:S(2)}, u32[]{:S(2)}) collective-permute-start(bf16[8,2048]{1,0:T(8,128)(2,1)S(1)} %advance.2), channel_id=1, source_target_pairs={{704,0},{0,64},{64,128},{128,192},{192,256},{256,320},{320,384},{3... | collective-permute-start | bytes 98312 | tf_op jit(solution)/shard_map/ppermute | solution.py:19
  81.7 9.9 %collective-permute-done.6.refs_1_.rows_ref = bf16[8,2048]{1,0:T(8,128)(2,1)S(1)} collective-permute-done((bf16[8,2048]{1,0:T(8,128)(2,1)S(1)}, bf16[8,2048]{1,0:T(8,128)(2,1)S(1)}, u32[]{:S(2)}, u32[]{:S(2)}) %collective-permute-start.6) | collective-permute-done | bytes 32800 | tf_op jit(solution)/shard_map/ppermute | solution.py:19
  91.5 0.0 copy-done.4
  91.5 0.0 copy-done.5
  91.5 1.5 spread.1
  93.0 12.3 %all-to-all-start.2 = ((bf16[16,8,2048]{2,1,0:T(8,128)(2,1)}), bf16[16,8,2048]{2,1,0:T(8,128)(2,1)S(1)}, u32[]{:S(2)}, u32[]{:S(2)}) async-start(bf16[16,8,2048]{2,1,0:T(8,128)(2,1)} %spread.1), calls=%async_computation.2 | async-start | bytes 1048576 | tf_op jit(solution)/shard_map/all_to_all | solution.py:46
  105.3 0.0 collective-permute-done.7.refs_2_
  105.3 0.0 collective-permute-done.9.refs_4_
  105.3 14.3 %all-to-all-done.2.refs_0_ = bf16[16,8,2048]{2,1,0:T(8,128)(2,1)S(1)} async-done(((bf16[16,8,2048]{2,1,0:T(8,128)(2,1)}), bf16[16,8,2048]{2,1,0:T(8,128)(2,1)S(1)}, u32[]{:S(2)}, u32[]{:S(2)}) %all-to-all-start.2) | async-done | bytes 524320 | tf_op jit(solution)/shard_map/all_to_all | solution.py:46
  119.6 3.6 %ffn.3 = bf16[16,8,2048]{2,1,0:T(8,128)(2,1)S(1)} custom-call(bf16[16,8,2048]{2,1,0:T(8,128)(2,1)S(1)} %all-to-all-done.2.refs_0_, bf16[6144,128]{1,0:T(8,128)(2,1)S(1)} %copy-done, bf16[6144,128]{1,0:T(8,128)(2,1)} %collective-permute-done.7.refs_2_, bf16[6144,128]{1,0:T(8,128)(2,1)} %collective-permute-done.8.refs_3_, ...), custom_call_target="tpu_custom_call" | custom-call | flops 805306368 | bytes 6291456 | tf_op jit(solution)/shard_map/ffn/pallas_call | solution.py:247
  123.2 21.0 %all_to_all.20.parts_ref = bf16[16,8,2048]{2,1,0:T(8,128)(2,1)S(1)} all-to-all(bf16[16,8,2048]{2,1,0:T(8,128)(2,1)S(1)} %ffn.3), channel_id=1, replica_groups={{0,4,10,14,16,20,26,30,32,36,42,46,48,52,58,62},{2,6,8,12,18,22,24,28,3..., dimensions={0} | all-to-all | bytes 1048576 | tf_op jit(solution)/shard_map/all_to_all | solution.py:46
  144.2 0.1 advance.3
  144.3 1.9 %collective-permute-start.10 = (bf16[8,2048]{1,0:T(8,128)(2,1)S(1)}, bf16[8,2048]{1,0:T(8,128)(2,1)S(1)}, u32[]{:S(2)}, u32[]{:S(2)}) collective-permute-start(bf16[8,2048]{1,0:T(8,128)(2,1)S(1)} %advance.3), channel_id=1, source_target_pairs={{704,0},{0,64},{64,128},{128,192},{192,256},{256,320},{320,384},{3... | collective-permute-start | bytes 98312 | tf_op jit(solution)/shard_map/ppermute | solution.py:19
  146.2 9.9 %collective-permute-done.10 = bf16[8,2048]{1,0:T(8,128)(2,1)S(1)} collective-permute-done((bf16[8,2048]{1,0:T(8,128)(2,1)S(1)}, bf16[8,2048]{1,0:T(8,128)(2,1)S(1)}, u32[]{:S(2)}, u32[]{:S(2)}) %collective-permute-start.10) | collective-permute-done | bytes 32800 | tf_op jit(solution)/shard_map/ppermute | solution.py:19
  156.1 0.6 copy.8
  (1 shorter events, 0.0 us)
Async XLA Ops:
  3.9 26.6 %collective-permute-start.2 = (bf16[3072,128]{1,0:T(8,128)(2,1)}, bf16[3072,128]{1,0:T(8,128)(2,1)}, u32[]{:S(2)}, u32[]{:S(2)}) collective-permute-start(bf16[3072,128]{1,0:T(8,128)(2,1)} %get-tuple-element.9.refs_1_), channel_id=1, source_target_pairs={{0,56},{1,3},{2,58},{3,1},{4,60},{5,7},{6,62},{7,5},{8,0},{9,11},{... | collective-permute-start | bytes 2359304 | tf_op jit(solution)/shard_map/ppermute | solution.py:42
  7.1 30.1 %collective-permute-start.3 = (bf16[3072,128]{1,0:T(8,128)(2,1)}, bf16[3072,128]{1,0:T(8,128)(2,1)}, u32[]{:S(2)}, u32[]{:S(2)}) collective-permute-start(bf16[3072,128]{1,0:T(8,128)(2,1)} %get-tuple-element.10.refs_2_), channel_id=1, source_target_pairs={{0,8},{1,3},{2,10},{3,1},{4,12},{5,7},{6,14},{7,5},{8,16},{9,11},{... | collective-permute-start | bytes 2359304 | tf_op jit(solution)/shard_map/ppermute | solution.py:42
  16.5 32.1 %all-to-all-start = ((bf16[16,8,2048]{2,1,0:T(8,128)(2,1)}), bf16[16,8,2048]{2,1,0:T(8,128)(2,1)S(1)}, u32[]{:S(2)}, u32[]{:S(2)}) async-start(bf16[16,8,2048]{2,1,0:T(8,128)(2,1)} %get-tuple-element.8), calls=%async_computation | async-start | bytes 1048576 | tf_op jit(solution)/shard_map/all_to_all | solution.py:46
  22.1 26.6 %copy-start.1 = (bf16[3072,128]{1,0:T(8,128)(2,1)S(1)}, bf16[3072,128]{1,0:T(8,128)(2,1)}, u32[]{:S(2)}) copy-start(bf16[3072,128]{1,0:T(8,128)(2,1)} %get-tuple-element.9.refs_1_) | copy-start | bytes 2359300
  22.1 26.5 %collective-permute-start = (bf16[3072,128]{1,0:T(8,128)(2,1)}, bf16[3072,128]{1,0:T(8,128)(2,1)}, u32[]{:S(2)}, u32[]{:S(2)}) collective-permute-start(bf16[3072,128]{1,0:T(8,128)(2,1)} %get-tuple-element.9.refs_1_), channel_id=1, source_target_pairs={{0,1},{1,0},{2,3},{3,2},{4,5},{5,4},{6,7},{7,6},{8,9},{9,8},{10,11... | collective-permute-start | bytes 2359304 | tf_op jit(solution)/shard_map/ppermute | solution.py:36
  24.1 24.5 %collective-permute-start.1 = (bf16[3072,128]{1,0:T(8,128)(2,1)}, bf16[3072,128]{1,0:T(8,128)(2,1)}, u32[]{:S(2)}, u32[]{:S(2)}) collective-permute-start(bf16[3072,128]{1,0:T(8,128)(2,1)} %get-tuple-element.10.refs_2_), channel_id=1, source_target_pairs={{0,1},{1,0},{2,3},{3,2},{4,5},{5,4},{6,7},{7,6},{8,9},{9,8},{10,11... | collective-permute-start | bytes 2359304 | tf_op jit(solution)/shard_map/ppermute | solution.py:36
  30.4 18.2 %collective-permute-start.4 = (bf16[3072,128]{1,0:T(8,128)(2,1)}, bf16[3072,128]{1,0:T(8,128)(2,1)}, u32[]{:S(2)}, u32[]{:S(2)}) collective-permute-start(bf16[3072,128]{1,0:T(8,128)(2,1)} %collective-permute-done.2.refs_5_), channel_id=1, source_target_pairs={{0,1},{1,0},{2,3},{3,2},{4,5},{5,4},{6,7},{7,6},{8,9},{9,8},{10,11... | collective-permute-start | bytes 2359304 | tf_op jit(solution)/shard_map/ppermute | solution.py:36
  37.2 11.4 %collective-permute-start.5 = (bf16[3072,128]{1,0:T(8,128)(2,1)}, bf16[3072,128]{1,0:T(8,128)(2,1)}, u32[]{:S(2)}, u32[]{:S(2)}) collective-permute-start(bf16[3072,128]{1,0:T(8,128)(2,1)} %collective-permute-done.3.refs_6_), channel_id=1, source_target_pairs={{0,1},{1,0},{2,3},{3,2},{4,5},{5,4},{6,7},{7,6},{8,9},{9,8},{10,11... | collective-permute-start | bytes 2359304 | tf_op jit(solution)/shard_map/ppermute | solution.py:36
  39.1 40.5 %copy-start.3 = (bf16[1,8,2048]{2,1,0:T(8,128)(2,1)S(1)}, bf16[1,8,2048]{2,1,0:T(8,128)(2,1)}, u32[]{:S(2)}) copy-start(bf16[1,8,2048]{2,1,0:T(8,128)(2,1)} %param.6) | copy-start | bytes 98308
  42.9 16.8 %copy-start = (bf16[6144,128]{1,0:T(8,128)(2,1)S(1)}, bf16[6144,128]{1,0:T(8,128)(2,1)}, u32[]{:S(2)}) copy-start(bf16[6144,128]{1,0:T(8,128)(2,1)} %pack.1.refs_1_) | copy-start | bytes 4718596
  42.9 34.8 %collective-permute-start.8 = (bf16[6144,128]{1,0:T(8,128)(2,1)}, bf16[6144,128]{1,0:T(8,128)(2,1)}, u32[]{:S(2)}, u32[]{:S(2)}) collective-permute-start(bf16[6144,128]{1,0:T(8,128)(2,1)} %pack.1.refs_1_), channel_id=1, source_target_pairs={{0,8},{1,3},{2,10},{3,1},{4,12},{5,7},{6,14},{7,5},{8,16},{9,11},{... | collective-permute-start | bytes 4718600 | tf_op jit(solution)/shard_map/ppermute | solution.py:42
  48.6 1.1 copy-start.2
  54.2 37.4 %copy-start.4 = (f32[1,2,2048]{2,1,0:T(2,128)S(1)}, f32[1,2,2048]{2,1,0:T(2,128)}, u32[]{:S(2)}) copy-start(f32[1,2,2048]{2,1,0:T(2,128)} %param.10) | copy-start | bytes 49156
  54.2 37.3 %copy-start.5 = (s32[2,1]{0,1:T(1,128)S(1)}, s32[2,1]{0,1:T(1,128)}, u32[]{:S(2)}) copy-start(s32[2,1]{0,1:T(1,128)} %param.11) | copy-start | bytes 28
  54.2 25.4 %all-to-all-start.1 = ((bf16[16,8,2048]{2,1,0:T(8,128)(2,1)}), bf16[16,8,2048]{2,1,0:T(8,128)(2,1)S(1)}, u32[]{:S(2)}, u32[]{:S(2)}) async-start(bf16[16,8,2048]{2,1,0:T(8,128)(2,1)} %ffn.2), calls=%async_computation.1 | async-start | bytes 1048576 | tf_op jit(solution)/shard_map/all_to_all | solution.py:46
  59.7 45.6 %collective-permute-start.7 = (bf16[6144,128]{1,0:T(8,128)(2,1)S(1)}, bf16[6144,128]{1,0:T(8,128)(2,1)}, u32[]{:S(2)}, u32[]{:S(2)}) collective-permute-start(bf16[6144,128]{1,0:T(8,128)(2,1)S(1)} %copy-done), channel_id=1, source_target_pairs={{0,1},{1,0},{2,3},{3,2},{4,5},{5,4},{6,7},{7,6},{8,9},{9,8},{10,11... | collective-permute-start | bytes 4718600 | tf_op jit(solution)/shard_map/ppermute | solution.py:36
  77.7 27.6 %collective-permute-start.9 = (bf16[6144,128]{1,0:T(8,128)(2,1)}, bf16[6144,128]{1,0:T(8,128)(2,1)}, u32[]{:S(2)}, u32[]{:S(2)}) collective-permute-start(bf16[6144,128]{1,0:T(8,128)(2,1)} %collective-permute-done.8.refs_3_), channel_id=1, source_target_pairs={{0,1},{1,0},{2,3},{3,2},{4,5},{5,4},{6,7},{7,6},{8,9},{9,8},{10,11... | collective-permute-start | bytes 4718600 | tf_op jit(solution)/shard_map/ppermute | solution.py:36
  79.7 11.8 %collective-permute-start.6 = (bf16[8,2048]{1,0:T(8,128)(2,1)S(1)}, bf16[8,2048]{1,0:T(8,128)(2,1)S(1)}, u32[]{:S(2)}, u32[]{:S(2)}) collective-permute-start(bf16[8,2048]{1,0:T(8,128)(2,1)S(1)} %advance.2), channel_id=1, source_target_pairs={{704,0},{0,64},{64,128},{128,192},{192,256},{256,320},{320,384},{3... | collective-permute-start | bytes 98312 | tf_op jit(solution)/shard_map/ppermute | solution.py:19
  93.0 26.6 %all-to-all-start.2 = ((bf16[16,8,2048]{2,1,0:T(8,128)(2,1)}), bf16[16,8,2048]{2,1,0:T(8,128)(2,1)S(1)}, u32[]{:S(2)}, u32[]{:S(2)}) async-start(bf16[16,8,2048]{2,1,0:T(8,128)(2,1)} %spread.1), calls=%async_computation.2 | async-start | bytes 1048576 | tf_op jit(solution)/shard_map/all_to_all | solution.py:46
  144.3 11.8 %collective-permute-start.10 = (bf16[8,2048]{1,0:T(8,128)(2,1)S(1)}, bf16[8,2048]{1,0:T(8,128)(2,1)S(1)}, u32[]{:S(2)}, u32[]{:S(2)}) collective-permute-start(bf16[8,2048]{1,0:T(8,128)(2,1)S(1)} %advance.3), channel_id=1, source_target_pairs={{704,0},{0,64},{64,128},{128,192},{192,256},{256,320},{320,384},{3... | collective-permute-start | bytes 98312 | tf_op jit(solution)/shard_map/ppermute | solution.py:19
